TPU v7x, 32 devices: a whole 2x2x4 slice. The times are simulated.
32 devices in a mesh: slab: 4 (over z), swap: 8 (over y, x, core).
Axes of the slice: x: 2, y: 2, z: 4, core: 2. Of those that a mesh axis runs over, the one named last changes fastest.
Arguments:
- fluid_state: float32 [2, 128, 128, 256], P(None, ('slab', 'swap')), may hold values from -0.45 to 1.6, as said below
- material: int32 [128, 128, 256], P(('slab', 'swap')), may hold values from 0 to 7
- table_colour: float32 [3, 8], replicated, may hold values from 0.2 to 2
- table_extinction: float32 [8], replicated, may hold values from 0.2 to 1.5
Outputs:
- new_density: float32 [128, 128, 256], P(('slab', 'swap'))
- rendered: float32 [4, 32768], P(None, 'swap')
Inputs may be any that keep to these rules, and one draw needn't show every extreme that they name: fluid_state[0] is the density, between 0.6 and 1.6; fluid_state[1] is the momentum along the view axis, between -0.45 and 0.45.
All inputs are finite; a program needn't handle non-finite values.
Results may differ from a plain program's by a relative error of at most 0.0003.
Values sent between devices are 32-bit elements; how exact they have to be, the bound alone decides.
No kernel may reach another device: no remote copies, remote signals or barrier semaphores. Data moves between devices by JAX's collectives and lax.ppermute only.
A program may use at most 64 MiB of HBM per device.

v0:
```python
import jax
import jax.numpy as jnp
from jax import lax
from jax.sharding import PartitionSpec as P

COURANT = 0.4
DEPTH_SCALE = 2.5


def with_halo(array, sides, width):
    for axis, dim in sides:
        devices, length = (lax.axis_size(axis), array.shape[dim])
        up = [(i, (i + 1) % devices) for i in range(devices)]
        down = [(j, i) for i, j in up]
        last = lax.slice_in_dim(array, length - width, length, axis=dim)
        leading = lax.slice_in_dim(array, 0, width, axis=dim)
        before = lax.ppermute(last, axis, up)
        after = lax.ppermute(leading, axis, down)
        array = jnp.concatenate([before, array, after], axis=dim)
    return array


def from_partner(block, axis, stride):
    count = lax.axis_size(axis)
    route = []
    for low in range(count):
        high = low | 1 << stride
        if high != low and high < count:
            route += [(low, high), (high, low)]
    return lax.ppermute(block, axis, route)


def hydro_step(fields):
    density = fields[0]
    momentum = fields[1]
    velocity = momentum / density
    speeds = jnp.abs(velocity) + 1.0
    fluxes = jnp.stack([momentum, momentum * velocity + density])
    face_speed = jnp.maximum(speeds[:-1], speeds[1:])
    face_flux = 0.5 * (fluxes[:, :-1] + fluxes[:, 1:]) - 0.5 * face_speed * (
        fields[:, 1:] - fields[:, :-1]
    )
    return fields[:, 1:-1] - COURANT * (face_flux[:, 1:] - face_flux[:, :-1])


def over_pair(nearer, farther):
    through = 1.0 - nearer[3:4]
    return jnp.concatenate(
        [nearer[:3] + through * farther[:3], nearer[3:4] + through * farther[3:4]], axis=0
    )


def stack_over(pieces):
    through = jnp.cumprod(1.0 - pieces[3], axis=0)
    before = jnp.concatenate([jnp.ones_like(through[:1]), through[:-1]], axis=0)
    colour = jnp.sum(before[None] * pieces[:3], axis=1)
    opacity = 1.0 - through[-1]
    return jnp.concatenate([colour, opacity[None]], axis=0)


def render_local(density, material, table_colour, table_extinction, total_cells):
    extinction = jnp.zeros(density.shape, jnp.float32)
    for number in range(table_extinction.shape[0]):
        extinction = extinction + jnp.where(material == number, table_extinction[number], 0.0)
    optical = DEPTH_SCALE * extinction * density / total_cells
    running = jnp.cumsum(optical, axis=0)
    weight = jnp.exp(optical - running) * (1.0 - jnp.exp(-optical))
    colour = jnp.zeros((3,) + density.shape[1:], jnp.float32)
    for number in range(table_extinction.shape[0]):
        summed = jnp.sum(jnp.where(material == number, weight, 0.0), axis=0)
        colour = colour + table_colour[:, number][:, None, None] * summed[None]
    opacity = 1.0 - jnp.exp(-running[-1])
    return jnp.concatenate([colour, opacity[None]], axis=0)


def per_device(fluid_state, material, table_colour, table_extinction):
    slabs = lax.axis_size("slab")
    members = lax.axis_size("swap")
    depth_cells = fluid_state.shape[1]
    fields = with_halo(fluid_state, ((("slab", "swap"), 1),), 4)
    for number in range(4):
        fields = hydro_step(fields)
    density = fields[0]
    local = render_local(
        density, material, table_colour, table_extinction, depth_cells * slabs * members
    )
    pixels = local.shape[1] * local.shape[2]
    tile_width = pixels // members
    holding = local.reshape(4, members, tile_width)
    position = lax.axis_index("swap")
    for number in range(members.bit_length() - 1):
        own_bit = position // 2**number % 2
        paired = holding.reshape(4, holding.shape[1] // 2, 2, tile_width)
        kept_half = lax.dynamic_index_in_dim(paired, own_bit, 2, keepdims=False)
        given_half = lax.dynamic_index_in_dim(paired, 1 - own_bit, 2, keepdims=False)
        received = from_partner(given_half, "swap", number)
        holding = jnp.where(
            own_bit == 0, over_pair(kept_half, received), over_pair(received, kept_half)
        )
    every_group = lax.all_gather(holding, "slab", axis=1, tiled=True)
    return (density, stack_over(every_group))


def solution(mesh):
    return jax.shard_map(
        per_device,
        mesh=mesh,
        in_specs=(P(None, ("slab", "swap"), None, None), P(("slab", "swap"), None, None), P(), P()),
        out_specs=(P(("slab", "swap"), None, None), P(None, "swap")),
        check_vma=False,
    )
```

profile of v0, /device:TPU:0, one launch (start us, length us, event | category | flops | bytes accessed | tf_op | source)
XLA Modules:
  0.0 74.6 jit_solution(14011646498176181556)
XLA Ops:
  0.6 0.5 collective-permute-start
  1.2 6.0 %collective-permute-start.1 = (f32[2,4,128,256]{3,2,1,0:T(8,128)}, f32[2,4,128,256]{3,2,1,0:T(8,128)S(1)}, u32[]{:S(2)}, u32[]{:S(2)}) collective-permute-start(f32[2,4,128,256]{3,2,1,0:T(8,128)} %param.4), channel_id=1, source_target_pairs={{1,0},{2,1},{3,2},{4,3},{5,4},{6,5},{7,6},{8,7},{9,8},{10,9},{11,1... | collective-permute-start | bytes 3145736 | tf_op jit(solution)/shard_map/ppermute | solution.py:18
  7.2 1.6 %fusion.51 = (f32[1]{0:T(128)}, f32[1]{0:T(128)}, f32[1]{0:T(128)}, f32[1]{0:T(128)}, f32[1]{0:T(128)}, /*index=5*/f32[1]{0:T(128)}, f32[1]{0:T(128)}, f32[1]{0:T(128)}) fusion(f32[8]{0:T(128)} %param.7), kind=kLoop, calls=%fused_computation.160 | loop fusion | bytes 64 | tf_op jit(solution)/shard_map/slice | solution.py:64
  8.8 1.3 %slice_reduce_fusion.7 = (f32[3]{0:T(128)S(1)}, f32[3]{0:T(128)S(1)}, f32[3]{0:T(128)S(1)}, f32[3]{0:T(128)S(1)}, f32[3]{0:T(128)S(1)}, /*index=5*/f32[3]{0:T(128)S(1)}, f32[3]{0:T(128)S(1)}, f32[3]{0:T(128)S(1)}) fusion(f32[3,8]{1,0:T(4,128)} %param.6), kind=kLoop, calls=%fused_computation.158 | loop fusion | bytes 192 | tf_op jit(solution)/shard_map/slice | solution.py:71
  10.1 9.8 %collective-permute-done = f32[2,4,128,256]{3,2,1,0:T(8,128)S(1)} collective-permute-done((f32[2,4,128,256]{3,2,1,0:T(8,128)}, f32[2,4,128,256]{3,2,1,0:T(8,128)S(1)}, u32[]{:S(2)}, u32[]{:S(2)}) %collective-permute-start) | collective-permute-done | bytes 1048608 | tf_op jit(solution)/shard_map/ppermute | solution.py:17
  20.2 0.5 abs_add_fusion
  20.6 0.1 fusion.22
  20.7 1.3 %fusion.3 = f32[2,11,128,256]{3,2,1,0:T(8,128)S(1)} fusion(f32[1,12,128,256]{3,2,1,0:T(8,128)S(1)} %get-tuple-element.30, f32[1,12,128,256]{3,2,1,0:T(8,128)S(1)} %get-tuple-element.29, f32[2,12,128,256]{3,2,1,0:T(8,128)S(1)} %constant_dynamic-update-slice_fusion, f32[11,128,256]{2,1,0:T(8,128)S(1)} %fusion.22), kind=kLoop, calls=%fused_computation.5 | loop fusion | flops 5046272 | bytes 13238272 | tf_op jit(solution)/shard_map/sub | solution.py:40
  22.0 0.4 fusion.6
  22.4 0.4 abs_add_fusion.1
  22.9 0.1 fusion.29
  23.0 0.6 fusion.10
  23.6 0.4 fusion.13
  24.0 0.3 abs_add_fusion.2
  24.4 0.4 fusion.17
  24.8 0.3 fusion.20
  25.0 0.2 abs_add_fusion.3
  25.3 0.9 %copy-done = f32[2,6,128,256]{3,2,1,0:T(8,128)} copy-done((f32[2,6,128,256]{3,2,1,0:T(8,128)}, f32[2,6,128,256]{3,2,1,0:T(8,128)S(1)}, u32[]{:S(2)}) %copy-start) | copy-done | bytes 1572888
  26.2 0.3 fusion.26
  26.5 0.2 fusion.50
  26.7 1.0 %slice-done = f32[2,4,128,256]{3,2,1,0:T(8,128)S(1)} async-done(((f32[2,6,128,256]{3,2,1,0:T(8,128)}), f32[2,4,128,256]{3,2,1,0:T(8,128)S(1)}, s32[]{:S(2)}) %slice-start) | async-done | bytes 1048600 | tf_op jit(solution)/shard_map/slice | solution.py:43
  27.7 0.1 copy-done.2
  27.8 6.7 %multiply_multiply_fusion = (f32[4,128,256]{2,1,0:T(8,128)S(1)}, pred[4,128,256]{2,1,0:T(8,128)(4,1)S(1)}, pred[4,128,256]{2,1,0:T(8,128)(4,1)S(1)}, pred[4,128,...) fusion(f32[]{:T(128)} %bitcast.12, f32[]{:T(128)} %bitcast.11, ...), kind=kLoop, calls=%fused_computation.85 | loop fusion | flops 3801088 | bytes 4194336 | tf_op jit(solution)/shard_map/div | solution.py:65
  34.5 0.3 fusion.52
  34.8 0.7 select_reduce_fusion.7
  36.3 0.1 concatenate.74
  36.4 0.6 multiply_add_fusion.4
  37.1 0.3 fusion.38
  37.3 8.6 %collective-permute-start.2 = (f32[4,4,4096]{2,0,1:T(4,128)S(1)}, f32[4,4,4096]{2,0,1:T(4,128)S(1)}, u32[]{:S(2)}, u32[]{:S(2)}) collective-permute-start(f32[4,4,4096]{2,0,1:T(4,128)S(1)} %get-tuple-element.43), channel_id=1, source_target_pairs={{0,1},{1,0},{2,3},{3,2},{4,5},{5,4},{6,7},{7,6},{8,9},{9,8},{10,11... | collective-permute-start | bytes 786440 | tf_op jit(solution)/shard_map/ppermute | solution.py:30
  46.1 1.0 %collective-permute-done.2 = f32[4,4,4096]{2,0,1:T(4,128)S(1)} collective-permute-done((f32[4,4,4096]{2,0,1:T(4,128)S(1)}, f32[4,4,4096]{2,0,1:T(4,128)S(1)}, u32[]{:S(2)}, u32[]{:S(2)}) %collective-permute-start.2) | collective-permute-done | bytes 262176 | tf_op jit(solution)/shard_map/ppermute | solution.py:30
  47.1 0.2 fusion.46
  47.3 0.1 multiply_add_fusion.5
  47.5 0.2 copy.26
  47.6 0.2 copy.27
  47.9 0.2 maximum_select_fusion
  48.1 0.1 constant_dynamic-slice_fusion
  48.3 0.1 constant_dynamic-slice_fusion.3
  48.4 0.1 copy.48
  48.5 1.6 %collective-permute-start.3 = (f32[4,2,4096]{2,0,1:T(4,128)S(1)}, f32[4,2,4096]{2,0,1:T(4,128)S(1)}, u32[]{:S(2)}, u32[]{:S(2)}) collective-permute-start(f32[4,2,4096]{2,0,1:T(4,128)S(1)} %bitcast.91), channel_id=1, source_target_pairs={{0,2},{2,0},{1,3},{3,1},{4,6},{6,4},{5,7},{7,5},{8,10},{10,8},{9,1... | collective-permute-start | bytes 393224 | tf_op jit(solution)/shard_map/ppermute | solution.py:30
  50.1 4.2 %collective-permute-done.3 = f32[4,2,4096]{2,0,1:T(4,128)S(1)} collective-permute-done((f32[4,2,4096]{2,0,1:T(4,128)S(1)}, f32[4,2,4096]{2,0,1:T(4,128)S(1)}, u32[]{:S(2)}, u32[]{:S(2)}) %collective-permute-start.3) | collective-permute-done | bytes 131104 | tf_op jit(solution)/shard_map/ppermute | solution.py:30
  54.3 0.1 fusion.48
  54.5 0.1 fusion.44
  54.6 0.1 maximum_select_fusion.1
  54.7 2.4 %collective-permute-start.4 = (f32[4,1,4096]{2,0,1:T(4,128)S(1)}, f32[4,1,4096]{2,0,1:T(4,128)S(1)}, u32[]{:S(2)}, u32[]{:S(2)}) collective-permute-start(f32[4,1,4096]{2,0,1:T(4,128)S(1)} %constant_dynamic-slice_fusion.1), channel_id=1, source_target_pairs={{0,4},{4,0},{1,5},{5,1},{2,6},{6,2},{3,7},{7,3},{8,12},{12,8},{9,1... | collective-permute-start | bytes 196616 | tf_op jit(solution)/shard_map/ppermute | solution.py:30
  57.2 2.2 %collective-permute-done.4 = f32[4,1,4096]{2,0,1:T(4,128)S(1)} collective-permute-done((f32[4,1,4096]{2,0,1:T(4,128)S(1)}, f32[4,1,4096]{2,0,1:T(4,128)S(1)}, u32[]{:S(2)}, u32[]{:S(2)}) %collective-permute-start.4) | collective-permute-done | bytes 65568 | tf_op jit(solution)/shard_map/ppermute | solution.py:30
  59.6 13.9 %all_gather.3 = f32[4,4,4096]{2,0,1:T(4,128)S(1)} all-gather(f32[4,1,4096]{2,0,1:T(4,128)S(1)} %maximum_select_fusion.2), channel_id=1, replica_groups=mesh['slab'=4,'swap'=8] {'slab'}, dimensions={1}, use_global_device_ids=true | all-gather | bytes 327680 | tf_op jit(solution)/shard_map/all_gather | solution.py:100
  73.6 0.1 reduce_window.9
  73.9 0.7 pad_maximum_fusion.4
  (37 shorter events, 1.9 us)
Async XLA Ops:
  0.6 19.3 %copy-start.1 = (f32[2,4,128,256]{3,2,1,0:T(8,128)S(1)}, f32[2,4,128,256]{3,2,1,0:T(8,128)}, u32[]{:S(2)}) copy-start(f32[2,4,128,256]{3,2,1,0:T(8,128)} %param.4) | copy-start | bytes 3145732
  0.6 19.3 %collective-permute-start = (f32[2,4,128,256]{3,2,1,0:T(8,128)}, f32[2,4,128,256]{3,2,1,0:T(8,128)S(1)}, u32[]{:S(2)}, u32[]{:S(2)}) collective-permute-start(f32[2,4,128,256]{3,2,1,0:T(8,128)} %param.4), channel_id=1, source_target_pairs={{0,1},{1,2},{2,3},{3,4},{4,5},{5,6},{6,7},{7,8},{8,9},{9,10},{10,1... | collective-permute-start | bytes 3145736 | tf_op jit(solution)/shard_map/ppermute | solution.py:17
  1.2 18.9 %collective-permute-start.1 = (f32[2,4,128,256]{3,2,1,0:T(8,128)}, f32[2,4,128,256]{3,2,1,0:T(8,128)S(1)}, u32[]{:S(2)}, u32[]{:S(2)}) collective-permute-start(f32[2,4,128,256]{3,2,1,0:T(8,128)} %param.4), channel_id=1, source_target_pairs={{1,0},{2,1},{3,2},{4,3},{5,4},{6,5},{7,6},{8,7},{9,8},{10,9},{11,1... | collective-permute-start | bytes 3145736 | tf_op jit(solution)/shard_map/ppermute | solution.py:18
  25.0 1.2 %copy-start = (f32[2,6,128,256]{3,2,1,0:T(8,128)}, f32[2,6,128,256]{3,2,1,0:T(8,128)S(1)}, u32[]{:S(2)}) copy-start(f32[2,6,128,256]{3,2,1,0:T(8,128)S(1)} %fusion.20) | copy-start | bytes 4718596
  26.4 1.2 %slice-start = ((f32[2,6,128,256]{3,2,1,0:T(8,128)}), f32[2,4,128,256]{3,2,1,0:T(8,128)S(1)}, s32[]{:S(2)}) async-start(f32[2,6,128,256]{3,2,1,0:T(8,128)} %copy-done), calls=%async_computation | async-start | bytes 2097152 | tf_op jit(solution)/shard_map/slice | solution.py:43
  26.5 1.3 %copy-start.2 = (s32[4,128,256]{2,1,0:T(8,128)S(1)}, s32[4,128,256]{2,1,0:T(8,128)}, u32[]{:S(2)}) copy-start(s32[4,128,256]{2,1,0:T(8,128)} %param.5) | copy-start | bytes 1572868
  37.3 9.8 %collective-permute-start.2 = (f32[4,4,4096]{2,0,1:T(4,128)S(1)}, f32[4,4,4096]{2,0,1:T(4,128)S(1)}, u32[]{:S(2)}, u32[]{:S(2)}) collective-permute-start(f32[4,4,4096]{2,0,1:T(4,128)S(1)} %get-tuple-element.43), channel_id=1, source_target_pairs={{0,1},{1,0},{2,3},{3,2},{4,5},{5,4},{6,7},{7,6},{8,9},{9,8},{10,11... | collective-permute-start | bytes 786440 | tf_op jit(solution)/shard_map/ppermute | solution.py:30
  48.5 5.8 %collective-permute-start.3 = (f32[4,2,4096]{2,0,1:T(4,128)S(1)}, f32[4,2,4096]{2,0,1:T(4,128)S(1)}, u32[]{:S(2)}, u32[]{:S(2)}) collective-permute-start(f32[4,2,4096]{2,0,1:T(4,128)S(1)} %bitcast.91), channel_id=1, source_target_pairs={{0,2},{2,0},{1,3},{3,1},{4,6},{6,4},{5,7},{7,5},{8,10},{10,8},{9,1... | collective-permute-start | bytes 393224 | tf_op jit(solution)/shard_map/ppermute | solution.py:30
  54.7 4.7 %collective-permute-start.4 = (f32[4,1,4096]{2,0,1:T(4,128)S(1)}, f32[4,1,4096]{2,0,1:T(4,128)S(1)}, u32[]{:S(2)}, u32[]{:S(2)}) collective-permute-start(f32[4,1,4096]{2,0,1:T(4,128)S(1)} %constant_dynamic-slice_fusion.1), channel_id=1, source_target_pairs={{0,4},{4,0},{1,5},{5,1},{2,6},{6,2},{3,7},{7,3},{8,12},{12,8},{9,1... | collective-permute-start | bytes 196616 | tf_op jit(solution)/shard_map/ppermute | solution.py:30
where the time goes:
time: 74.8 us; the launch traced here: 74.6 us
  starting transfers between devices  19.1 us (26%)
  waiting for transfers between devices  17.3 us (23%)
  other arithmetic  16 us (21%)
  blocking collectives  13.9 us (19%)
  local copies, waits for them, and re-layouts  7.1 us (9%)
  between operations  1.11 us (1%)
    all_gather x1, blocking collectives, per_device(): every_group = lax.all_gather(holding, 'slab', axis=1, tiled=True)  13.9 us
    ppermute x3, starting transfers between devices, from_partner(): return lax.ppermute(block, axis, route)  12.6 us
    ppermute x1, waiting for transfers between devices, with_halo(): before = lax.ppermute(last, axis, up)  9.84 us
    ppermute x3, waiting for transfers between devices, from_partner(): return lax.ppermute(block, axis, route)  7.47 us
    div x1, other arithmetic, render_local(): optical = DEPTH_SCALE * extinction * density / total_cells  6.71 us
    ppermute x1, starting transfers between devices, with_halo(): after = lax.ppermute(leading, axis, down)  5.97 us
    sub x4, other arithmetic, hydro_step(): 0.5 * (fluxes[:, :-1] + fluxes[:, 1:])  2.5 us
    slice x1, local copies, waits for them, and re-layouts, render_local(): table_extinction[number]  1.63 us
  transfers between devices with their start and end apart: 5, of which 4 were waited for; matrix products, arithmetic and copies ran while one was open for 4% of the time, Pallas kernels for 0%

commit v1 on v0

v1 whole, which is shorter than its diff:
```python
import functools

import jax
import jax.numpy as jnp
from jax import lax
from jax.experimental import pallas as pl
from jax.experimental.pallas import tpu as pltpu
from jax.sharding import PartitionSpec as P

COURANT = 0.4
DEPTH_SCALE = 2.5
LANES = 128
VMEM = pl.BlockSpec(memory_space=pltpu.VMEM)


def routes(members):
    half = members // 2
    return [[(w, 2 * ((w % half) ^ r) + w // half) for w in range(members)] for r in range(half)]


def pick(arrays, index):
    out = arrays[0]
    for number in range(1, len(arrays)):
        out = jnp.where(index == number, arrays[number], out)
    return out


def advance(state, stage, density, momentum, emit):
    if stage == 4:
        emit(density)
        return
    last = stage == 3
    velocity = momentum / density
    speed = jnp.abs(velocity) + 1.0
    pressure = None if last else momentum * velocity + density
    held = state[stage]
    if held is None:
        state[stage] = (density, momentum, speed, pressure, None, None)
        return
    density0, momentum0, speed0, pressure0, mass0, force0 = held
    face = jnp.maximum(speed0, speed)
    mass = (momentum0 + momentum) - face * (density - density0)
    force = None if last else (pressure0 + pressure) - face * (momentum - momentum0)
    state[stage] = (density, momentum, speed, pressure, mass, force)
    if mass0 is None:
        return
    density1 = density0 - (0.5 * COURANT) * (mass - mass0)
    momentum1 = None if last else momentum0 - (0.5 * COURANT) * (force - force0)
    advance(state, stage + 1, density1, momentum1, emit)


def sweep_kernel(half, *refs):
    blocks, materials = refs[:half], refs[half : 2 * half]
    near, far, table = refs[2 * half : 2 * half + 3]
    density_out = refs[2 * half + 3 : 3 * half + 3]
    image, fluid, kind, dense = refs[3 * half + 3 :]
    member = lax.axis_index("swap")
    chip, upper = member // 2, member % 2
    layers, rows, columns = blocks[0].shape[1:]
    for r in range(half):
        fluid[:, pl.ds((1 + (chip ^ r)) * layers, layers)] = blocks[r][...]
        kind[pl.ds((chip ^ r) * layers, layers)] = materials[r][...]
    near_at = jnp.where(upper == 1, 0, half + 1)
    far_at = jnp.where(upper == 1, half + 1, 0)
    fluid[:, pl.ds(near_at * layers, layers)] = near[...]
    fluid[:, pl.ds(far_at * layers, layers)] = far[...]

    tall = min(8, rows)
    across = columns // LANES

    def tile(number, carry):
        row = pl.ds(pl.multiple_of(number // across * tall, tall), tall)
        column = pl.ds(pl.multiple_of(number % across * LANES, LANES), LANES)

        def block(state, light, position):
            for layer in range(layers):
                at = position * layers + layer

                def emit(density):
                    own = at - 2 * layers
                    dense[own, row, column] = density
                    which = kind[own, row, column]
                    factor, red, green, blue = (
                        jnp.take_along_axis(table[n, :tall, :], which, axis=1) for n in range(4)
                    )
                    through = jnp.exp(-(factor * density))
                    weight = light[0] * (1.0 - through)
                    light[0] = light[0] * through
                    light[1] = light[1] + weight * red
                    light[2] = light[2] + weight * green
                    light[3] = light[3] + weight * blue

                advance(state, 0, fluid[0, at, row, column], fluid[1, at, row, column], emit)

        state = [None] * 4
        zero = jnp.zeros((tall, LANES), jnp.float32)
        light = [zero + 1.0, zero, zero, zero]
        block(state, light, 0)
        block(state, light, 1)
        if half <= 4:
            for position in range(2, half + 2):
                block(state, light, position)
        else:

            def step(position, carry):
                state, light = [list(part) for part in carry]
                state = [tuple(held) for held in state]
                block(state, light, position)
                return state, light

            state, light = lax.fori_loop(2, half + 2, step, (state, light))
        image[0, row, column] = light[1]
        image[1, row, column] = light[2]
        image[2, row, column] = light[3]
        image[3, row, column] = 1.0 - light[0]
        return carry

    lax.fori_loop(0, rows // tall * across, tile, 0)
    for r in range(half):
        density_out[r][...] = dense[pl.ds((chip ^ r) * layers, layers)]


def sweep(blocks, materials, near, far, table):
    half = len(blocks)
    layers, rows, columns = blocks[0].shape[1:]
    f32 = jnp.float32
    cells = half * layers * rows * columns
    outs = pl.pallas_call(
        functools.partial(sweep_kernel, half),
        out_shape=[jax.ShapeDtypeStruct((layers, rows, columns), f32)] * half
        + [jax.ShapeDtypeStruct((4, rows, columns), f32)],
        in_specs=[VMEM] * (2 * half + 3),
        out_specs=[VMEM] * (half + 1),
        scratch_shapes=[
            pltpu.VMEM((2, (half + 2) * layers, rows, columns), f32),
            pltpu.VMEM((half * layers, rows, columns), jnp.int32),
            pltpu.VMEM((half * layers, rows, columns), f32),
        ],
        cost_estimate=pl.CostEstimate(flops=200 * cells, bytes_accessed=16 * cells, transcendentals=6 * cells),
        name="sweep",
    )(*blocks, *materials, near, far, table)
    return outs[:half], outs[half]


def over(nearer, farther):
    through = 1.0 - nearer[3:4]
    return jnp.concatenate([nearer[:3] + through * farther[:3], nearer[3:4] + through * farther[3:4]], axis=0)


def per_device(fluid_state, material, table_colour, table_extinction):
    slabs = lax.axis_size("slab")
    members = lax.axis_size("swap")
    half = members // 2
    member = lax.axis_index("swap")
    slab = lax.axis_index("slab")
    chip, upper = member // 2, member % 2
    _, layers, height, width = fluid_state.shape
    rows = height // half
    forward = routes(members)
    backward = [[(b, a) for a, b in pairs] for pairs in forward]

    scale = DEPTH_SCALE / (layers * slabs * members)
    table = jnp.concatenate([table_extinction[None] * scale, table_colour], axis=0)
    table = jnp.pad(table, ((0, 0), (0, LANES - table.shape[1])))
    table = jnp.broadcast_to(table[:, None, :], (4, 8, LANES))

    place = member % half
    blocks, materials = [], []
    for r in range(half):
        chunk = lax.dynamic_slice_in_dim(fluid_state, (place ^ r) * rows, rows, axis=2)
        blocks.append(lax.ppermute(chunk, "swap", forward[r]))
    for r in range(half):
        chunk = lax.dynamic_slice_in_dim(material, (place ^ r) * rows, rows, axis=1)
        materials.append(lax.ppermute(chunk, "swap", forward[r]))

    first = pick(blocks, chip)
    final = pick(blocks, chip ^ (half - 1))
    outer = jnp.where(upper == 1, final, first)
    inner = jnp.where(upper == 1, first, final)
    ring = []
    for z in range(slabs):
        for w in range(members):
            to = ((z + 1) % slabs, w - 1) if w % 2 else ((z - 1) % slabs, w + 1)
            ring.append((z * members + w, to[0] * members + to[1]))
    far = lax.ppermute(outer, ("slab", "swap"), ring)
    near = lax.ppermute(inner, "swap", [(w, w ^ 1) for w in range(members)])

    returned, image = sweep(blocks, materials, near, far, table)

    image = image.reshape(4, 2, rows // 2, width)
    kept = lax.dynamic_index_in_dim(image, upper, 1, keepdims=False)
    given = lax.dynamic_index_in_dim(image, 1 - upper, 1, keepdims=False)
    got = lax.ppermute(given, "swap", [(w, w ^ 1) for w in range(members)])
    tile = over(jnp.where(upper == 1, got, kept), jnp.where(upper == 1, kept, got))
    pieces = [tile]
    for away in range(1, slabs):
        pieces.append(lax.ppermute(tile, "slab", [(z, z ^ away) for z in range(slabs)]))
    chunks = [lax.ppermute(returned[r], "swap", backward[r]) for r in range(half)]
    ordered = [pick(pieces, slab ^ z) for z in range(slabs)]
    rendered = functools.reduce(over, ordered).reshape(4, height * width // members)
    density = jnp.concatenate([pick(chunks, place ^ j) for j in range(half)], axis=1)
    return density, rendered


def solution(mesh):
    return jax.shard_map(
        per_device,
        mesh=mesh,
        in_specs=(P(None, ("slab", "swap"), None, None), P(("slab", "swap"), None, None), P(), P()),
        out_specs=(P(("slab", "swap"), None, None), P(None, "swap")),
        check_vma=False,
    )
```

time: 74.8 us -> 59.6 us (0.80)
  the two profiles are of different devices: /device:TPU:0 before, /device:TPU:1 now
where the time goes in v1:
time: 59.6 us; the launch traced here: 59.2 us
  starting transfers between devices  37 us (62%)
  waiting for transfers between devices  10.1 us (17%)
  local copies, waits for them, and re-layouts  4.98 us (8%)
  Pallas kernels  4.81 us (8%)
  other arithmetic  1.2 us (2%)
  between operations  1.11 us (2%)
    ppermute x4, starting transfers between devices, per_device(): materials.append(lax.ppermute(chunk, 'swap', forward[r]))  12.5 us
    ppermute x4, starting transfers between devices, per_device(): blocks.append(lax.ppermute(chunk, 'swap', forward[r]))  9.15 us
    ppermute x4, starting transfers between devices, per_device(): lax.ppermute(returned[r], 'swap', backward[r])  7.6 us
    ppermute x1, waiting for transfers between devices, per_device(): far = lax.ppermute(outer, ('slab', 'swap'), ring)  5.5 us
    pallas_call x1, Pallas kernels, sweep(): pl.pallas_call(functools.partial(sweep_kernel, half), out_shape=[jax.Shap...  4.81 us
    ppermute x4, waiting for transfers between devices, per_device(): lax.ppermute(returned[r], 'swap', backward[r])  3.62 us
    ppermute x3, starting transfers between devices, per_device(): lax.ppermute(tile, 'slab', [(z, z ^ away) for z in range(slabs)])  3.61 us
    ppermute x1, starting transfers between devices, per_device(): got = lax.ppermute(given, 'swap', [(w, w ^ 1) for w in range(members)])  2.45 us
  transfers between devices with their start and end apart: 18, of which 6 were waited for; matrix products, arithmetic and copies ran while one was open for 2% of the time, Pallas kernels for 0%

profile of v1, /device:TPU:1, one launch (start us, length us, event | category | flops | bytes accessed | tf_op | source)
XLA Modules:
  0.0 59.2 jit_solution(16669161566663753622)
XLA Ops:
  0.7 1.3 %constant_dynamic-slice_fusion.4 = (f32[2,4,32,256]{3,2,1,0:T(8,128)S(1)}, f32[2,4,32,256]{3,2,1,0:T(8,128)S(1)}, f32[2,4,32,256]{3,2,1,0:T(8,128)S(1)}, f32[2,4,32,256]{3,2,1,0:T(8,128)S(1)}) fusion(f32[2,4,128,256]{3,2,1,0:T(8,128)} %param.4, s32[]{:T(128)S(6)} %select_n.249, s32[]{:T(128)S(6)} %select_n.247, s32[]{:T(128)S(6)} %select_n.246, s32[]{:T(128)S(6)} %select_n.248), kind=kLoop, calls=%fused_computation.44 | loop fusion | bytes 2097168 | tf_op jit(solution)/shard_map/dynamic_slice | solution.py:170
  2.0 4.5 %collective-permute-start = (f32[2,4,32,256]{3,2,1,0:T(8,128)S(1)}, f32[2,4,32,256]{3,2,1,0:T(8,128)S(1)}, u32[]{:S(2)}, u32[]{:S(2)}) collective-permute-start(f32[2,4,32,256]{3,2,1,0:T(8,128)S(1)} %get-tuple-element.17), channel_id=1, source_target_pairs={{0,0},{1,2},{2,4},{3,6},{4,1},{5,3},{6,5},{7,7},{8,8},{9,10},{10,1... | collective-permute-start | bytes 786440 | tf_op jit(solution)/shard_map/ppermute | solution.py:171
  6.5 0.1 collective-permute-start.1
  6.6 1.0 %collective-permute-start.2 = (f32[2,4,32,256]{3,2,1,0:T(8,128)S(1)}, f32[2,4,32,256]{3,2,1,0:T(8,128)S(1)}, u32[]{:S(2)}, u32[]{:S(2)}) collective-permute-start(f32[2,4,32,256]{3,2,1,0:T(8,128)S(1)} %get-tuple-element.18), channel_id=1, source_target_pairs={{0,4},{1,6},{2,0},{3,2},{4,5},{5,7},{6,1},{7,3},{8,12},{9,14},{10,... | collective-permute-start | bytes 786440 | tf_op jit(solution)/shard_map/ppermute | solution.py:171
  7.6 3.6 %collective-permute-start.3 = (f32[2,4,32,256]{3,2,1,0:T(8,128)S(1)}, f32[2,4,32,256]{3,2,1,0:T(8,128)S(1)}, u32[]{:S(2)}, u32[]{:S(2)}) collective-permute-start(f32[2,4,32,256]{3,2,1,0:T(8,128)S(1)} %get-tuple-element.15), channel_id=1, source_target_pairs={{0,6},{1,4},{2,2},{3,0},{4,7},{5,5},{6,3},{7,1},{8,14},{9,12},{10,... | collective-permute-start | bytes 786440 | tf_op jit(solution)/shard_map/ppermute | solution.py:171
  11.2 0.1 constant_dynamic-slice_fusion
  11.3 1.9 %collective-permute-start.4 = (s32[4,32,256]{2,1,0:T(8,128)S(1)}, s32[4,32,256]{2,1,0:T(8,128)S(1)}, u32[]{:S(2)}, u32[]{:S(2)}) collective-permute-start(s32[4,32,256]{2,1,0:T(8,128)S(1)} %get-tuple-element.25), channel_id=1, source_target_pairs={{0,0},{1,2},{2,4},{3,6},{4,1},{5,3},{6,5},{7,7},{8,8},{9,10},{10,1... | collective-permute-start | bytes 393224 | tf_op jit(solution)/shard_map/ppermute | solution.py:174
  13.2 0.0 collective-permute-done.refs_0_
  13.2 0.0 copy-start
  13.2 0.1 collective-permute-start.5
  13.3 0.1 collective-permute-done.1.refs_1_
  13.4 6.8 %collective-permute-start.6 = (s32[4,32,256]{2,1,0:T(8,128)S(1)}, s32[4,32,256]{2,1,0:T(8,128)S(1)}, u32[]{:S(2)}, u32[]{:S(2)}) collective-permute-start(s32[4,32,256]{2,1,0:T(8,128)S(1)} %get-tuple-element.26), channel_id=1, source_target_pairs={{0,4},{1,6},{2,0},{3,2},{4,5},{5,7},{6,1},{7,3},{8,12},{9,14},{10,... | collective-permute-start | bytes 393224 | tf_op jit(solution)/shard_map/ppermute | solution.py:174
  20.2 0.0 collective-permute-done.2.refs_2_
  20.2 3.7 %collective-permute-start.7 = (s32[4,32,256]{2,1,0:T(8,128)S(1)}, s32[4,32,256]{2,1,0:T(8,128)S(1)}, u32[]{:S(2)}, u32[]{:S(2)}) collective-permute-start(s32[4,32,256]{2,1,0:T(8,128)S(1)} %get-tuple-element.23), channel_id=1, source_target_pairs={{0,6},{1,4},{2,2},{3,0},{4,7},{5,5},{6,3},{7,1},{8,14},{9,12},{10,... | collective-permute-start | bytes 393224 | tf_op jit(solution)/shard_map/ppermute | solution.py:174
  23.9 0.0 collective-permute-done.3.refs_3_
  23.9 0.1 broadcast_select_fusion
  24.1 0.6 copy-done.3
  24.7 0.0 copy-start.17
  24.7 0.1 collective-permute-start.8
  24.8 0.0 collective-permute-done.4.refs_4_
  24.8 1.7 %collective-permute-start.9 = (f32[2,4,32,256]{3,2,1,0:T(8,128)S(1)}, f32[2,4,32,256]{3,2,1,0:T(8,128)S(1)}, u32[]{:S(2)}, u32[]{:S(2)}) collective-permute-start(f32[2,4,32,256]{3,2,1,0:T(8,128)S(1)} %get-tuple-element.12), channel_id=1, source_target_pairs={{0,25},{1,8},{2,27},{3,10},{4,29},{5,12},{6,31},{7,14},{8,1},{9,16... | collective-permute-start | bytes 786440 | tf_op jit(solution)/shard_map/ppermute | solution.py:185
  26.4 0.7 %copy-done.12 = f32[3,8]{1,0:T(4,128)S(1)} copy-done((f32[3,8]{1,0:T(4,128)S(1)}, f32[3,8]{1,0:T(4,128)}, u32[]{:S(2)}) %copy-start.12) | copy-done | bytes 120
  27.1 0.0 collective-permute-done.5.refs_5_
  27.1 0.0 collective-permute-done.6.refs_6_
  27.2 0.0 collective-permute-done.7.refs_7_
  27.2 0.0 collective-permute-done.8.refs_8_
  27.2 5.5 %collective-permute-done.9.refs_9_ = f32[2,4,32,256]{3,2,1,0:T(8,128)S(1)} collective-permute-done((f32[2,4,32,256]{3,2,1,0:T(8,128)S(1)}, f32[2,4,32,256]{3,2,1,0:T(8,128)S(1)}, u32[]{:S(2)}, u32[]{:S(2)}) %collective-permute-start.9) | collective-permute-done | bytes 262176 | tf_op jit(solution)/shard_map/ppermute | solution.py:185
  32.7 0.6 %broadcast_in_dim.2.refs_10_ = f32[4,8,128]{2,1,0:T(8,128)} broadcast(f32[4,128]{1,0:T(4,128)S(1)} %select_maximum_fusion), dimensions={0,2} | broadcast | bytes 18432 | tf_op jit(solution)/shard_map/broadcast_in_dim | solution.py:165
  33.4 0.0 copy-done.6
  33.4 4.8 %sweep.1 = (f32[4,32,256]{2,1,0:T(8,128)}, f32[4,32,256]{2,1,0:T(8,128)}, f32[4,32,256]{2,1,0:T(8,128)}, f32[4,32,256]{2,1,0:T(8,128)}, f32[4,32,256]{2,1,0:T(8,128)}) custom-call(f32[2,4,32,256]{3,2,1,0:T(8,128)} %copy-done, f32[2,4,32,256]{3,2,1,0:T(8,128)} %copy-done.1, f32[2,4,32,256]{3,2,1,0:T(8,128)} %copy-done.2, f32[2,4,32,256]{3,2,1,0:T(8,128)} %copy-done.3, ...), custom_call_target="tpu_custom_call" | custom-call | flops 26214400 | bytes 2097152 | tf_op jit(solution)/shard_map/sweep/pallas_call | solution.py:128
  38.2 0.9 %dynamic-slice_bitcast_fusion = f32[4,16,256]{2,1,0:T(8,128)S(1)} fusion(f32[4,2,16,256]{3,2,1,0:T(8,128)} %bitcast.19, s32[]{:T(128)S(6)} %select_n.292), kind=kLoop, calls=%fused_computation.17 | loop fusion | bytes 131076 | tf_op jit(solution)/shard_map/jit(dynamic_index_in_dim)/squeeze | solution.py:192
  39.2 2.4 %collective-permute-start.14 = (f32[4,16,256]{2,1,0:T(8,128)S(1)}, f32[4,16,256]{2,1,0:T(8,128)S(1)}, u32[]{:S(2)}, u32[]{:S(2)}) collective-permute-start(f32[4,16,256]{2,1,0:T(8,128)S(1)} %dynamic-slice_bitcast_fusion), channel_id=1, source_target_pairs={{0,1},{1,0},{2,3},{3,2},{4,5},{5,4},{6,7},{7,6},{8,9},{9,8},{10,11... | collective-permute-start | bytes 196616 | tf_op jit(solution)/shard_map/ppermute | solution.py:193
  41.6 0.9 %collective-permute-done.14 = f32[4,16,256]{2,1,0:T(8,128)S(1)} collective-permute-done((f32[4,16,256]{2,1,0:T(8,128)S(1)}, f32[4,16,256]{2,1,0:T(8,128)S(1)}, u32[]{:S(2)}, u32[]{:S(2)}) %collective-permute-start.14) | collective-permute-done | bytes 65568 | tf_op jit(solution)/shard_map/ppermute | solution.py:193
  42.6 2.1 %collective-permute-start.15 = (f32[4,16,256]{2,1,0:T(8,128)S(1)}, f32[4,16,256]{2,1,0:T(8,128)S(1)}, u32[]{:S(2)}, u32[]{:S(2)}) collective-permute-start(f32[4,16,256]{2,1,0:T(8,128)S(1)} %pad_maximum_fusion.1), channel_id=1, source_target_pairs={{0,24},{8,16},{16,8},{24,0},{1,25},{9,17},{17,9},{25,1},{2,26},{10... | collective-permute-start | bytes 196616 | tf_op jit(solution)/shard_map/ppermute | solution.py:197
  44.7 1.5 %collective-permute-start.17 = (f32[4,16,256]{2,1,0:T(8,128)S(1)}, f32[4,16,256]{2,1,0:T(8,128)S(1)}, u32[]{:S(2)}, u32[]{:S(2)}) collective-permute-start(f32[4,16,256]{2,1,0:T(8,128)S(1)} %pad_maximum_fusion.1), channel_id=1, source_target_pairs={{0,8},{8,0},{16,24},{24,16},{1,9},{9,1},{17,25},{25,17},{2,10},{10... | collective-permute-start | bytes 196616 | tf_op jit(solution)/shard_map/ppermute | solution.py:197
  46.2 2.4 %collective-permute-start.10 = (f32[4,32,256]{2,1,0:T(8,128)S(1)}, f32[4,32,256]{2,1,0:T(8,128)S(1)}, u32[]{:S(2)}, u32[]{:S(2)}) collective-permute-start(f32[4,32,256]{2,1,0:T(8,128)S(1)} %copy-done.16), channel_id=1, source_target_pairs={{6,0},{4,1},{2,2},{0,3},{7,4},{5,5},{3,6},{1,7},{14,8},{12,9},{10,... | collective-permute-start | bytes 393224 | tf_op jit(solution)/shard_map/ppermute | solution.py:198
  48.7 3.2 %collective-permute-start.11 = (f32[4,32,256]{2,1,0:T(8,128)S(1)}, f32[4,32,256]{2,1,0:T(8,128)S(1)}, u32[]{:S(2)}, u32[]{:S(2)}) collective-permute-start(f32[4,32,256]{2,1,0:T(8,128)S(1)} %copy-done.15), channel_id=1, source_target_pairs={{4,0},{6,1},{0,2},{2,3},{5,4},{7,5},{1,6},{3,7},{12,8},{14,9},{8,1... | collective-permute-start | bytes 393224 | tf_op jit(solution)/shard_map/ppermute | solution.py:198
  51.9 0.0 collective-permute-done.15
  51.9 0.0 collective-permute-start.12
  52.0 1.9 %collective-permute-start.13 = (f32[4,32,256]{2,1,0:T(8,128)S(1)}, f32[4,32,256]{2,1,0:T(8,128)S(1)}, u32[]{:S(2)}, u32[]{:S(2)}) collective-permute-start(f32[4,32,256]{2,1,0:T(8,128)S(1)} %copy-done.13), channel_id=1, source_target_pairs={{0,0},{2,1},{4,2},{6,3},{1,4},{3,5},{5,6},{7,7},{8,8},{10,9},{12,1... | collective-permute-start | bytes 393224 | tf_op jit(solution)/shard_map/ppermute | solution.py:198
  53.9 0.0 collective-permute-done.17
  54.0 0.7 %copy.6 = f32[1,4,16,256]{3,1,2,0:T(4,128)} copy(f32[1,4,16,256]{3,2,1,0:T(8,128)S(1)} %maximum_bitcast_fusion) | data formatting | bytes 131072
  54.7 0.0 collective-permute-done.10
  54.7 1.9 %collective-permute-done.11 = f32[4,32,256]{2,1,0:T(8,128)S(1)} collective-permute-done((f32[4,32,256]{2,1,0:T(8,128)S(1)}, f32[4,32,256]{2,1,0:T(8,128)S(1)}, u32[]{:S(2)}, u32[]{:S(2)}) %collective-permute-start.11) | collective-permute-done | bytes 131104 | tf_op jit(solution)/shard_map/ppermute | solution.py:198
  56.6 0.1 collective-permute-done.12
  56.7 1.7 %collective-permute-done.13 = f32[4,32,256]{2,1,0:T(8,128)S(1)} collective-permute-done((f32[4,32,256]{2,1,0:T(8,128)S(1)}, f32[4,32,256]{2,1,0:T(8,128)S(1)}, u32[]{:S(2)}, u32[]{:S(2)}) %collective-permute-start.13) | collective-permute-done | bytes 131104 | tf_op jit(solution)/shard_map/ppermute | solution.py:198
  58.3 0.1 select_select_fusion.5
  58.4 0.8 %pad_maximum_fusion = f32[4,128,256]{2,1,0:T(8,128)} fusion(f32[4,32,256]{2,1,0:T(8,128)S(1)} %get-tuple-element.20, f32[4,32,256]{2,1,0:T(8,128)S(1)} %get-tuple-element.21, f32[4,32,256]{2,1,0:T(8,128)S(1)} %get-tuple-element.22, f32[4,32,256]{2,1,0:T(8,128)S(1)} %get-tuple-element.19), kind=kLoop, calls=%fused_computation | loop fusion | flops 393216 | bytes 1048576 | tf_op jit(solution)/shard_map/concatenate | solution.py:201
  (45 shorter events, 0.2 us)
Async XLA Ops:
  0.7 10.5 %copy-start.4 = (s32[4,128,256]{2,1,0:T(8,128)S(1)}, s32[4,128,256]{2,1,0:T(8,128)}, u32[]{:S(2)}) copy-start(s32[4,128,256]{2,1,0:T(8,128)} %param.5) | copy-start | bytes 1572868
  2.0 11.2 %collective-permute-start = (f32[2,4,32,256]{3,2,1,0:T(8,128)S(1)}, f32[2,4,32,256]{3,2,1,0:T(8,128)S(1)}, u32[]{:S(2)}, u32[]{:S(2)}) collective-permute-start(f32[2,4,32,256]{3,2,1,0:T(8,128)S(1)} %get-tuple-element.17), channel_id=1, source_target_pairs={{0,0},{1,2},{2,4},{3,6},{4,1},{5,3},{6,5},{7,7},{8,8},{9,10},{10,1... | collective-permute-start | bytes 786440 | tf_op jit(solution)/shard_map/ppermute | solution.py:171
  6.5 6.9 %collective-permute-start.1 = (f32[2,4,32,256]{3,2,1,0:T(8,128)S(1)}, f32[2,4,32,256]{3,2,1,0:T(8,128)S(1)}, u32[]{:S(2)}, u32[]{:S(2)}) collective-permute-start(f32[2,4,32,256]{3,2,1,0:T(8,128)S(1)} %get-tuple-element.16), channel_id=1, source_target_pairs={{0,2},{1,0},{2,6},{3,4},{4,3},{5,1},{6,7},{7,5},{8,10},{9,8},{10,1... | collective-permute-start | bytes 786440 | tf_op jit(solution)/shard_map/ppermute | solution.py:171
  6.6 13.6 %collective-permute-start.2 = (f32[2,4,32,256]{3,2,1,0:T(8,128)S(1)}, f32[2,4,32,256]{3,2,1,0:T(8,128)S(1)}, u32[]{:S(2)}, u32[]{:S(2)}) collective-permute-start(f32[2,4,32,256]{3,2,1,0:T(8,128)S(1)} %get-tuple-element.18), channel_id=1, source_target_pairs={{0,4},{1,6},{2,0},{3,2},{4,5},{5,7},{6,1},{7,3},{8,12},{9,14},{10,... | collective-permute-start | bytes 786440 | tf_op jit(solution)/shard_map/ppermute | solution.py:171
  7.6 16.3 %collective-permute-start.3 = (f32[2,4,32,256]{3,2,1,0:T(8,128)S(1)}, f32[2,4,32,256]{3,2,1,0:T(8,128)S(1)}, u32[]{:S(2)}, u32[]{:S(2)}) collective-permute-start(f32[2,4,32,256]{3,2,1,0:T(8,128)S(1)} %get-tuple-element.15), channel_id=1, source_target_pairs={{0,6},{1,4},{2,2},{3,0},{4,7},{5,5},{6,3},{7,1},{8,14},{9,12},{10,... | collective-permute-start | bytes 786440 | tf_op jit(solution)/shard_map/ppermute | solution.py:171
  11.3 13.5 %collective-permute-start.4 = (s32[4,32,256]{2,1,0:T(8,128)S(1)}, s32[4,32,256]{2,1,0:T(8,128)S(1)}, u32[]{:S(2)}, u32[]{:S(2)}) collective-permute-start(s32[4,32,256]{2,1,0:T(8,128)S(1)} %get-tuple-element.25), channel_id=1, source_target_pairs={{0,0},{1,2},{2,4},{3,6},{4,1},{5,3},{6,5},{7,7},{8,8},{9,10},{10,1... | collective-permute-start | bytes 393224 | tf_op jit(solution)/shard_map/ppermute | solution.py:174
  13.2 10.8 %copy-start = (f32[2,4,32,256]{3,2,1,0:T(8,128)}, f32[2,4,32,256]{3,2,1,0:T(8,128)S(1)}, u32[]{:S(2)}) copy-start(f32[2,4,32,256]{3,2,1,0:T(8,128)S(1)} %collective-permute-done.refs_0_) | copy-start | bytes 786436
  13.2 13.9 %collective-permute-start.5 = (s32[4,32,256]{2,1,0:T(8,128)S(1)}, s32[4,32,256]{2,1,0:T(8,128)S(1)}, u32[]{:S(2)}, u32[]{:S(2)}) collective-permute-start(s32[4,32,256]{2,1,0:T(8,128)S(1)} %get-tuple-element.24), channel_id=1, source_target_pairs={{0,2},{1,0},{2,6},{3,4},{4,3},{5,1},{6,7},{7,5},{8,10},{9,8},{10,1... | collective-permute-start | bytes 393224 | tf_op jit(solution)/shard_map/ppermute | solution.py:174
  13.4 10.6 %copy-start.1 = (f32[2,4,32,256]{3,2,1,0:T(8,128)}, f32[2,4,32,256]{3,2,1,0:T(8,128)S(1)}, u32[]{:S(2)}) copy-start(f32[2,4,32,256]{3,2,1,0:T(8,128)S(1)} %collective-permute-done.1.refs_1_) | copy-start | bytes 786436
  13.4 13.7 %collective-permute-start.6 = (s32[4,32,256]{2,1,0:T(8,128)S(1)}, s32[4,32,256]{2,1,0:T(8,128)S(1)}, u32[]{:S(2)}, u32[]{:S(2)}) collective-permute-start(s32[4,32,256]{2,1,0:T(8,128)S(1)} %get-tuple-element.26), channel_id=1, source_target_pairs={{0,4},{1,6},{2,0},{3,2},{4,5},{5,7},{6,1},{7,3},{8,12},{9,14},{10,... | collective-permute-start | bytes 393224 | tf_op jit(solution)/shard_map/ppermute | solution.py:174
  20.2 3.8 %copy-start.2 = (f32[2,4,32,256]{3,2,1,0:T(8,128)}, f32[2,4,32,256]{3,2,1,0:T(8,128)S(1)}, u32[]{:S(2)}) copy-start(f32[2,4,32,256]{3,2,1,0:T(8,128)S(1)} %collective-permute-done.2.refs_2_) | copy-start | bytes 786436
  20.2 7.0 %collective-permute-start.7 = (s32[4,32,256]{2,1,0:T(8,128)S(1)}, s32[4,32,256]{2,1,0:T(8,128)S(1)}, u32[]{:S(2)}, u32[]{:S(2)}) collective-permute-start(s32[4,32,256]{2,1,0:T(8,128)S(1)} %get-tuple-element.23), channel_id=1, source_target_pairs={{0,6},{1,4},{2,2},{3,0},{4,7},{5,5},{6,3},{7,1},{8,14},{9,12},{10,... | collective-permute-start | bytes 393224 | tf_op jit(solution)/shard_map/ppermute | solution.py:174
  23.9 0.7 %copy-start.3 = (f32[2,4,32,256]{3,2,1,0:T(8,128)}, f32[2,4,32,256]{3,2,1,0:T(8,128)S(1)}, u32[]{:S(2)}) copy-start(f32[2,4,32,256]{3,2,1,0:T(8,128)S(1)} %collective-permute-done.3.refs_3_) | copy-start | bytes 786436
  24.7 1.8 %copy-start.17 = (f32[8]{0:T(128)S(1)}, f32[8]{0:T(128)}, u32[]{:S(2)}) copy-start(f32[8]{0:T(128)} %param.7) | copy-start | bytes 100
  24.7 2.5 %collective-permute-start.8 = (f32[2,4,32,256]{3,2,1,0:T(8,128)S(1)}, f32[2,4,32,256]{3,2,1,0:T(8,128)S(1)}, u32[]{:S(2)}, u32[]{:S(2)}) collective-permute-start(f32[2,4,32,256]{3,2,1,0:T(8,128)S(1)} %broadcast_select_fusion.1), channel_id=1, source_target_pairs={{0,1},{1,0},{2,3},{3,2},{4,5},{5,4},{6,7},{7,6},{8,9},{9,8},{10,11... | collective-permute-start | bytes 786440 | tf_op jit(solution)/shard_map/ppermute | solution.py:186
  24.8 8.6 %copy-start.7 = (s32[4,32,256]{2,1,0:T(8,128)}, s32[4,32,256]{2,1,0:T(8,128)S(1)}, u32[]{:S(2)}) copy-start(s32[4,32,256]{2,1,0:T(8,128)S(1)} %collective-permute-done.4.refs_4_) | copy-start | bytes 393220
  24.8 7.9 %collective-permute-start.9 = (f32[2,4,32,256]{3,2,1,0:T(8,128)S(1)}, f32[2,4,32,256]{3,2,1,0:T(8,128)S(1)}, u32[]{:S(2)}, u32[]{:S(2)}) collective-permute-start(f32[2,4,32,256]{3,2,1,0:T(8,128)S(1)} %get-tuple-element.12), channel_id=1, source_target_pairs={{0,25},{1,8},{2,27},{3,10},{4,29},{5,12},{6,31},{7,14},{8,1},{9,16... | collective-permute-start | bytes 786440 | tf_op jit(solution)/shard_map/ppermute | solution.py:185
  26.4 0.7 %copy-start.12 = (f32[3,8]{1,0:T(4,128)S(1)}, f32[3,8]{1,0:T(4,128)}, u32[]{:S(2)}) copy-start(f32[3,8]{1,0:T(4,128)} %param.6) | copy-start | bytes 292
  27.1 6.2 %copy-start.8 = (s32[4,32,256]{2,1,0:T(8,128)}, s32[4,32,256]{2,1,0:T(8,128)S(1)}, u32[]{:S(2)}) copy-start(s32[4,32,256]{2,1,0:T(8,128)S(1)} %collective-permute-done.5.refs_5_) | copy-start | bytes 393220
  27.2 6.2 %copy-start.9 = (s32[4,32,256]{2,1,0:T(8,128)}, s32[4,32,256]{2,1,0:T(8,128)S(1)}, u32[]{:S(2)}) copy-start(s32[4,32,256]{2,1,0:T(8,128)S(1)} %collective-permute-done.6.refs_6_) | copy-start | bytes 393220
  27.2 6.2 %copy-start.10 = (s32[4,32,256]{2,1,0:T(8,128)}, s32[4,32,256]{2,1,0:T(8,128)S(1)}, u32[]{:S(2)}) copy-start(s32[4,32,256]{2,1,0:T(8,128)S(1)} %collective-permute-done.7.refs_7_) | copy-start | bytes 393220
  27.2 6.2 %copy-start.5 = (f32[2,4,32,256]{3,2,1,0:T(8,128)}, f32[2,4,32,256]{3,2,1,0:T(8,128)S(1)}, u32[]{:S(2)}) copy-start(f32[2,4,32,256]{3,2,1,0:T(8,128)S(1)} %collective-permute-done.8.refs_8_) | copy-start | bytes 786436
  32.7 0.7 %copy-start.6 = (f32[2,4,32,256]{3,2,1,0:T(8,128)}, f32[2,4,32,256]{3,2,1,0:T(8,128)S(1)}, u32[]{:S(2)}) copy-start(f32[2,4,32,256]{3,2,1,0:T(8,128)S(1)} %collective-permute-done.9.refs_9_) | copy-start | bytes 786436
  38.2 4.3 %copy-start.11 = (f32[4,32,256]{2,1,0:T(8,128)S(1)}, f32[4,32,256]{2,1,0:T(8,128)}, u32[]{:S(2)}) copy-start(f32[4,32,256]{2,1,0:T(8,128)} %get-tuple-element.11) | copy-start | bytes 393220
  39.2 3.3 %collective-permute-start.14 = (f32[4,16,256]{2,1,0:T(8,128)S(1)}, f32[4,16,256]{2,1,0:T(8,128)S(1)}, u32[]{:S(2)}, u32[]{:S(2)}) collective-permute-start(f32[4,16,256]{2,1,0:T(8,128)S(1)} %dynamic-slice_bitcast_fusion), channel_id=1, source_target_pairs={{0,1},{1,0},{2,3},{3,2},{4,5},{5,4},{6,7},{7,6},{8,9},{9,8},{10,11... | collective-permute-start | bytes 196616 | tf_op jit(solution)/shard_map/ppermute | solution.py:193
  42.5 3.7 %copy-start.16 = (f32[4,32,256]{2,1,0:T(8,128)S(1)}, f32[4,32,256]{2,1,0:T(8,128)}, u32[]{:S(2)}) copy-start(f32[4,32,256]{2,1,0:T(8,128)} %get-tuple-element.7) | copy-start | bytes 393220
  42.5 6.1 %copy-start.15 = (f32[4,32,256]{2,1,0:T(8,128)S(1)}, f32[4,32,256]{2,1,0:T(8,128)}, u32[]{:S(2)}) copy-start(f32[4,32,256]{2,1,0:T(8,128)} %get-tuple-element.8) | copy-start | bytes 393220
  42.6 9.4 %copy-start.14 = (f32[4,32,256]{2,1,0:T(8,128)S(1)}, f32[4,32,256]{2,1,0:T(8,128)}, u32[]{:S(2)}) copy-start(f32[4,32,256]{2,1,0:T(8,128)} %get-tuple-element.9) | copy-start | bytes 393220
  42.6 9.4 %copy-start.13 = (f32[4,32,256]{2,1,0:T(8,128)S(1)}, f32[4,32,256]{2,1,0:T(8,128)}, u32[]{:S(2)}) copy-start(f32[4,32,256]{2,1,0:T(8,128)} %get-tuple-element.10) | copy-start | bytes 393220
  42.6 9.3 %collective-permute-start.15 = (f32[4,16,256]{2,1,0:T(8,128)S(1)}, f32[4,16,256]{2,1,0:T(8,128)S(1)}, u32[]{:S(2)}, u32[]{:S(2)}) collective-permute-start(f32[4,16,256]{2,1,0:T(8,128)S(1)} %pad_maximum_fusion.1), channel_id=1, source_target_pairs={{0,24},{8,16},{16,8},{24,0},{1,25},{9,17},{17,9},{25,1},{2,26},{10... | collective-permute-start | bytes 196616 | tf_op jit(solution)/shard_map/ppermute | solution.py:197
  44.7 7.2 %collective-permute-start.16 = (f32[4,16,256]{2,1,0:T(8,128)S(1)}, f32[4,16,256]{2,1,0:T(8,128)S(1)}, u32[]{:S(2)}, u32[]{:S(2)}) collective-permute-start(f32[4,16,256]{2,1,0:T(8,128)S(1)} %pad_maximum_fusion.1), channel_id=1, source_target_pairs={{0,16},{8,24},{16,0},{24,8},{1,17},{9,25},{17,1},{25,9},{2,18},{10... | collective-permute-start | bytes 196616 | tf_op jit(solution)/shard_map/ppermute | solution.py:197
  44.7 9.2 %collective-permute-start.17 = (f32[4,16,256]{2,1,0:T(8,128)S(1)}, f32[4,16,256]{2,1,0:T(8,128)S(1)}, u32[]{:S(2)}, u32[]{:S(2)}) collective-permute-start(f32[4,16,256]{2,1,0:T(8,128)S(1)} %pad_maximum_fusion.1), channel_id=1, source_target_pairs={{0,8},{8,0},{16,24},{24,16},{1,9},{9,1},{17,25},{25,17},{2,10},{10... | collective-permute-start | bytes 196616 | tf_op jit(solution)/shard_map/ppermute | solution.py:197
  46.2 8.5 %collective-permute-start.10 = (f32[4,32,256]{2,1,0:T(8,128)S(1)}, f32[4,32,256]{2,1,0:T(8,128)S(1)}, u32[]{:S(2)}, u32[]{:S(2)}) collective-permute-start(f32[4,32,256]{2,1,0:T(8,128)S(1)} %copy-done.16), channel_id=1, source_target_pairs={{6,0},{4,1},{2,2},{0,3},{7,4},{5,5},{3,6},{1,7},{14,8},{12,9},{10,... | collective-permute-start | bytes 393224 | tf_op jit(solution)/shard_map/ppermute | solution.py:198
  48.7 7.9 %collective-permute-start.11 = (f32[4,32,256]{2,1,0:T(8,128)S(1)}, f32[4,32,256]{2,1,0:T(8,128)S(1)}, u32[]{:S(2)}, u32[]{:S(2)}) collective-permute-start(f32[4,32,256]{2,1,0:T(8,128)S(1)} %copy-done.15), channel_id=1, source_target_pairs={{4,0},{6,1},{0,2},{2,3},{5,4},{7,5},{1,6},{3,7},{12,8},{14,9},{8,1... | collective-permute-start | bytes 393224 | tf_op jit(solution)/shard_map/ppermute | solution.py:198
  51.9 4.7 %collective-permute-start.12 = (f32[4,32,256]{2,1,0:T(8,128)S(1)}, f32[4,32,256]{2,1,0:T(8,128)S(1)}, u32[]{:S(2)}, u32[]{:S(2)}) collective-permute-start(f32[4,32,256]{2,1,0:T(8,128)S(1)} %copy-done.14), channel_id=1, source_target_pairs={{2,0},{0,1},{6,2},{4,3},{3,4},{1,5},{7,6},{5,7},{10,8},{8,9},{14,1... | collective-permute-start | bytes 393224 | tf_op jit(solution)/shard_map/ppermute | solution.py:198
  52.0 6.4 %collective-permute-start.13 = (f32[4,32,256]{2,1,0:T(8,128)S(1)}, f32[4,32,256]{2,1,0:T(8,128)S(1)}, u32[]{:S(2)}, u32[]{:S(2)}) collective-permute-start(f32[4,32,256]{2,1,0:T(8,128)S(1)} %copy-done.13), channel_id=1, source_target_pairs={{0,0},{2,1},{4,2},{6,3},{1,4},{3,5},{5,6},{7,7},{8,8},{10,9},{12,1... | collective-permute-start | bytes 393224 | tf_op jit(solution)/shard_map/ppermute | solution.py:198

commit v2 on v1

v2 whole, which is shorter than its diff:
```python
import functools

import jax
import jax.numpy as jnp
from jax import lax
from jax.experimental import pallas as pl
from jax.experimental.pallas import tpu as pltpu
from jax.sharding import PartitionSpec as P

COURANT = 0.4
DEPTH_SCALE = 2.5
LANES = 128
F32 = jnp.float32
VMEM = pl.BlockSpec(memory_space=pltpu.VMEM)


def swap_pairs(members, mask):
    return [(w, w ^ mask) for w in range(members)]


def pick(arrays, index):
    out = arrays[0]
    for number in range(1, len(arrays)):
        out = jnp.where(index == number, arrays[number], out)
    return out


def advance(state, stage, density, momentum, emit):
    if stage == 4:
        emit(density)
        return
    last = stage == 3
    velocity = momentum / density
    speed = jnp.abs(velocity) + 1.0
    pressure = None if last else momentum * velocity + density
    held = state[stage]
    if held is None:
        state[stage] = (density, momentum, speed, pressure, None, None)
        return
    density0, momentum0, speed0, pressure0, mass0, force0 = held
    face = jnp.maximum(speed0, speed)
    mass = (momentum0 + momentum) - face * (density - density0)
    force = None if last else (pressure0 + pressure) - face * (momentum - momentum0)
    state[stage] = (density, momentum, speed, pressure, mass, force)
    if mass0 is None:
        return
    density1 = density0 - (0.5 * COURANT) * (mass - mass0)
    momentum1 = None if last else momentum0 - (0.5 * COURANT) * (force - force0)
    advance(state, stage + 1, density1, momentum1, emit)


def sweep_tiles(rows, columns, layers, count, backwards, load, dense_at, dense, kind_at, kind, table, finish):
    tall = min(8, rows)
    across = columns // LANES

    def tile(number, carry):
        row = pl.ds(pl.multiple_of(number // across * tall, tall), tall)
        column = pl.ds(pl.multiple_of(number % across * LANES, LANES), LANES)

        def block(state, light, position):
            for layer in range(layers):
                at = position * layers + layer

                def emit(density):
                    own = at - 2 * layers
                    dense[dense_at(own), row, column] = density
                    which = kind[kind_at(own), row, column]
                    factor, red, green, blue = (
                        jnp.take_along_axis(table[n, :tall, :], which, axis=1) for n in range(4)
                    )
                    through = jnp.exp(-(factor * density))
                    hidden = 1.0 - through
                    weight = jnp.where(backwards, hidden, hidden * light[0])
                    keep = jnp.where(backwards, through, 1.0)
                    light[0] = light[0] * through
                    light[1] = light[1] * keep + weight * red
                    light[2] = light[2] * keep + weight * green
                    light[3] = light[3] * keep + weight * blue

                advance(state, 0, *load(at, row, column), emit)

        state = [None] * 4
        zero = jnp.zeros((tall, LANES), F32)
        light = [zero + 1.0, zero, zero, zero]
        block(state, light, 0)
        block(state, light, 1)
        if count <= 5:
            for position in range(2, count):
                block(state, light, position)
        else:

            def step(position, carry):
                state, light = [list(part) for part in carry]
                block(state, light, position)
                return state, light

            state, light = lax.fori_loop(2, count, step, (state, light))
        finish(light, row, column)
        return carry

    lax.fori_loop(0, rows // tall * across, tile, 0)


def inner_kernel(chips, *refs):
    own, own_kind = refs[:chips], refs[chips : 2 * chips]
    other, other_kind, table, dense, image, edge, edge_kind, fluid, kind = refs[2 * chips :]
    member = lax.axis_index("swap")
    chip, upper = member // 2, member % 2
    half = chips // 2
    _, layers, rows, columns = own[0].shape
    shift = upper
    for d in range(chips):
        k = chip ^ d

        @pl.when(k // half == upper)
        def _():
            at = 2 * (k - upper * half) + upper
            fluid[:, pl.ds((at + shift) * layers, layers)] = own[d][...]
            kind[pl.ds(at * layers, layers)] = own_kind[d][...]

        @pl.when(k == jnp.where(upper == 1, half - 1, half))
        def _():
            at = jnp.where(upper == 1, 0, chips)
            fluid[:, pl.ds(at * layers, layers)] = own[d][...]

    for i in range(half):
        at = 2 * i + 1 - upper
        fluid[:, pl.ds((at + shift) * layers, layers)] = other[i]
        kind[pl.ds(at * layers, layers)] = other_kind[i]

    total = (chips + 1) * layers
    sign = jnp.where(upper == 1, 1.0, -1.0)

    def load(at, row, column):
        at = jnp.where(upper == 1, at, total - 1 - at)
        return fluid[0, at, row, column], sign * fluid[1, at, row, column]

    def place(own):
        return jnp.where(upper == 1, own, chips * layers - 1 - own)

    def finish(light, row, column):
        for n in range(4):
            image[n, row, column] = light[n]

    sweep_tiles(rows, columns, layers, chips + 1, upper == 0, load, place, dense, place, kind, table, finish)
    start = jnp.where(upper == 1, chips - 1, 0) * layers
    edge[...] = fluid[:, pl.ds(start, 2 * layers)]
    start = jnp.where(upper == 1, chips - 1, 0) * layers
    edge_kind[...] = kind[pl.ds(start, layers)]


def outer_kernel(chips, far, edge, edge_kind, table, dense, image, keep, give, tile, last, drawn):
    upper = lax.axis_index("swap") % 2
    half = chips // 2
    _, layers, rows, columns = far.shape
    sign = jnp.where(upper == 1, -1.0, 1.0)

    def load(at, row, column):
        source, base, size = (far, at, layers) if at < layers else (edge, at - layers, 2 * layers)
        base = jnp.where(upper == 1, size - 1 - base, base)
        return source[0, base, row, column], sign * source[1, base, row, column]

    def place(own):
        return jnp.where(upper == 1, layers - 1 - own, own)

    def finish(light, row, column):
        inner = [image[n, row, column] for n in range(4)]
        front = [jnp.where(upper == 1, a, b) for a, b in zip(inner, light)]
        back = [jnp.where(upper == 1, b, a) for a, b in zip(inner, light)]
        drawn[3, row, column] = front[0] * back[0]
        for n in range(1, 4):
            drawn[n - 1, row, column] = front[n] + front[0] * back[n]

    sweep_tiles(rows, columns, layers, 3, upper == 1, load, place, last, place, edge_kind, table, finish)
    for i in range(half):
        keep[i] = dense[pl.ds((2 * i + upper) * layers, layers)]
        give[pl.ds(i * layers, layers)] = dense[pl.ds((2 * i + 1 - upper) * layers, layers)]

    @pl.when(upper == 0)
    def _():
        keep[0] = last[...]

    @pl.when(upper == 1)
    def _():
        keep[half - 1] = last[...]

    short = rows // 2
    for n in range(4):
        low, high = drawn[n, :short], drawn[n, short:]
        tile[n] = jnp.where(upper == 1, high, low)
        given = jnp.where(upper == 1, low, high)
        give[half * layers + n // 2, (n % 2) * short : (n % 2 + 1) * short] = given


def cost(cells):
    return pl.CostEstimate(flops=300 * cells, bytes_accessed=16 * cells, transcendentals=6 * cells)


def sweep_inner(own, own_kind, other, other_kind, table):
    chips = len(own)
    _, layers, rows, columns = own[0].shape
    shape = lambda *dims, dtype=F32: jax.ShapeDtypeStruct((*dims, rows, columns), dtype)
    return pl.pallas_call(
        functools.partial(inner_kernel, chips),
        out_shape=[
            shape(chips * layers),
            shape(4),
            shape(2, 2 * layers),
            shape(layers, dtype=jnp.int32),
        ],
        in_specs=[VMEM] * (2 * chips + 3),
        out_specs=[VMEM] * 4,
        scratch_shapes=[
            pltpu.VMEM((2, (chips + 1) * layers, rows, columns), F32),
            pltpu.VMEM((chips * layers, rows, columns), jnp.int32),
        ],
        cost_estimate=cost(chips * layers * rows * columns),
        name="sweep_inner",
    )(*own, *own_kind, other, other_kind, table)


def sweep_outer(far, edge, edge_kind, table, dense, image):
    layers, rows, columns = edge_kind.shape
    half = dense.shape[0] // layers // 2
    shape = lambda *dims: jax.ShapeDtypeStruct(dims, F32)
    return pl.pallas_call(
        functools.partial(outer_kernel, 2 * half),
        out_shape=[
            shape(half, layers, rows, columns),
            shape(half * layers + 2, rows, columns),
            shape(4, rows // 2, columns),
        ],
        in_specs=[VMEM] * 6,
        out_specs=[VMEM] * 3,
        scratch_shapes=[
            pltpu.VMEM((layers, rows, columns), F32),
            pltpu.VMEM((4, rows, columns), F32),
        ],
        cost_estimate=cost(layers * rows * columns),
        name="sweep_outer",
    )(far, edge, edge_kind, table, dense, image)


def over(nearer, farther):
    return jnp.concatenate([nearer[:3] + nearer[3:4] * farther[:3], nearer[3:4] * farther[3:4]], axis=0)


def per_device(fluid_state, material, table_colour, table_extinction):
    slabs = lax.axis_size("slab")
    members = lax.axis_size("swap")
    chips = members // 2
    half = chips // 2
    member = lax.axis_index("swap")
    slab = lax.axis_index("slab")
    chip, upper = member // 2, member % 2
    _, layers, height, width = fluid_state.shape
    rows = height // chips

    def to_chip(block, d):
        return lax.ppermute(block, "swap", swap_pairs(members, 2 * d)) if d else block

    def to_core(block):
        return lax.ppermute(block, "swap", swap_pairs(members, 1))

    scale = DEPTH_SCALE / (layers * slabs * members)
    table = jnp.concatenate([table_extinction[None] * scale, table_colour], axis=0)
    table = jnp.pad(table, ((0, 0), (0, LANES - table.shape[1])))
    table = jnp.broadcast_to(table[:, None, :], (4, 8, LANES))

    own = [
        to_chip(lax.dynamic_slice_in_dim(fluid_state, (chip ^ d) * rows, rows, axis=2), d) for d in range(chips)
    ]
    own_kind = [
        to_chip(lax.dynamic_slice_in_dim(material, (chip ^ d) * rows, rows, axis=1), d) for d in range(chips)
    ]

    def others(blocks):
        return jnp.stack([pick(blocks, chip ^ ((1 - upper) * half + i)) for i in range(half)])

    other = to_core(others(own))
    ring = []
    for z in range(slabs):
        for w in range(members):
            to = ((z + 1) % slabs, w - 1) if w % 2 else ((z - 1) % slabs, w + 1)
            ring.append((z * members + w, to[0] * members + to[1]))
    far = lax.ppermute(pick(own, chip ^ (upper * (chips - 1))), ("slab", "swap"), ring)
    other_kind = to_core(others(own_kind))

    dense, image, edge, edge_kind = sweep_inner(own, own_kind, other, other_kind, table)
    keep, give, tile = sweep_outer(far, edge, edge_kind, table, dense, image)
    got = to_core(give)

    partner = got[half * layers :].reshape(4, rows // 2, width)
    tile = over(jnp.where(upper == 1, partner, tile), jnp.where(upper == 1, tile, partner))
    pieces = [tile]
    for away in range(1, slabs):
        pieces.append(lax.ppermute(tile, "slab", swap_pairs(slabs, away)))
    ordered = [pick(pieces, slab ^ z) for z in range(slabs)]
    rendered = functools.reduce(over, ordered)
    rendered = jnp.concatenate([rendered[:3], 1.0 - rendered[3:4]], axis=0).reshape(4, height * width // members)

    kept = [keep[i] for i in range(half)]
    gotten = [got[i * layers : (i + 1) * layers] for i in range(half)]
    chunks = []
    for d in range(chips):
        k = chip ^ d
        block = jnp.where(k // half == upper, pick(kept, k % half), pick(gotten, k % half))
        chunks.append(to_chip(block, d))
    density = jnp.concatenate([pick(chunks, chip ^ j) for j in range(chips)], axis=1)
    return density, rendered


def solution(mesh):
    return jax.shard_map(
        per_device,
        mesh=mesh,
        in_specs=(P(None, ("slab", "swap"), None, None), P(("slab", "swap"), None, None), P(), P()),
        out_specs=(P(("slab", "swap"), None, None), P(None, "swap")),
        check_vma=False,
    )
```

time: 59.6 us -> 56.5 us (0.948)
  the two profiles are of different devices: /device:TPU:1 before, /device:TPU:0 now
where the time goes in v2:
time: 56.5 us; the launch traced here: 56.2 us
  starting transfers between devices  21.3 us (38%)
  waiting for transfers between devices  17.1 us (30%)
  Pallas kernels  8.31 us (15%)
  local copies, waits for them, and re-layouts  5.12 us (9%)
  other arithmetic  3.47 us (6%)
  between operations  0.97 us (2%)
    ppermute x9, waiting for transfers between devices, to_chip(): lax.ppermute(block, 'swap', swap_pairs(members, 2 * d))  14 us
    ppermute x9, starting transfers between devices, to_chip(): lax.ppermute(block, 'swap', swap_pairs(members, 2 * d))  12.9 us
    pallas_call x1, Pallas kernels, sweep_inner(): pl.pallas_call(functools.partial(inner_kernel, chips), out_shape=[shape(c...  4.91 us
    ppermute x3, starting transfers between devices, per_device(): pieces.append(lax.ppermute(tile, 'slab', swap_pairs(slabs, away)))  4.45 us
    pallas_call x1, Pallas kernels, sweep_outer(): pl.pallas_call(functools.partial(outer_kernel, 2 * half), out_shape=[shap...  3.4 us
    ppermute x1, starting transfers between devices, per_device(): lax.ppermute(pick(own, chip ^ upper * (chips - 1)), ('slab', 'swap'), ring)  3.29 us
    another operation x6, other arithmetic, others(): jnp.stack([pick(blocks, chip ^ (1 - upper) * half + i) for i in range(hal...  2.33 us
    unnamed x31, local copies, waits for them, and re-layouts  2.21 us
  transfers between devices with their start and end apart: 16, of which 10 were waited for; matrix products, arithmetic and copies ran while one was open for 7% of the time, Pallas kernels for 9%

profile of v2, /device:TPU:0, one launch (start us, length us, event | category | flops | bytes accessed | tf_op | source)
XLA Modules:
  0.0 56.2 jit_solution(338522459750893762)
XLA Ops:
  0.7 1.1 %constant_dynamic-slice_fusion.2 = (s32[4,32,256]{2,1,0:T(8,128)S(1)}, s32[4,32,256]{2,1,0:T(8,128)S(1)}, s32[4,32,256]{2,1,0:T(8,128)S(1)}) fusion(s32[4,128,256]{2,1,0:T(8,128)} %param.5, s32[]{:T(128)S(6)} %select_n.411, s32[]{:T(128)S(6)} %select_n.407, s32[]{:T(128)S(6)} %select_n.409), kind=kLoop, calls=%fused_computation.44 | loop fusion | bytes 786444 | tf_op jit(solution)/shard_map/dynamic_slice | solution.py:274
  1.7 4.0 %collective-permute-start.6 = (s32[4,32,256]{2,1,0:T(8,128)S(1)}, s32[4,32,256]{2,1,0:T(8,128)S(1)}, u32[]{:S(2)}, u32[]{:S(2)}) collective-permute-start(s32[4,32,256]{2,1,0:T(8,128)S(1)} %get-tuple-element.34), channel_id=1, source_target_pairs={{0,6},{1,7},{2,4},{3,5},{4,2},{5,3},{6,0},{7,1},{8,14},{9,15},{10,... | collective-permute-start | bytes 393224 | tf_op jit(solution)/shard_map/ppermute | solution.py:260
  5.7 0.5 collective-permute-start.5
  6.2 0.1 collective-permute-start.4
  6.4 1.2 %constant_dynamic-slice_fusion.5 = (f32[2,4,32,256]{3,2,1,0:T(8,128)S(1)}, f32[2,4,32,256]{3,2,1,0:T(8,128)S(1)}, f32[2,4,32,256]{3,2,1,0:T(8,128)S(1)}) fusion(f32[2,4,128,256]{3,2,1,0:T(8,128)} %param.4, s32[]{:T(128)S(6)} %select_n.411, s32[]{:T(128)S(6)} %select_n.409, s32[]{:T(128)S(6)} %select_n.407), kind=kLoop, calls=%fused_computation.47 | loop fusion | bytes 1572876 | tf_op jit(solution)/shard_map/dynamic_slice | solution.py:271
  7.5 2.9 %collective-permute-start = (f32[2,4,32,256]{3,2,1,0:T(8,128)S(1)}, f32[2,4,32,256]{3,2,1,0:T(8,128)S(1)}, u32[]{:S(2)}, u32[]{:S(2)}) collective-permute-start(f32[2,4,32,256]{3,2,1,0:T(8,128)S(1)} %get-tuple-element.26), channel_id=1, source_target_pairs={{0,6},{1,7},{2,4},{3,5},{4,2},{5,3},{6,0},{7,1},{8,14},{9,15},{10,... | collective-permute-start | bytes 786440 | tf_op jit(solution)/shard_map/ppermute | solution.py:260
  10.5 0.5 collective-permute-start.1
  11.0 0.0 collective-permute-done.6.refs_7_
  11.0 1.1 %collective-permute-start.2 = (f32[2,4,32,256]{3,2,1,0:T(8,128)S(1)}, f32[2,4,32,256]{3,2,1,0:T(8,128)S(1)}, u32[]{:S(2)}, u32[]{:S(2)}) collective-permute-start(f32[2,4,32,256]{3,2,1,0:T(8,128)S(1)} %get-tuple-element.24), channel_id=1, source_target_pairs={{0,2},{1,3},{2,0},{3,1},{4,6},{5,7},{6,4},{7,5},{8,10},{9,11},{10,... | collective-permute-start | bytes 786440 | tf_op jit(solution)/shard_map/ppermute | solution.py:260
  12.0 4.3 %collective-permute-done.5.refs_6_ = s32[4,32,256]{2,1,0:T(8,128)S(1)} collective-permute-done((s32[4,32,256]{2,1,0:T(8,128)S(1)}, s32[4,32,256]{2,1,0:T(8,128)S(1)}, u32[]{:S(2)}, u32[]{:S(2)}) %collective-permute-start.5) | collective-permute-done | bytes 131104 | tf_op jit(solution)/shard_map/ppermute | solution.py:260
  16.4 0.0 collective-permute-done.4.refs_5_
  16.4 1.0 %select_bitcast_fusion.3 = (s32[1,4,32,256]{3,2,1,0:T(8,128)S(1)}, s32[4,32,256]{2,1,0:T(8,128)S(1)}) fusion(s32[4,32,256]{2,1,0:T(8,128)S(1)} %collective-permute-done.6.refs_7_, s32[4,32,256]{2,1,0:T(8,128)S(1)} %collective-permute-done.5.refs_6_, s32[4,32,256]{2,1,0:T(8,128)S(1)} %collective-permute-done.4.refs_5_, pred[]{:T(512)S(6)} %eq.155, ...), kind=kLoop, calls=%fused_computation.15 | loop fusion | flops 98304 | bytes 786439 | tf_op jit(solution)/shard_map/stack | solution.py:278
  17.4 1.8 %collective-permute-done.refs_3_ = f32[2,4,32,256]{3,2,1,0:T(8,128)S(1)} collective-permute-done((f32[2,4,32,256]{3,2,1,0:T(8,128)S(1)}, f32[2,4,32,256]{3,2,1,0:T(8,128)S(1)}, u32[]{:S(2)}, u32[]{:S(2)}) %collective-permute-start) | collective-permute-done | bytes 262176 | tf_op jit(solution)/shard_map/ppermute | solution.py:260
  19.2 4.1 %collective-permute-done.1.refs_2_ = f32[2,4,32,256]{3,2,1,0:T(8,128)S(1)} collective-permute-done((f32[2,4,32,256]{3,2,1,0:T(8,128)S(1)}, f32[2,4,32,256]{3,2,1,0:T(8,128)S(1)}, u32[]{:S(2)}, u32[]{:S(2)}) %collective-permute-start.1) | collective-permute-done | bytes 262176 | tf_op jit(solution)/shard_map/ppermute | solution.py:260
  23.3 0.3 collective-permute-done.2.refs_1_
  23.6 1.1 %select_bitcast_fusion.1 = (f32[1,2,4,32,256]{4,3,2,1,0:T(8,128)S(1)}, f32[2,4,32,256]{3,2,1,0:T(8,128)S(1)}) fusion(f32[2,4,32,256]{3,2,1,0:T(8,128)S(1)} %collective-permute-done.refs_3_, f32[2,4,32,256]{3,2,1,0:T(8,128)S(1)} %collective-permute-done.1.refs_2_, f32[2,4,32,256]{3,2,1,0:T(8,128)S(1)} %collective-permute-done.2.refs_1_, pred[]{:T(512)S(6)} %eq.155, ...), kind=kLoop, calls=%fused_computation.4 | loop fusion | flops 196608 | bytes 1572871 | tf_op jit(solution)/shard_map/stack | solution.py:278
  24.7 0.1 select_bitcast_fusion
  24.8 0.6 %copy-done.3 = f32[2,4,32,256]{3,2,1,0:T(8,128)} copy-done((f32[2,4,32,256]{3,2,1,0:T(8,128)}, f32[2,4,32,256]{3,2,1,0:T(8,128)S(1)}, u32[]{:S(2)}) %copy-start.3) | copy-done | bytes 262168
  25.4 0.1 collective-permute-start.7
  25.6 0.0 copy-start.14
  25.7 0.0 copy-start.13
  25.7 0.5 collective-permute-start.8
  26.2 3.3 %collective-permute-start.3 = (f32[2,4,32,256]{3,2,1,0:T(8,128)S(1)}, f32[2,4,32,256]{3,2,1,0:T(8,128)S(1)}, u32[]{:S(2)}, u32[]{:S(2)}) collective-permute-start(f32[2,4,32,256]{3,2,1,0:T(8,128)S(1)} %get-tuple-element.23), channel_id=1, source_target_pairs={{0,25},{1,8},{2,27},{3,10},{4,29},{5,12},{6,31},{7,14},{8,1},{9,16... | collective-permute-start | bytes 786440 | tf_op jit(solution)/shard_map/ppermute | solution.py:286
  29.5 0.0 collective-permute-done.8.refs_9_
  29.5 0.0 collective-permute-done.7.refs_8_
  29.5 0.0 copy-start.9
  29.6 0.7 %broadcast_in_dim.2.refs_10_.table = f32[4,8,128]{2,1,0:T(8,128)} broadcast(f32[4,128]{1,0:T(4,128)S(1)} %select_maximum_fusion), dimensions={0,2} | broadcast | bytes 18432 | tf_op jit(solution)/shard_map/broadcast_in_dim | solution.py:268
  30.2 0.0 copy-done.11
  30.2 0.2 copy-done.9
  30.4 4.9 %sweep_inner.1 = (f32[16,32,256]{2,1,0:T(8,128)}, f32[4,32,256]{2,1,0:T(8,128)}, f32[2,8,32,256]{3,2,1,0:T(8,128)}, s32[4,32,256]{2,1,0:T(8,128)}) custom-call(f32[2,4,32,256]{3,2,1,0:T(8,128)} %copy-done.3, f32[2,4,32,256]{3,2,1,0:T(8,128)} %copy-done.2, f32[2,4,32,256]{3,2,1,0:T(8,128)} %copy-done.1, f32[2,4,32,256]{3,2,1,0:T(8,128)} %copy-done, ...), custom_call_target="tpu_custom_call" | custom-call | flops 39321600 | bytes 2097152 | tf_op jit(solution)/shard_map/sweep_inner/pallas_call | solution.py:203
  35.3 0.8 %collective-permute-done.3.far = f32[2,4,32,256]{3,2,1,0:T(8,128)S(1)} collective-permute-done((f32[2,4,32,256]{3,2,1,0:T(8,128)S(1)}, f32[2,4,32,256]{3,2,1,0:T(8,128)S(1)}, u32[]{:S(2)}, u32[]{:S(2)}) %collective-permute-start.3) | collective-permute-done | bytes 262176 | tf_op jit(solution)/shard_map/ppermute | solution.py:286
  36.1 0.7 %copy-done.10 = f32[2,4,32,256]{3,2,1,0:T(8,128)} copy-done((f32[2,4,32,256]{3,2,1,0:T(8,128)}, f32[2,4,32,256]{3,2,1,0:T(8,128)S(1)}, u32[]{:S(2)}) %copy-start.10) | copy-done | bytes 262168
  36.8 3.4 %sweep_outer.1 = (f32[2,4,32,256]{3,2,1,0:T(8,128)}, f32[10,32,256]{2,1,0:T(8,128)}, f32[4,16,256]{2,1,0:T(8,128)}) custom-call(f32[2,4,32,256]{3,2,1,0:T(8,128)} %copy-done.10, f32[2,8,32,256]{3,2,1,0:T(8,128)} %get-tuple-element.9.edge, s32[4,32,256]{2,1,0:T(8,128)} %get-tuple-element.10.edge_kind, f32[4,8,128]{2,1,0:T(8,128)} %broadcast_in_dim.2.refs_10_.table, ...), custom_call_target="tpu_custom_call" | custom-call | flops 9830400 | bytes 524288 | tf_op jit(solution)/shard_map/sweep_outer/pallas_call | solution.py:226
  40.2 1.8 %collective-permute-done.9 = f32[10,32,256]{2,1,0:T(8,128)S(1)} collective-permute-done((f32[10,32,256]{2,1,0:T(8,128)}, f32[10,32,256]{2,1,0:T(8,128)S(1)}, u32[]{:S(2)}, u32[]{:S(2)}) %collective-permute-start.9) | collective-permute-done | bytes 327712 | tf_op jit(solution)/shard_map/ppermute | solution.py:263
  42.2 2.4 %collective-permute-start.13 = (f32[4,16,256]{2,1,0:T(8,128)S(1)}, f32[4,16,256]{2,1,0:T(8,128)S(1)}, u32[]{:S(2)}, u32[]{:S(2)}) collective-permute-start(f32[4,16,256]{2,1,0:T(8,128)S(1)} %pad_maximum_fusion.2), channel_id=1, source_target_pairs={{0,24},{8,16},{16,8},{24,0},{1,25},{9,17},{17,9},{25,1},{2,26},{10... | collective-permute-start | bytes 196616 | tf_op jit(solution)/shard_map/ppermute | solution.py:297
  44.5 2.1 %collective-permute-start.15 = (f32[4,16,256]{2,1,0:T(8,128)S(1)}, f32[4,16,256]{2,1,0:T(8,128)S(1)}, u32[]{:S(2)}, u32[]{:S(2)}) collective-permute-start(f32[4,16,256]{2,1,0:T(8,128)S(1)} %pad_maximum_fusion.2), channel_id=1, source_target_pairs={{0,8},{8,0},{16,24},{24,16},{1,9},{9,1},{17,25},{25,17},{2,10},{10... | collective-permute-start | bytes 196616 | tf_op jit(solution)/shard_map/ppermute | solution.py:297
  46.7 1.6 %collective-permute-start.10 = (f32[4,32,256]{2,1,0:T(8,128)S(1)}, f32[4,32,256]{2,1,0:T(8,128)S(1)}, u32[]{:S(2)}, u32[]{:S(2)}) collective-permute-start(f32[4,32,256]{2,1,0:T(8,128)S(1)} %get-tuple-element.28), channel_id=1, source_target_pairs={{0,6},{1,7},{2,4},{3,5},{4,2},{5,3},{6,0},{7,1},{8,14},{9,15},{10,... | collective-permute-start | bytes 393224 | tf_op jit(solution)/shard_map/ppermute | solution.py:260
  48.3 1.5 %collective-permute-start.11 = (f32[4,32,256]{2,1,0:T(8,128)S(1)}, f32[4,32,256]{2,1,0:T(8,128)S(1)}, u32[]{:S(2)}, u32[]{:S(2)}) collective-permute-start(f32[4,32,256]{2,1,0:T(8,128)S(1)} %get-tuple-element.29), channel_id=1, source_target_pairs={{0,4},{1,5},{2,6},{3,7},{4,0},{5,1},{6,2},{7,3},{8,12},{9,13},{10,... | collective-permute-start | bytes 393224 | tf_op jit(solution)/shard_map/ppermute | solution.py:260
  49.7 0.0 collective-permute-done.13
  49.7 0.8 %collective-permute-start.12 = (f32[4,32,256]{2,1,0:T(8,128)S(1)}, f32[4,32,256]{2,1,0:T(8,128)S(1)}, u32[]{:S(2)}, u32[]{:S(2)}) collective-permute-start(f32[4,32,256]{2,1,0:T(8,128)S(1)} %get-tuple-element.27), channel_id=1, source_target_pairs={{0,2},{1,3},{2,0},{3,1},{4,6},{5,7},{6,4},{7,5},{8,10},{9,11},{10,... | collective-permute-start | bytes 393224 | tf_op jit(solution)/shard_map/ppermute | solution.py:260
  50.5 0.5 collective-permute-done.14
  51.1 0.7 %copy.6 = f32[1,4,16,256]{3,1,2,0:T(4,128)} copy(f32[1,4,16,256]{3,2,1,0:T(8,128)S(1)} %maximum_bitcast_fusion) | data formatting | bytes 131072
  51.8 2.1 %collective-permute-done.10 = f32[4,32,256]{2,1,0:T(8,128)S(1)} collective-permute-done((f32[4,32,256]{2,1,0:T(8,128)S(1)}, f32[4,32,256]{2,1,0:T(8,128)S(1)}, u32[]{:S(2)}, u32[]{:S(2)}) %collective-permute-start.10) | collective-permute-done | bytes 131104 | tf_op jit(solution)/shard_map/ppermute | solution.py:260
  53.9 1.3 %collective-permute-done.11 = f32[4,32,256]{2,1,0:T(8,128)S(1)} collective-permute-done((f32[4,32,256]{2,1,0:T(8,128)S(1)}, f32[4,32,256]{2,1,0:T(8,128)S(1)}, u32[]{:S(2)}, u32[]{:S(2)}) %collective-permute-start.11) | collective-permute-done | bytes 131104 | tf_op jit(solution)/shard_map/ppermute | solution.py:260
  55.1 0.1 collective-permute-done.12
  55.3 0.1 select_select_fusion.4
  55.3 0.1 select_select_fusion.3
  55.4 0.8 %pad_maximum_fusion.1 = f32[4,128,256]{2,1,0:T(8,128)} fusion(f32[4,32,256]{2,1,0:T(8,128)S(1)} %get-tuple-element.31, f32[4,32,256]{2,1,0:T(8,128)S(1)} %get-tuple-element.32, f32[4,32,256]{2,1,0:T(8,128)S(1)} %get-tuple-element.30, f32[4,32,256]{2,1,0:T(8,128)S(1)} %get-tuple-element.16), kind=kLoop, calls=%fused_computation.1 | loop fusion | flops 393216 | bytes 1048576 | tf_op jit(solution)/shard_map/concatenate | solution.py:309
  (42 shorter events, 0.3 us)
Async XLA Ops:
  1.7 9.2 %collective-permute-start.6 = (s32[4,32,256]{2,1,0:T(8,128)S(1)}, s32[4,32,256]{2,1,0:T(8,128)S(1)}, u32[]{:S(2)}, u32[]{:S(2)}) collective-permute-start(s32[4,32,256]{2,1,0:T(8,128)S(1)} %get-tuple-element.34), channel_id=1, source_target_pairs={{0,6},{1,7},{2,4},{3,5},{4,2},{5,3},{6,0},{7,1},{8,14},{9,15},{10,... | collective-permute-start | bytes 393224 | tf_op jit(solution)/shard_map/ppermute | solution.py:260
  5.7 10.6 %collective-permute-start.5 = (s32[4,32,256]{2,1,0:T(8,128)S(1)}, s32[4,32,256]{2,1,0:T(8,128)S(1)}, u32[]{:S(2)}, u32[]{:S(2)}) collective-permute-start(s32[4,32,256]{2,1,0:T(8,128)S(1)} %get-tuple-element.35), channel_id=1, source_target_pairs={{0,4},{1,5},{2,6},{3,7},{4,0},{5,1},{6,2},{7,3},{8,12},{9,13},{10,... | collective-permute-start | bytes 393224 | tf_op jit(solution)/shard_map/ppermute | solution.py:260
  6.2 10.1 %collective-permute-start.4 = (s32[4,32,256]{2,1,0:T(8,128)S(1)}, s32[4,32,256]{2,1,0:T(8,128)S(1)}, u32[]{:S(2)}, u32[]{:S(2)}) collective-permute-start(s32[4,32,256]{2,1,0:T(8,128)S(1)} %get-tuple-element.33), channel_id=1, source_target_pairs={{0,2},{1,3},{2,0},{3,1},{4,6},{5,7},{6,4},{7,5},{8,10},{9,11},{10,... | collective-permute-start | bytes 393224 | tf_op jit(solution)/shard_map/ppermute | solution.py:260
  7.5 11.6 %collective-permute-start = (f32[2,4,32,256]{3,2,1,0:T(8,128)S(1)}, f32[2,4,32,256]{3,2,1,0:T(8,128)S(1)}, u32[]{:S(2)}, u32[]{:S(2)}) collective-permute-start(f32[2,4,32,256]{3,2,1,0:T(8,128)S(1)} %get-tuple-element.26), channel_id=1, source_target_pairs={{0,6},{1,7},{2,4},{3,5},{4,2},{5,3},{6,0},{7,1},{8,14},{9,15},{10,... | collective-permute-start | bytes 786440 | tf_op jit(solution)/shard_map/ppermute | solution.py:260
  10.5 12.8 %collective-permute-start.1 = (f32[2,4,32,256]{3,2,1,0:T(8,128)S(1)}, f32[2,4,32,256]{3,2,1,0:T(8,128)S(1)}, u32[]{:S(2)}, u32[]{:S(2)}) collective-permute-start(f32[2,4,32,256]{3,2,1,0:T(8,128)S(1)} %get-tuple-element.25), channel_id=1, source_target_pairs={{0,4},{1,5},{2,6},{3,7},{4,0},{5,1},{6,2},{7,3},{8,12},{9,13},{10,... | collective-permute-start | bytes 786440 | tf_op jit(solution)/shard_map/ppermute | solution.py:260
  11.0 14.6 %copy-start.4 = (s32[4,32,256]{2,1,0:T(8,128)}, s32[4,32,256]{2,1,0:T(8,128)S(1)}, u32[]{:S(2)}) copy-start(s32[4,32,256]{2,1,0:T(8,128)S(1)} %collective-permute-done.6.refs_7_) | copy-start | bytes 393220
  11.0 12.6 %collective-permute-start.2 = (f32[2,4,32,256]{3,2,1,0:T(8,128)S(1)}, f32[2,4,32,256]{3,2,1,0:T(8,128)S(1)}, u32[]{:S(2)}, u32[]{:S(2)}) collective-permute-start(f32[2,4,32,256]{3,2,1,0:T(8,128)S(1)} %get-tuple-element.24), channel_id=1, source_target_pairs={{0,2},{1,3},{2,0},{3,1},{4,6},{5,7},{6,4},{7,5},{8,10},{9,11},{10,... | collective-permute-start | bytes 786440 | tf_op jit(solution)/shard_map/ppermute | solution.py:260
  16.4 9.2 %copy-start.5 = (s32[4,32,256]{2,1,0:T(8,128)}, s32[4,32,256]{2,1,0:T(8,128)S(1)}, u32[]{:S(2)}) copy-start(s32[4,32,256]{2,1,0:T(8,128)S(1)} %collective-permute-done.5.refs_6_) | copy-start | bytes 393220
  16.4 9.2 %copy-start.6 = (s32[4,32,256]{2,1,0:T(8,128)}, s32[4,32,256]{2,1,0:T(8,128)S(1)}, u32[]{:S(2)}) copy-start(s32[4,32,256]{2,1,0:T(8,128)S(1)} %collective-permute-done.4.refs_5_) | copy-start | bytes 393220
  17.4 8.2 %copy-start.7 = (s32[4,32,256]{2,1,0:T(8,128)}, s32[4,32,256]{2,1,0:T(8,128)S(1)}, u32[]{:S(2)}) copy-start(s32[4,32,256]{2,1,0:T(8,128)S(1)} %get-tuple-element.19.refs_4_) | copy-start | bytes 393220
  19.2 5.5 %copy-start = (f32[2,4,32,256]{3,2,1,0:T(8,128)}, f32[2,4,32,256]{3,2,1,0:T(8,128)S(1)}, u32[]{:S(2)}) copy-start(f32[2,4,32,256]{3,2,1,0:T(8,128)S(1)} %collective-permute-done.refs_3_) | copy-start | bytes 786436
  23.3 1.4 %copy-start.1 = (f32[2,4,32,256]{3,2,1,0:T(8,128)}, f32[2,4,32,256]{3,2,1,0:T(8,128)S(1)}, u32[]{:S(2)}) copy-start(f32[2,4,32,256]{3,2,1,0:T(8,128)S(1)} %collective-permute-done.1.refs_2_) | copy-start | bytes 786436
  23.6 1.2 %copy-start.2 = (f32[2,4,32,256]{3,2,1,0:T(8,128)}, f32[2,4,32,256]{3,2,1,0:T(8,128)S(1)}, u32[]{:S(2)}) copy-start(f32[2,4,32,256]{3,2,1,0:T(8,128)S(1)} %collective-permute-done.2.refs_1_) | copy-start | bytes 786436
  24.7 0.7 %copy-start.3 = (f32[2,4,32,256]{3,2,1,0:T(8,128)}, f32[2,4,32,256]{3,2,1,0:T(8,128)S(1)}, u32[]{:S(2)}) copy-start(f32[2,4,32,256]{3,2,1,0:T(8,128)S(1)} %get-tuple-element.21.refs_0_) | copy-start | bytes 786436
  25.4 4.1 %collective-permute-start.7 = (f32[2,2,4,32,256]{4,3,2,1,0:T(8,128)S(1)}, f32[2,2,4,32,256]{4,3,2,1,0:T(8,128)S(1)}, u32[]{:S(2)}, u32[]{:S(2)}) collective-permute-start(f32[2,2,4,32,256]{4,3,2,1,0:T(8,128)S(1)} %pad_maximum_fusion), channel_id=1, source_target_pairs={{0,1},{1,0},{2,3},{3,2},{4,5},{5,4},{6,7},{7,6},{8,9},{9,8},{10,11... | collective-permute-start | bytes 1572872 | tf_op jit(solution)/shard_map/ppermute | solution.py:263
  25.6 3.9 %copy-start.14 = (f32[8]{0:T(128)S(1)}, f32[8]{0:T(128)}, u32[]{:S(2)}) copy-start(f32[8]{0:T(128)} %param.7) | copy-start | bytes 100
  25.7 3.8 %copy-start.13 = (f32[3,8]{1,0:T(4,128)S(1)}, f32[3,8]{1,0:T(4,128)}, u32[]{:S(2)}) copy-start(f32[3,8]{1,0:T(4,128)} %param.6) | copy-start | bytes 292
  25.7 3.8 %collective-permute-start.8 = (s32[2,4,32,256]{3,2,1,0:T(8,128)S(1)}, s32[2,4,32,256]{3,2,1,0:T(8,128)S(1)}, u32[]{:S(2)}, u32[]{:S(2)}) collective-permute-start(s32[2,4,32,256]{3,2,1,0:T(8,128)S(1)} %pad_add_fusion), channel_id=1, source_target_pairs={{0,1},{1,0},{2,3},{3,2},{4,5},{5,4},{6,7},{7,6},{8,9},{9,8},{10,11... | collective-permute-start | bytes 786440 | tf_op jit(solution)/shard_map/ppermute | solution.py:263
  26.2 9.9 %collective-permute-start.3 = (f32[2,4,32,256]{3,2,1,0:T(8,128)S(1)}, f32[2,4,32,256]{3,2,1,0:T(8,128)S(1)}, u32[]{:S(2)}, u32[]{:S(2)}) collective-permute-start(f32[2,4,32,256]{3,2,1,0:T(8,128)S(1)} %get-tuple-element.23), channel_id=1, source_target_pairs={{0,25},{1,8},{2,27},{3,10},{4,29},{5,12},{6,31},{7,14},{8,1},{9,16... | collective-permute-start | bytes 786440 | tf_op jit(solution)/shard_map/ppermute | solution.py:286
  29.5 0.7 %copy-start.11 = (s32[2,4,32,256]{3,2,1,0:T(8,128)}, s32[2,4,32,256]{3,2,1,0:T(8,128)S(1)}, u32[]{:S(2)}) copy-start(s32[2,4,32,256]{3,2,1,0:T(8,128)S(1)} %collective-permute-done.8.refs_9_) | copy-start | bytes 786436
  29.5 0.9 %copy-start.9 = (f32[2,2,4,32,256]{4,3,2,1,0:T(8,128)}, f32[2,2,4,32,256]{4,3,2,1,0:T(8,128)S(1)}, u32[]{:S(2)}) copy-start(f32[2,2,4,32,256]{4,3,2,1,0:T(8,128)S(1)} %collective-permute-done.7.refs_8_) | copy-start | bytes 1572868
  36.1 0.7 %copy-start.10 = (f32[2,4,32,256]{3,2,1,0:T(8,128)}, f32[2,4,32,256]{3,2,1,0:T(8,128)S(1)}, u32[]{:S(2)}) copy-start(f32[2,4,32,256]{3,2,1,0:T(8,128)S(1)} %collective-permute-done.3.far) | copy-start | bytes 786436
  40.2 1.8 %collective-permute-start.9 = (f32[10,32,256]{2,1,0:T(8,128)}, f32[10,32,256]{2,1,0:T(8,128)S(1)}, u32[]{:S(2)}, u32[]{:S(2)}) collective-permute-start(f32[10,32,256]{2,1,0:T(8,128)} %get-tuple-element.14), channel_id=1, source_target_pairs={{0,1},{1,0},{2,3},{3,2},{4,5},{5,4},{6,7},{7,6},{8,9},{9,8},{10,11... | collective-permute-start | bytes 983048 | tf_op jit(solution)/shard_map/ppermute | solution.py:263
  40.2 1.8 %copy-start.12 = (f32[4,16,256]{2,1,0:T(8,128)S(1)}, f32[4,16,256]{2,1,0:T(8,128)}, u32[]{:S(2)}) copy-start(f32[4,16,256]{2,1,0:T(8,128)} %get-tuple-element.15) | copy-start | bytes 196612
  42.1 4.5 %copy-start.8 = (f32[2,4,32,256]{3,2,1,0:T(8,128)S(1)}, f32[2,4,32,256]{3,2,1,0:T(8,128)}, u32[]{:S(2)}) copy-start(f32[2,4,32,256]{3,2,1,0:T(8,128)} %get-tuple-element.13) | copy-start | bytes 786436
  42.2 7.6 %collective-permute-start.13 = (f32[4,16,256]{2,1,0:T(8,128)S(1)}, f32[4,16,256]{2,1,0:T(8,128)S(1)}, u32[]{:S(2)}, u32[]{:S(2)}) collective-permute-start(f32[4,16,256]{2,1,0:T(8,128)S(1)} %pad_maximum_fusion.2), channel_id=1, source_target_pairs={{0,24},{8,16},{16,8},{24,0},{1,25},{9,17},{17,9},{25,1},{2,26},{10... | collective-permute-start | bytes 196616 | tf_op jit(solution)/shard_map/ppermute | solution.py:297
  44.5 6.4 %collective-permute-start.14 = (f32[4,16,256]{2,1,0:T(8,128)S(1)}, f32[4,16,256]{2,1,0:T(8,128)S(1)}, u32[]{:S(2)}, u32[]{:S(2)}) collective-permute-start(f32[4,16,256]{2,1,0:T(8,128)S(1)} %pad_maximum_fusion.2), channel_id=1, source_target_pairs={{0,16},{8,24},{16,0},{24,8},{1,17},{9,25},{17,1},{25,9},{2,18},{10... | collective-permute-start | bytes 196616 | tf_op jit(solution)/shard_map/ppermute | solution.py:297
  44.5 6.4 %collective-permute-start.15 = (f32[4,16,256]{2,1,0:T(8,128)S(1)}, f32[4,16,256]{2,1,0:T(8,128)S(1)}, u32[]{:S(2)}, u32[]{:S(2)}) collective-permute-start(f32[4,16,256]{2,1,0:T(8,128)S(1)} %pad_maximum_fusion.2), channel_id=1, source_target_pairs={{0,8},{8,0},{16,24},{24,16},{1,9},{9,1},{17,25},{25,17},{2,10},{10... | collective-permute-start | bytes 196616 | tf_op jit(solution)/shard_map/ppermute | solution.py:297
  46.7 7.2 %collective-permute-start.10 = (f32[4,32,256]{2,1,0:T(8,128)S(1)}, f32[4,32,256]{2,1,0:T(8,128)S(1)}, u32[]{:S(2)}, u32[]{:S(2)}) collective-permute-start(f32[4,32,256]{2,1,0:T(8,128)S(1)} %get-tuple-element.28), channel_id=1, source_target_pairs={{0,6},{1,7},{2,4},{3,5},{4,2},{5,3},{6,0},{7,1},{8,14},{9,15},{10,... | collective-permute-start | bytes 393224 | tf_op jit(solution)/shard_map/ppermute | solution.py:260
  48.3 6.9 %collective-permute-start.11 = (f32[4,32,256]{2,1,0:T(8,128)S(1)}, f32[4,32,256]{2,1,0:T(8,128)S(1)}, u32[]{:S(2)}, u32[]{:S(2)}) collective-permute-start(f32[4,32,256]{2,1,0:T(8,128)S(1)} %get-tuple-element.29), channel_id=1, source_target_pairs={{0,4},{1,5},{2,6},{3,7},{4,0},{5,1},{6,2},{7,3},{8,12},{9,13},{10,... | collective-permute-start | bytes 393224 | tf_op jit(solution)/shard_map/ppermute | solution.py:260
  49.7 5.5 %collective-permute-start.12 = (f32[4,32,256]{2,1,0:T(8,128)S(1)}, f32[4,32,256]{2,1,0:T(8,128)S(1)}, u32[]{:S(2)}, u32[]{:S(2)}) collective-permute-start(f32[4,32,256]{2,1,0:T(8,128)S(1)} %get-tuple-element.27), channel_id=1, source_target_pairs={{0,2},{1,3},{2,0},{3,1},{4,6},{5,7},{6,4},{7,5},{8,10},{9,11},{10,... | collective-permute-start | bytes 393224 | tf_op jit(solution)/shard_map/ppermute | solution.py:260

commit v3 on v2

--- a/solution.py
+++ b/solution.py
@@ -11,6 +11,7 @@
 DEPTH_SCALE = 2.5
 LANES = 128
 F32 = jnp.float32
+GRANT = 12 << 20
 VMEM = pl.BlockSpec(memory_space=pltpu.VMEM)
 
 
@@ -192,6 +193,40 @@
         give[half * layers + n // 2, (n % 2) * short : (n % 2 + 1) * short] = given
 
 
+def route_kernel(chips, with_far, *refs):
+    own, given = refs[:chips], refs[chips]
+    member = lax.axis_index("swap")
+    chip, upper = member // 2, member % 2
+    half = chips // 2
+    for d in range(chips):
+        k = chip ^ d
+
+        @pl.when(k // half != upper)
+        def _():
+            given[k - (1 - upper) * half] = own[d][...]
+
+        if with_far:
+
+            @pl.when(k == upper * (chips - 1))
+            def _():
+                refs[chips + 1][...] = own[d][...]
+
+
+def route(blocks, with_far):
+    chips = len(blocks)
+    shape, dtype = blocks[0].shape, blocks[0].dtype
+    shapes = [jax.ShapeDtypeStruct((chips // 2, *shape), dtype)] + [jax.ShapeDtypeStruct(shape, dtype)] * with_far
+    return pl.pallas_call(
+        functools.partial(route_kernel, chips, with_far),
+        out_shape=shapes,
+        in_specs=[VMEM] * chips,
+        out_specs=[VMEM] * len(shapes),
+        compiler_params=pltpu.CompilerParams(vmem_limit_bytes=GRANT),
+        cost_estimate=pl.CostEstimate(flops=1000, bytes_accessed=1 << 20, transcendentals=0),
+        name="route",
+    )(*blocks)
+
+
 def cost(cells):
     return pl.CostEstimate(flops=300 * cells, bytes_accessed=16 * cells, transcendentals=6 * cells)
 
@@ -215,6 +250,7 @@
             pltpu.VMEM((chips * layers, rows, columns), jnp.int32),
         ],
         cost_estimate=cost(chips * layers * rows * columns),
+        compiler_params=pltpu.CompilerParams(vmem_limit_bytes=GRANT),
         name="sweep_inner",
     )(*own, *own_kind, other, other_kind, table)
 
@@ -237,6 +273,7 @@
             pltpu.VMEM((4, rows, columns), F32),
         ],
         cost_estimate=cost(layers * rows * columns),
+        compiler_params=pltpu.CompilerParams(vmem_limit_bytes=GRANT),
         name="sweep_outer",
     )(far, edge, edge_kind, table, dense, image)
 
@@ -257,7 +294,9 @@
     rows = height // chips
 
     def to_chip(block, d):
-        return lax.ppermute(block, "swap", swap_pairs(members, 2 * d)) if d else block
+        if d == 0:
+            return block
+        return lax.ppermute(block, "swap", swap_pairs(members, 2 * d))
 
     def to_core(block):
         return lax.ppermute(block, "swap", swap_pairs(members, 1))
@@ -267,28 +306,32 @@
     table = jnp.pad(table, ((0, 0), (0, LANES - table.shape[1])))
     table = jnp.broadcast_to(table[:, None, :], (4, 8, LANES))
 
-    own = [
-        to_chip(lax.dynamic_slice_in_dim(fluid_state, (chip ^ d) * rows, rows, axis=2), d) for d in range(chips)
-    ]
-    own_kind = [
-        to_chip(lax.dynamic_slice_in_dim(material, (chip ^ d) * rows, rows, axis=1), d) for d in range(chips)
-    ]
-
-    def others(blocks):
-        return jnp.stack([pick(blocks, chip ^ ((1 - upper) * half + i)) for i in range(half)])
-
-    other = to_core(others(own))
+    sent = [lax.dynamic_slice_in_dim(fluid_state, (chip ^ d) * rows, rows, axis=2) for d in range(chips)]
+    own = [to_chip(sent[d], d) for d in range(chips)]
+    own_kind = [to_chip(lax.dynamic_slice_in_dim(material, (chip ^ d) * rows, rows, axis=1), d) for d in range(chips)]
+    other, outer = route(own, True)
+    *own_kind, table, _ = lax.optimization_barrier((*own_kind, table, outer))
+    other = to_core(other)
     ring = []
     for z in range(slabs):
         for w in range(members):
             to = ((z + 1) % slabs, w - 1) if w % 2 else ((z - 1) % slabs, w + 1)
             ring.append((z * members + w, to[0] * members + to[1]))
-    far = lax.ppermute(pick(own, chip ^ (upper * (chips - 1))), ("slab", "swap"), ring)
-    other_kind = to_core(others(own_kind))
+    far = lax.ppermute(outer, ("slab", "swap"), ring)
+    other_kind = to_core(route(own_kind, False)[0])
 
     dense, image, edge, edge_kind = sweep_inner(own, own_kind, other, other_kind, table)
     keep, give, tile = sweep_outer(far, edge, edge_kind, table, dense, image)
     got = to_core(give)
+
+    kept = [keep[i] for i in range(half)]
+    gotten = [got[i * layers : (i + 1) * layers] for i in range(half)]
+    chunks = []
+    for d in range(chips):
+        k = chip ^ d
+        block = jnp.where(k // half == upper, pick(kept, k % half), pick(gotten, k % half))
+        chunks.append(to_chip(block, d))
+    density = jnp.concatenate([pick(chunks, chip ^ j) for j in range(chips)], axis=1)
 
     partner = got[half * layers :].reshape(4, rows // 2, width)
     tile = over(jnp.where(upper == 1, partner, tile), jnp.where(upper == 1, tile, partner))
@@ -298,15 +341,6 @@
     ordered = [pick(pieces, slab ^ z) for z in range(slabs)]
     rendered = functools.reduce(over, ordered)
     rendered = jnp.concatenate([rendered[:3], 1.0 - rendered[3:4]], axis=0).reshape(4, height * width // members)
-
-    kept = [keep[i] for i in range(half)]
-    gotten = [got[i * layers : (i + 1) * layers] for i in range(half)]
-    chunks = []
-    for d in range(chips):
-        k = chip ^ d
-        block = jnp.where(k // half == upper, pick(kept, k % half), pick(gotten, k % half))
-        chunks.append(to_chip(block, d))
-    density = jnp.concatenate([pick(chunks, chip ^ j) for j in range(chips)], axis=1)
     return density, rendered
 
 

time: 56.5 us -> 51.2 us (0.906)
  Pallas kernels: 8.31 us -> 3.65 us
  local copies, waits for them, and re-layouts: 5.12 us -> 2.66 us
  waiting for transfers between devices: 17.1 us -> 19.5 us
  other arithmetic: 3.47 us -> 1.15 us
  starting transfers between devices: 21.3 us -> 23 us
    pallas_call x1, Pallas kernels: 4.91 us -> 2.29 us  [sweep_inner(): pl.pallas_call(functools.partial(inner_kernel, chips), out_shape=[shape(c...]
    ppermute x10, waiting for transfers between devices: 14.8 us -> 17.4 us  [the longest x9 13.5 us: to_chip(): return lax.ppermute(block, 'swap', swap_pairs(members, 2 * d))]
    another operation x6 -> x0, other arithmetic: 2.33 us -> none  [others(): jnp.stack([pick(blocks, chip ^ (1 - upper) * half + i) for i in range(hal...]
    pallas_call x1, Pallas kernels: 3.4 us -> 1.24 us  [sweep_outer(): pl.pallas_call(functools.partial(outer_kernel, 2 * half), out_shape=[shap...]
    ppermute x10, starting transfers between devices: 16.2 us -> 18.3 us  [the longest x9 14.6 us: to_chip(): return lax.ppermute(block, 'swap', swap_pairs(members, 2 * d))]
    dynamic_slice x1, local copies, waits for them, and re-layouts: 1.07 us -> 0.04 us  [per_device(): lax.dynamic_slice_in_dim(material, (chip ^ d) * rows, rows, axis=1)]
    unnamed x31 -> x7, local copies, waits for them, and re-layouts: 2.21 us -> 1.27 us
    broadcast_in_dim x1, local copies, waits for them, and re-layouts: 0.67 us -> 0.01 us  [per_device(): table = jnp.broadcast_to(table[:, None, :], (4, 8, LANES))]
  transfers between devices with their start and end apart: 16 -> 16, of which waited for: 10 -> 9; matrix products, arithmetic and copies ran while one was open for 7% -> 2% of each run, Pallas kernels for 9% -> 5%
where the time goes in v3:
time: 51.2 us; the launch traced here: 51.1 us
  starting transfers between devices  23 us (45%)
  waiting for transfers between devices  19.5 us (38%)
  Pallas kernels  3.65 us (7%)
  local copies, waits for them, and re-layouts  2.66 us (5%)
  other arithmetic  1.15 us (2%)
  between operations  1.06 us (2%)
    ppermute x9, starting transfers between devices, to_chip(): return lax.ppermute(block, 'swap', swap_pairs(members, 2 * d))  14.6 us
    ppermute x9, waiting for transfers between devices, to_chip(): return lax.ppermute(block, 'swap', swap_pairs(members, 2 * d))  13.5 us
    ppermute x3, starting transfers between devices, per_device(): pieces.append(lax.ppermute(tile, 'slab', swap_pairs(slabs, away)))  4.45 us
    ppermute x1, waiting for transfers between devices, per_device(): far = lax.ppermute(outer, ('slab', 'swap'), ring)  3.82 us
    ppermute x1, starting transfers between devices, per_device(): far = lax.ppermute(outer, ('slab', 'swap'), ring)  3.7 us
    pallas_call x1, Pallas kernels, sweep_inner(): pl.pallas_call(functools.partial(inner_kernel, chips), out_shape=[shape(c...  2.29 us
    ppermute x3, waiting for transfers between devices, to_core(): return lax.ppermute(block, 'swap', swap_pairs(members, 1))  1.41 us
    dynamic_slice x1, local copies, waits for them, and re-layouts, per_device(): lax.dynamic_slice_in_dim(fluid_state, (chip ^ d) * rows, rows, axis=2)  1.34 us
  transfers between devices with their start and end apart: 16, of which 9 were waited for; matrix products, arithmetic and copies ran while one was open for 2% of the time, Pallas kernels for 5%

profile of v3, /device:TPU:0, one launch (start us, length us, event | category | flops | bytes accessed | tf_op | source)
XLA Modules:
  0.0 51.1 jit_solution(8008488709732684306)
XLA Ops:
  0.7 0.0 copy-start
  0.7 1.3 %constant_dynamic-slice_fusion.4 = (f32[2,4,32,256]{3,2,1,0:T(8,128)S(1)}, f32[2,4,32,256]{3,2,1,0:T(8,128)S(1)}, f32[2,4,32,256]{3,2,1,0:T(8,128)S(1)}, f32[2,4,32,256]{3,2,1,0:T(8,128)S(1)}) fusion(f32[2,4,128,256]{3,2,1,0:T(8,128)} %param.4, s32[]{:T(128)S(6)} %select_n.315, s32[]{:T(128)S(6)} %select_n.313, s32[]{:T(128)S(6)} %select_n.312, s32[]{:T(128)S(6)} %select_n.314), kind=kLoop, calls=%fused_computation.39 | loop fusion | bytes 2097168 | tf_op jit(solution)/shard_map/dynamic_slice | solution.py:309
  2.0 3.0 %collective-permute-start = (f32[2,4,32,256]{3,2,1,0:T(8,128)S(1)}, f32[2,4,32,256]{3,2,1,0:T(8,128)S(1)}, u32[]{:S(2)}, u32[]{:S(2)}) collective-permute-start(f32[2,4,32,256]{3,2,1,0:T(8,128)S(1)} %get-tuple-element.33), channel_id=1, source_target_pairs={{0,2},{1,3},{2,0},{3,1},{4,6},{5,7},{6,4},{7,5},{8,10},{9,11},{10,... | collective-permute-start | bytes 786440 | tf_op jit(solution)/shard_map/ppermute | solution.py:299
  5.1 1.5 %collective-permute-start.1 = (f32[2,4,32,256]{3,2,1,0:T(8,128)S(1)}, f32[2,4,32,256]{3,2,1,0:T(8,128)S(1)}, u32[]{:S(2)}, u32[]{:S(2)}) collective-permute-start(f32[2,4,32,256]{3,2,1,0:T(8,128)S(1)} %get-tuple-element.35), channel_id=1, source_target_pairs={{0,4},{1,5},{2,6},{3,7},{4,0},{5,1},{6,2},{7,3},{8,12},{9,13},{10,... | collective-permute-start | bytes 786440 | tf_op jit(solution)/shard_map/ppermute | solution.py:299
  6.6 0.0 collective-permute-start.2
  6.6 0.0 copy-done
  6.7 2.0 %collective-permute-start.4 = (s32[4,32,256]{2,1,0:T(8,128)S(1)}, s32[4,32,256]{2,1,0:T(8,128)S(1)}, u32[]{:S(2)}, u32[]{:S(2)}) collective-permute-start(s32[4,32,256]{2,1,0:T(8,128)S(1)} %get-tuple-element.43), channel_id=1, source_target_pairs={{0,2},{1,3},{2,0},{3,1},{4,6},{5,7},{6,4},{7,5},{8,10},{9,11},{10,... | collective-permute-start | bytes 393224 | tf_op jit(solution)/shard_map/ppermute | solution.py:299
  8.7 1.5 %collective-permute-start.5 = (s32[4,32,256]{2,1,0:T(8,128)S(1)}, s32[4,32,256]{2,1,0:T(8,128)S(1)}, u32[]{:S(2)}, u32[]{:S(2)}) collective-permute-start(s32[4,32,256]{2,1,0:T(8,128)S(1)} %get-tuple-element.45), channel_id=1, source_target_pairs={{0,4},{1,5},{2,6},{3,7},{4,0},{5,1},{6,2},{7,3},{8,12},{9,13},{10,... | collective-permute-start | bytes 393224 | tf_op jit(solution)/shard_map/ppermute | solution.py:299
  10.2 2.0 %collective-permute-done.refs_1_ = f32[2,4,32,256]{3,2,1,0:T(8,128)S(1)} collective-permute-done((f32[2,4,32,256]{3,2,1,0:T(8,128)S(1)}, f32[2,4,32,256]{3,2,1,0:T(8,128)S(1)}, u32[]{:S(2)}, u32[]{:S(2)}) %collective-permute-start) | collective-permute-done | bytes 262176 | tf_op jit(solution)/shard_map/ppermute | solution.py:299
  12.2 3.0 %collective-permute-start.6 = (s32[4,32,256]{2,1,0:T(8,128)S(1)}, s32[4,32,256]{2,1,0:T(8,128)S(1)}, u32[]{:S(2)}, u32[]{:S(2)}) collective-permute-start(s32[4,32,256]{2,1,0:T(8,128)S(1)} %get-tuple-element.42), channel_id=1, source_target_pairs={{0,6},{1,7},{2,4},{3,5},{4,2},{5,3},{6,0},{7,1},{8,14},{9,15},{10,... | collective-permute-start | bytes 393224 | tf_op jit(solution)/shard_map/ppermute | solution.py:299
  15.2 4.7 %collective-permute-done.1.refs_2_ = f32[2,4,32,256]{3,2,1,0:T(8,128)S(1)} collective-permute-done((f32[2,4,32,256]{3,2,1,0:T(8,128)S(1)}, f32[2,4,32,256]{3,2,1,0:T(8,128)S(1)}, u32[]{:S(2)}, u32[]{:S(2)}) %collective-permute-start.1) | collective-permute-done | bytes 262176 | tf_op jit(solution)/shard_map/ppermute | solution.py:299
  19.9 0.0 collective-permute-done.2.refs_3_
  19.9 0.0 copy-start.2
  19.9 0.1 route.2
  20.0 0.0 copy-start.1
  20.0 0.1 collective-permute-start.7
  20.1 0.5 copy-done.2
  20.5 0.1 copy-done.1
  20.7 0.0 collective-permute-done.4.refs_1_.refs_5_
  20.7 3.4 %collective-permute-done.5.refs_2_.refs_6_ = s32[4,32,256]{2,1,0:T(8,128)S(1)} collective-permute-done((s32[4,32,256]{2,1,0:T(8,128)S(1)}, s32[4,32,256]{2,1,0:T(8,128)S(1)}, u32[]{:S(2)}, u32[]{:S(2)}) %collective-permute-start.5) | collective-permute-done | bytes 131104 | tf_op jit(solution)/shard_map/ppermute | solution.py:299
  24.1 0.0 collective-permute-done.6.refs_3_.refs_7_
  24.1 0.1 collective-permute-start.8
  24.2 3.7 %collective-permute-start.3 = (f32[2,4,32,256]{3,2,1,0:T(8,128)S(1)}, f32[2,4,32,256]{3,2,1,0:T(8,128)S(1)}, u32[]{:S(2)}, u32[]{:S(2)}) collective-permute-start(f32[2,4,32,256]{3,2,1,0:T(8,128)S(1)} %get-tuple-element.16), channel_id=1, source_target_pairs={{0,25},{1,8},{2,27},{3,10},{4,29},{5,12},{6,31},{7,14},{8,1},{9,16... | collective-permute-start | bytes 786440 | tf_op jit(solution)/shard_map/ppermute | solution.py:320
  27.9 0.0 collective-permute-done.8.refs_9_
  27.9 0.0 collective-permute-done.7.refs_8_
  27.9 2.3 %sweep_inner.1 = (f32[16,32,256]{2,1,0:T(8,128)S(1)}, f32[4,32,256]{2,1,0:T(8,128)S(1)}, f32[2,8,32,256]{3,2,1,0:T(8,128)S(1)}, s32[4,32,256]{2,1,0:T(8,128)S(1)}) custom-call(f32[2,4,32,256]{3,2,1,0:T(8,128)S(1)} %get-tuple-element.34.refs_0_, f32[2,4,32,256]{3,2,1,0:T(8,128)S(1)} %collective-permute-done.refs_1_, ...), custom_call_target="tpu_custom_call" | custom-call | flops 39321600 | bytes 2097152 | tf_op jit(solution)/shard_map/sweep_inner/pallas_call | solution.py:238
  30.2 3.8 %collective-permute-done.3.far = f32[2,4,32,256]{3,2,1,0:T(8,128)S(1)} collective-permute-done((f32[2,4,32,256]{3,2,1,0:T(8,128)S(1)}, f32[2,4,32,256]{3,2,1,0:T(8,128)S(1)}, u32[]{:S(2)}, u32[]{:S(2)}) %collective-permute-start.3) | collective-permute-done | bytes 262176 | tf_op jit(solution)/shard_map/ppermute | solution.py:320
  34.0 1.2 %sweep_outer.1 = (f32[2,4,32,256]{3,2,1,0:T(8,128)S(1)}, f32[10,32,256]{2,1,0:T(8,128)S(1)}, f32[4,16,256]{2,1,0:T(8,128)S(1)}) custom-call(f32[2,4,32,256]{3,2,1,0:T(8,128)S(1)} %collective-permute-done.3.far, f32[2,8,32,256]{3,2,1,0:T(8,128)S(1)} %get-tuple-element.23.edge, s32[4,32,256]{2,1,0:T(8,128)S(1)} %get-tuple-element.24.edge_kind, ...), custom_call_target="tpu_custom_call" | custom-call | flops 9830400 | bytes 524288 | tf_op jit(solution)/shard_map/sweep_outer/pallas_call | solution.py:262
  35.3 0.1 collective-permute-start.9
  35.5 1.4 %collective-permute-done.9 = f32[10,32,256]{2,1,0:T(8,128)S(1)} collective-permute-done((f32[10,32,256]{2,1,0:T(8,128)S(1)}, f32[10,32,256]{2,1,0:T(8,128)S(1)}, u32[]{:S(2)}, u32[]{:S(2)}) %collective-permute-start.9) | collective-permute-done | bytes 327712 | tf_op jit(solution)/shard_map/ppermute | solution.py:302
  37.0 2.5 %collective-permute-start.13 = (f32[4,16,256]{2,1,0:T(8,128)S(1)}, f32[4,16,256]{2,1,0:T(8,128)S(1)}, u32[]{:S(2)}, u32[]{:S(2)}) collective-permute-start(f32[4,16,256]{2,1,0:T(8,128)S(1)} %pad_maximum_fusion.1), channel_id=1, source_target_pairs={{0,24},{8,16},{16,8},{24,0},{1,25},{9,17},{17,9},{25,1},{2,26},{10... | collective-permute-start | bytes 196616 | tf_op jit(solution)/shard_map/ppermute | solution.py:340
  39.5 0.0 collective-permute-start.14
  39.5 1.9 %collective-permute-start.15 = (f32[4,16,256]{2,1,0:T(8,128)S(1)}, f32[4,16,256]{2,1,0:T(8,128)S(1)}, u32[]{:S(2)}, u32[]{:S(2)}) collective-permute-start(f32[4,16,256]{2,1,0:T(8,128)S(1)} %pad_maximum_fusion.1), channel_id=1, source_target_pairs={{0,8},{8,0},{16,24},{24,16},{1,9},{9,1},{17,25},{25,17},{2,10},{10... | collective-permute-start | bytes 196616 | tf_op jit(solution)/shard_map/ppermute | solution.py:340
  41.5 1.6 %collective-permute-start.10 = (f32[4,32,256]{2,1,0:T(8,128)S(1)}, f32[4,32,256]{2,1,0:T(8,128)S(1)}, u32[]{:S(2)}, u32[]{:S(2)}) collective-permute-start(f32[4,32,256]{2,1,0:T(8,128)S(1)} %get-tuple-element.37), channel_id=1, source_target_pairs={{0,6},{1,7},{2,4},{3,5},{4,2},{5,3},{6,0},{7,1},{8,14},{9,15},{10,... | collective-permute-start | bytes 393224 | tf_op jit(solution)/shard_map/ppermute | solution.py:299
  43.1 1.2 %collective-permute-start.11 = (f32[4,32,256]{2,1,0:T(8,128)S(1)}, f32[4,32,256]{2,1,0:T(8,128)S(1)}, u32[]{:S(2)}, u32[]{:S(2)}) collective-permute-start(f32[4,32,256]{2,1,0:T(8,128)S(1)} %get-tuple-element.38), channel_id=1, source_target_pairs={{0,4},{1,5},{2,6},{3,7},{4,0},{5,1},{6,2},{7,3},{8,12},{9,13},{10,... | collective-permute-start | bytes 393224 | tf_op jit(solution)/shard_map/ppermute | solution.py:299
  44.3 0.0 collective-permute-done.13
  44.3 0.8 %collective-permute-start.12 = (f32[4,32,256]{2,1,0:T(8,128)S(1)}, f32[4,32,256]{2,1,0:T(8,128)S(1)}, u32[]{:S(2)}, u32[]{:S(2)}) collective-permute-start(f32[4,32,256]{2,1,0:T(8,128)S(1)} %get-tuple-element.36), channel_id=1, source_target_pairs={{0,2},{1,3},{2,0},{3,1},{4,6},{5,7},{6,4},{7,5},{8,10},{9,11},{10,... | collective-permute-start | bytes 393224 | tf_op jit(solution)/shard_map/ppermute | solution.py:299
  45.1 0.7 %collective-permute-done.14 = f32[4,16,256]{2,1,0:T(8,128)S(1)} collective-permute-done((f32[4,16,256]{2,1,0:T(8,128)S(1)}, f32[4,16,256]{2,1,0:T(8,128)S(1)}, u32[]{:S(2)}, u32[]{:S(2)}) %collective-permute-start.14) | collective-permute-done | bytes 65568 | tf_op jit(solution)/shard_map/ppermute | solution.py:340
  45.8 0.0 collective-permute-done.15
  46.0 0.7 %copy.6 = f32[1,4,16,256]{3,1,2,0:T(4,128)} copy(f32[1,4,16,256]{3,2,1,0:T(8,128)S(1)} %maximum_bitcast_fusion) | data formatting | bytes 131072
  46.6 2.1 %collective-permute-done.10 = f32[4,32,256]{2,1,0:T(8,128)S(1)} collective-permute-done((f32[4,32,256]{2,1,0:T(8,128)S(1)}, f32[4,32,256]{2,1,0:T(8,128)S(1)}, u32[]{:S(2)}, u32[]{:S(2)}) %collective-permute-start.10) | collective-permute-done | bytes 131104 | tf_op jit(solution)/shard_map/ppermute | solution.py:299
  48.7 1.3 %collective-permute-done.11 = f32[4,32,256]{2,1,0:T(8,128)S(1)} collective-permute-done((f32[4,32,256]{2,1,0:T(8,128)S(1)}, f32[4,32,256]{2,1,0:T(8,128)S(1)}, u32[]{:S(2)}, u32[]{:S(2)}) %collective-permute-start.11) | collective-permute-done | bytes 131104 | tf_op jit(solution)/shard_map/ppermute | solution.py:299
  50.0 0.1 collective-permute-done.12
  50.1 0.1 select_select_fusion.3
  50.2 0.1 select_select_fusion.2
  50.2 0.8 %pad_maximum_fusion = f32[4,128,256]{2,1,0:T(8,128)} fusion(f32[4,32,256]{2,1,0:T(8,128)S(1)} %get-tuple-element.40, f32[4,32,256]{2,1,0:T(8,128)S(1)} %get-tuple-element.41, f32[4,32,256]{2,1,0:T(8,128)S(1)} %get-tuple-element.39, f32[4,32,256]{2,1,0:T(8,128)S(1)} %get-tuple-element.30), kind=kLoop, calls=%fused_computation | loop fusion | flops 393216 | bytes 1048576 | tf_op jit(solution)/shard_map/concatenate | solution.py:334
  (16 shorter events, 0.3 us)
Async XLA Ops:
  0.7 5.9 %copy-start = (s32[4,128,256]{2,1,0:T(8,128)S(1)}, s32[4,128,256]{2,1,0:T(8,128)}, u32[]{:S(2)}) copy-start(s32[4,128,256]{2,1,0:T(8,128)} %param.5) | copy-start | bytes 1572868
  2.0 10.2 %collective-permute-start = (f32[2,4,32,256]{3,2,1,0:T(8,128)S(1)}, f32[2,4,32,256]{3,2,1,0:T(8,128)S(1)}, u32[]{:S(2)}, u32[]{:S(2)}) collective-permute-start(f32[2,4,32,256]{3,2,1,0:T(8,128)S(1)} %get-tuple-element.33), channel_id=1, source_target_pairs={{0,2},{1,3},{2,0},{3,1},{4,6},{5,7},{6,4},{7,5},{8,10},{9,11},{10,... | collective-permute-start | bytes 786440 | tf_op jit(solution)/shard_map/ppermute | solution.py:299
  5.1 14.8 %collective-permute-start.1 = (f32[2,4,32,256]{3,2,1,0:T(8,128)S(1)}, f32[2,4,32,256]{3,2,1,0:T(8,128)S(1)}, u32[]{:S(2)}, u32[]{:S(2)}) collective-permute-start(f32[2,4,32,256]{3,2,1,0:T(8,128)S(1)} %get-tuple-element.35), channel_id=1, source_target_pairs={{0,4},{1,5},{2,6},{3,7},{4,0},{5,1},{6,2},{7,3},{8,12},{9,13},{10,... | collective-permute-start | bytes 786440 | tf_op jit(solution)/shard_map/ppermute | solution.py:299
  6.6 13.3 %collective-permute-start.2 = (f32[2,4,32,256]{3,2,1,0:T(8,128)S(1)}, f32[2,4,32,256]{3,2,1,0:T(8,128)S(1)}, u32[]{:S(2)}, u32[]{:S(2)}) collective-permute-start(f32[2,4,32,256]{3,2,1,0:T(8,128)S(1)} %get-tuple-element.32), channel_id=1, source_target_pairs={{0,6},{1,7},{2,4},{3,5},{4,2},{5,3},{6,0},{7,1},{8,14},{9,15},{10,... | collective-permute-start | bytes 786440 | tf_op jit(solution)/shard_map/ppermute | solution.py:299
  6.7 14.0 %collective-permute-start.4 = (s32[4,32,256]{2,1,0:T(8,128)S(1)}, s32[4,32,256]{2,1,0:T(8,128)S(1)}, u32[]{:S(2)}, u32[]{:S(2)}) collective-permute-start(s32[4,32,256]{2,1,0:T(8,128)S(1)} %get-tuple-element.43), channel_id=1, source_target_pairs={{0,2},{1,3},{2,0},{3,1},{4,6},{5,7},{6,4},{7,5},{8,10},{9,11},{10,... | collective-permute-start | bytes 393224 | tf_op jit(solution)/shard_map/ppermute | solution.py:299
  8.7 15.4 %collective-permute-start.5 = (s32[4,32,256]{2,1,0:T(8,128)S(1)}, s32[4,32,256]{2,1,0:T(8,128)S(1)}, u32[]{:S(2)}, u32[]{:S(2)}) collective-permute-start(s32[4,32,256]{2,1,0:T(8,128)S(1)} %get-tuple-element.45), channel_id=1, source_target_pairs={{0,4},{1,5},{2,6},{3,7},{4,0},{5,1},{6,2},{7,3},{8,12},{9,13},{10,... | collective-permute-start | bytes 393224 | tf_op jit(solution)/shard_map/ppermute | solution.py:299
  12.2 11.8 %collective-permute-start.6 = (s32[4,32,256]{2,1,0:T(8,128)S(1)}, s32[4,32,256]{2,1,0:T(8,128)S(1)}, u32[]{:S(2)}, u32[]{:S(2)}) collective-permute-start(s32[4,32,256]{2,1,0:T(8,128)S(1)} %get-tuple-element.42), channel_id=1, source_target_pairs={{0,6},{1,7},{2,4},{3,5},{4,2},{5,3},{6,0},{7,1},{8,14},{9,15},{10,... | collective-permute-start | bytes 393224 | tf_op jit(solution)/shard_map/ppermute | solution.py:299
  19.9 0.7 %copy-start.2 = (f32[8]{0:T(128)S(1)}, f32[8]{0:T(128)}, u32[]{:S(2)}) copy-start(f32[8]{0:T(128)} %param.7) | copy-start | bytes 100
  20.0 0.7 %copy-start.1 = (f32[3,8]{1,0:T(4,128)S(1)}, f32[3,8]{1,0:T(4,128)}, u32[]{:S(2)}) copy-start(f32[3,8]{1,0:T(4,128)} %param.6) | copy-start | bytes 292
  20.0 7.9 %collective-permute-start.7 = (f32[2,2,4,32,256]{4,3,2,1,0:T(8,128)S(1)}, f32[2,2,4,32,256]{4,3,2,1,0:T(8,128)S(1)}, u32[]{:S(2)}, u32[]{:S(2)}) collective-permute-start(f32[2,2,4,32,256]{4,3,2,1,0:T(8,128)S(1)} %get-tuple-element.21), channel_id=1, source_target_pairs={{0,1},{1,0},{2,3},{3,2},{4,5},{5,4},{6,7},{7,6},{8,9},{9,8},{10,11... | collective-permute-start | bytes 1572872 | tf_op jit(solution)/shard_map/ppermute | solution.py:302
  24.1 3.8 %collective-permute-start.8 = (s32[2,4,32,256]{3,2,1,0:T(8,128)S(1)}, s32[2,4,32,256]{3,2,1,0:T(8,128)S(1)}, u32[]{:S(2)}, u32[]{:S(2)}) collective-permute-start(s32[2,4,32,256]{3,2,1,0:T(8,128)S(1)} %route.3), channel_id=1, source_target_pairs={{0,1},{1,0},{2,3},{3,2},{4,5},{5,4},{6,7},{7,6},{8,9},{9,8},{10,11... | collective-permute-start | bytes 786440 | tf_op jit(solution)/shard_map/ppermute | solution.py:302
  24.2 9.8 %collective-permute-start.3 = (f32[2,4,32,256]{3,2,1,0:T(8,128)S(1)}, f32[2,4,32,256]{3,2,1,0:T(8,128)S(1)}, u32[]{:S(2)}, u32[]{:S(2)}) collective-permute-start(f32[2,4,32,256]{3,2,1,0:T(8,128)S(1)} %get-tuple-element.16), channel_id=1, source_target_pairs={{0,25},{1,8},{2,27},{3,10},{4,29},{5,12},{6,31},{7,14},{8,1},{9,16... | collective-permute-start | bytes 786440 | tf_op jit(solution)/shard_map/ppermute | solution.py:320
  35.3 1.7 %collective-permute-start.9 = (f32[10,32,256]{2,1,0:T(8,128)S(1)}, f32[10,32,256]{2,1,0:T(8,128)S(1)}, u32[]{:S(2)}, u32[]{:S(2)}) collective-permute-start(f32[10,32,256]{2,1,0:T(8,128)S(1)} %get-tuple-element.28), channel_id=1, source_target_pairs={{0,1},{1,0},{2,3},{3,2},{4,5},{5,4},{6,7},{7,6},{8,9},{9,8},{10,11... | collective-permute-start | bytes 983048 | tf_op jit(solution)/shard_map/ppermute | solution.py:302
  37.0 7.3 %collective-permute-start.13 = (f32[4,16,256]{2,1,0:T(8,128)S(1)}, f32[4,16,256]{2,1,0:T(8,128)S(1)}, u32[]{:S(2)}, u32[]{:S(2)}) collective-permute-start(f32[4,16,256]{2,1,0:T(8,128)S(1)} %pad_maximum_fusion.1), channel_id=1, source_target_pairs={{0,24},{8,16},{16,8},{24,0},{1,25},{9,17},{17,9},{25,1},{2,26},{10... | collective-permute-start | bytes 196616 | tf_op jit(solution)/shard_map/ppermute | solution.py:340
  39.5 6.3 %collective-permute-start.14 = (f32[4,16,256]{2,1,0:T(8,128)S(1)}, f32[4,16,256]{2,1,0:T(8,128)S(1)}, u32[]{:S(2)}, u32[]{:S(2)}) collective-permute-start(f32[4,16,256]{2,1,0:T(8,128)S(1)} %pad_maximum_fusion.1), channel_id=1, source_target_pairs={{0,16},{8,24},{16,0},{24,8},{1,17},{9,25},{17,1},{25,9},{2,18},{10... | collective-permute-start | bytes 196616 | tf_op jit(solution)/shard_map/ppermute | solution.py:340
  39.5 6.3 %collective-permute-start.15 = (f32[4,16,256]{2,1,0:T(8,128)S(1)}, f32[4,16,256]{2,1,0:T(8,128)S(1)}, u32[]{:S(2)}, u32[]{:S(2)}) collective-permute-start(f32[4,16,256]{2,1,0:T(8,128)S(1)} %pad_maximum_fusion.1), channel_id=1, source_target_pairs={{0,8},{8,0},{16,24},{24,16},{1,9},{9,1},{17,25},{25,17},{2,10},{10... | collective-permute-start | bytes 196616 | tf_op jit(solution)/shard_map/ppermute | solution.py:340
  41.5 7.2 %collective-permute-start.10 = (f32[4,32,256]{2,1,0:T(8,128)S(1)}, f32[4,32,256]{2,1,0:T(8,128)S(1)}, u32[]{:S(2)}, u32[]{:S(2)}) collective-permute-start(f32[4,32,256]{2,1,0:T(8,128)S(1)} %get-tuple-element.37), channel_id=1, source_target_pairs={{0,6},{1,7},{2,4},{3,5},{4,2},{5,3},{6,0},{7,1},{8,14},{9,15},{10,... | collective-permute-start | bytes 393224 | tf_op jit(solution)/shard_map/ppermute | solution.py:299
  43.1 6.9 %collective-permute-start.11 = (f32[4,32,256]{2,1,0:T(8,128)S(1)}, f32[4,32,256]{2,1,0:T(8,128)S(1)}, u32[]{:S(2)}, u32[]{:S(2)}) collective-permute-start(f32[4,32,256]{2,1,0:T(8,128)S(1)} %get-tuple-element.38), channel_id=1, source_target_pairs={{0,4},{1,5},{2,6},{3,7},{4,0},{5,1},{6,2},{7,3},{8,12},{9,13},{10,... | collective-permute-start | bytes 393224 | tf_op jit(solution)/shard_map/ppermute | solution.py:299
  44.3 5.7 %collective-permute-start.12 = (f32[4,32,256]{2,1,0:T(8,128)S(1)}, f32[4,32,256]{2,1,0:T(8,128)S(1)}, u32[]{:S(2)}, u32[]{:S(2)}) collective-permute-start(f32[4,32,256]{2,1,0:T(8,128)S(1)} %get-tuple-element.36), channel_id=1, source_target_pairs={{0,2},{1,3},{2,0},{3,1},{4,6},{5,7},{6,4},{7,5},{8,10},{9,11},{10,... | collective-permute-start | bytes 393224 | tf_op jit(solution)/shard_map/ppermute | solution.py:299

commit v4 on v3

v4 whole, which is shorter than its diff:
```python
import functools

import jax
import jax.numpy as jnp
from jax import lax
from jax.experimental import pallas as pl
from jax.experimental.pallas import tpu as pltpu
from jax.sharding import PartitionSpec as P

COURANT = 0.4
DEPTH_SCALE = 2.5
LANES = 128
F32 = jnp.float32
GRANT = 12 << 20
VMEM = pl.BlockSpec(memory_space=pltpu.VMEM)


def swap_pairs(members, mask):
    return [(w, w ^ mask) for w in range(members)]


def pick(arrays, index):
    out = arrays[0]
    for number in range(1, len(arrays)):
        out = jnp.where(index == number, arrays[number], out)
    return out


def advance(state, stage, density, momentum, emit):
    if stage == 4:
        emit(density)
        return
    last = stage == 3
    velocity = momentum / density
    speed = jnp.abs(velocity) + 1.0
    pressure = None if last else momentum * velocity + density
    held = state[stage]
    if held is None:
        state[stage] = (density, momentum, speed, pressure, None, None)
        return
    density0, momentum0, speed0, pressure0, mass0, force0 = held
    face = jnp.maximum(speed0, speed)
    mass = (momentum0 + momentum) - face * (density - density0)
    force = None if last else (pressure0 + pressure) - face * (momentum - momentum0)
    state[stage] = (density, momentum, speed, pressure, mass, force)
    if mass0 is None:
        return
    density1 = density0 - (0.5 * COURANT) * (mass - mass0)
    momentum1 = None if last else momentum0 - (0.5 * COURANT) * (force - force0)
    advance(state, stage + 1, density1, momentum1, emit)


def sweep_tiles(rows, columns, layers, count, load, place, dense):
    tall = min(8, rows)
    across = columns // LANES

    def tile(number, carry):
        row = pl.ds(pl.multiple_of(number // across * tall, tall), tall)
        column = pl.ds(pl.multiple_of(number % across * LANES, LANES), LANES)

        def block(state, position):
            for layer in range(layers):
                at = position * layers + layer

                def emit(density):
                    dense[place(at - 2 * layers), row, column] = density

                advance(state, 0, *load(at, row, column), emit)

        state = [None] * 4
        block(state, 0)
        block(state, 1)
        if count <= 5:
            for position in range(2, count):
                block(state, position)
        else:

            def step(position, state):
                state = list(state)
                block(state, position)
                return state

            lax.fori_loop(2, count, step, state)
        return carry

    lax.fori_loop(0, rows // tall * across, tile, 0)


def inner_kernel(chips, *refs):
    own, (other, dense, edge, fluid) = refs[:chips], refs[chips:]
    member = lax.axis_index("swap")
    chip, upper = member // 2, member % 2
    half = chips // 2
    _, layers, rows, columns = own[0].shape
    for d in range(chips):
        k = chip ^ d

        @pl.when(k // half == upper)
        def _():
            at = 2 * (k - upper * half) + 2 * upper
            fluid[:, pl.ds(at * layers, layers)] = own[d][...]

        @pl.when(k == jnp.where(upper == 1, half - 1, half))
        def _():
            at = jnp.where(upper == 1, 0, chips)
            fluid[:, pl.ds(at * layers, layers)] = own[d][...]

    for i in range(half):
        fluid[:, pl.ds((2 * i + 1) * layers, layers)] = other[i]

    total = (chips + 1) * layers
    sign = jnp.where(upper == 1, 1.0, -1.0)

    def load(at, row, column):
        at = jnp.where(upper == 1, at, total - 1 - at)
        return fluid[0, at, row, column], sign * fluid[1, at, row, column]

    def place(own):
        return jnp.where(upper == 1, own, chips * layers - 1 - own)

    sweep_tiles(rows, columns, layers, chips + 1, load, place, dense)
    edge[...] = fluid[:, pl.ds(jnp.where(upper == 1, chips - 1, 0) * layers, 2 * layers)]


def outer_kernel(chips, far, edge, dense, keep, give, last):
    upper = lax.axis_index("swap") % 2
    half = chips // 2
    _, layers, rows, columns = far.shape
    sign = jnp.where(upper == 1, -1.0, 1.0)

    def load(at, row, column):
        source, base, size = (far, at, layers) if at < layers else (edge, at - layers, 2 * layers)
        base = jnp.where(upper == 1, size - 1 - base, base)
        return source[0, base, row, column], sign * source[1, base, row, column]

    def place(own):
        return jnp.where(upper == 1, layers - 1 - own, own)

    sweep_tiles(rows, columns, layers, 3, load, place, last)
    for i in range(half):
        keep[i] = dense[pl.ds((2 * i + upper) * layers, layers)]
        give[i] = dense[pl.ds((2 * i + 1 - upper) * layers, layers)]
    keep[jnp.where(upper == 1, half - 1, 0)] = last[...]


def render_kernel(chips, *refs):
    kinds, (table, keep, given, tile, sent, dense, kind) = refs[:chips], refs[chips:]
    member = lax.axis_index("swap")
    chip, upper = member // 2, member % 2
    half, layers, rows, columns = keep.shape
    for d in range(chips):
        k = chip ^ d

        @pl.when(k // half == upper)
        def _():
            kind[pl.ds(2 * (k - upper * half) * layers, 2 * layers)] = kinds[d][...].reshape(2 * layers, rows, columns)

    for i in range(half):
        dense[pl.ds((2 * i + upper) * layers, layers)] = keep[i]
        dense[pl.ds((2 * i + 1 - upper) * layers, layers)] = given[i]

    tall = min(8, rows // 2)
    across = columns // LANES
    tables = [table[n, :tall, :] for n in range(4)]

    def shade(at, light, row, column):
        which = kind[at, row, column]
        factor, *colours = (jnp.take_along_axis(values, which, axis=1) for values in tables)
        through = jnp.exp(-(factor * dense[at, row, column]))
        weight = light[0] * (1.0 - through)
        return (light[0] * through, *(sum_ + weight * colour for sum_, colour in zip(light[1:], colours)))

    depth = chips * layers
    half_rows = rows // 2

    def strip(number, carry):
        column = pl.ds(pl.multiple_of(number * LANES, LANES), LANES)
        for row in range(0, rows, tall):
            zero = jnp.zeros((tall, LANES), F32)
            light = (zero + 1.0, zero, zero, zero)
            where = pl.ds(row, tall)
            if depth <= 16:
                for at in range(depth):
                    light = shade(at, light, where, column)
            else:
                light = lax.fori_loop(0, depth, lambda at, light: shade(at, light, where, column), light)
            base = row % half_rows
            for n, value in enumerate((*light[1:], light[0])):

                @pl.when(upper == row // half_rows)
                def _():
                    tile[n, base : base + tall, column] = value

                @pl.when(upper != row // half_rows)
                def _():
                    sent[n, base : base + tall, column] = value

        return carry

    lax.fori_loop(0, across, strip, 0)


def route_kernel(chips, *refs):
    own, (other, outer) = refs[:chips], refs[chips:]
    member = lax.axis_index("swap")
    chip, upper = member // 2, member % 2
    half = chips // 2
    for d in range(chips):
        k = chip ^ d

        @pl.when(k // half != upper)
        def _():
            other[k - (1 - upper) * half] = own[d][...]

        @pl.when(k == upper * (chips - 1))
        def _():
            outer[...] = own[d][...]


def call(kernel, operands, outs, scratch=(), cells=0):
    return pl.pallas_call(
        kernel,
        out_shape=[jax.ShapeDtypeStruct(shape, F32) for shape in outs],
        in_specs=[VMEM] * len(operands),
        out_specs=[VMEM] * len(outs),
        scratch_shapes=[pltpu.VMEM(shape, dtype) for shape, dtype in scratch],
        compiler_params=pltpu.CompilerParams(vmem_limit_bytes=GRANT),
        cost_estimate=pl.CostEstimate(flops=300 * cells, bytes_accessed=16 * cells, transcendentals=6 * cells),
    )(*operands)


def over(nearer, farther):
    return jnp.concatenate([nearer[:3] + nearer[3:4] * farther[:3], nearer[3:4] * farther[3:4]], axis=0)


def per_device(fluid_state, material, table_colour, table_extinction):
    slabs = lax.axis_size("slab")
    members = lax.axis_size("swap")
    chips = members // 2
    half = chips // 2
    member = lax.axis_index("swap")
    slab = lax.axis_index("slab")
    chip, upper = member // 2, member % 2
    _, layers, height, width = fluid_state.shape
    rows = height // chips

    def to_chip(block, d):
        if d == 0:
            return block
        return lax.ppermute(block, "swap", swap_pairs(members, 2 * d))

    def to_core(block):
        return lax.ppermute(block, "swap", swap_pairs(members, 1))

    scale = DEPTH_SCALE / (layers * slabs * members)
    table = jnp.concatenate([table_extinction[None] * scale, table_colour], axis=0)
    table = jnp.pad(table, ((0, 0), (0, LANES - table.shape[1])))
    table = jnp.broadcast_to(table[:, None, :], (4, 8, LANES))

    def cut(array, j, axis):
        return lax.dynamic_slice_in_dim(array, j * rows, rows, axis=axis)

    own = [to_chip(cut(fluid_state, chip ^ d, 2), d) for d in range(chips)]

    theirs = to_core(material)
    both = jnp.stack([jnp.where(upper == 1, theirs, material), jnp.where(upper == 1, material, theirs)])
    cuts = [cut(both, chip ^ d, 2) for d in range(chips)]
    senders = [w for w in range(members) if w % 2 == w // 2 // half]
    kinds = [cuts[0]]
    for d in range(1, chips):
        kinds.append(lax.ppermute(cuts[d], "swap", [(w, w ^ (2 * d)) for w in senders]))

    block = (layers, rows, width)
    cells = layers * rows * width
    other, outer = call(functools.partial(route_kernel, chips), own, [(half, 2, *block), (2, *block)])
    other = to_core(other)
    ring = []
    for z in range(slabs):
        for w in range(members):
            to = ((z + 1) % slabs, w - 1) if w % 2 else ((z - 1) % slabs, w + 1)
            ring.append((z * members + w, to[0] * members + to[1]))
    far = lax.ppermute(outer, ("slab", "swap"), ring)

    dense, edge = call(
        functools.partial(inner_kernel, chips),
        [*own, other],
        [(chips * layers, rows, width), (2, 2 * layers, rows, width)],
        [((2, (chips + 1) * layers, rows, width), F32)],
        chips * cells,
    )
    keep, give = call(
        functools.partial(outer_kernel, chips),
        [far, edge, dense],
        [(half, *block), (half, *block)],
        [(block, F32)],
        cells,
    )
    got = to_core(give)
    short = (4, rows // 2, width)
    tile, sent = call(
        functools.partial(render_kernel, chips),
        [*kinds, table, keep, give],
        [short, short],
        [((chips * layers, rows, width), F32), ((chips * layers, rows, width), jnp.int32)],
        chips * cells,
    )
    partner = to_core(sent)

    kept = [keep[i] for i in range(half)]
    gotten = [got[i] for i in range(half)]
    chunks = []
    for d in range(chips):
        k = chip ^ d
        back = jnp.where(k // half == upper, pick(kept, k % half), pick(gotten, k % half))
        chunks.append(to_chip(back, d))
    density = jnp.concatenate([pick(chunks, chip ^ j) for j in range(chips)], axis=1)

    tile = over(jnp.where(upper == 1, partner, tile), jnp.where(upper == 1, tile, partner))
    pieces = [tile]
    for away in range(1, slabs):
        pieces.append(lax.ppermute(tile, "slab", swap_pairs(slabs, away)))
    ordered = [pick(pieces, slab ^ z) for z in range(slabs)]
    rendered = functools.reduce(over, ordered)
    rendered = jnp.concatenate([rendered[:3], 1.0 - rendered[3:4]], axis=0).reshape(4, height * width // members)
    return density, rendered


def solution(mesh):
    return jax.shard_map(
        per_device,
        mesh=mesh,
        in_specs=(P(None, ("slab", "swap"), None, None), P(("slab", "swap"), None, None), P(), P()),
        out_specs=(P(("slab", "swap"), None, None), P(None, "swap")),
        check_vma=False,
    )
```

time: 51.2 us -> 56.7 us (1.11)
  waiting for transfers between devices: 19.5 us -> 24.7 us
  Pallas kernels: 3.65 us -> 4.84 us
  local copies, waits for them, and re-layouts: 2.66 us -> 1.96 us
    ppermute x9 -> x6, starting transfers between devices: 14.6 us -> 8.14 us  [to_chip(): return lax.ppermute(block, 'swap', swap_pairs(members, 2 * d))]
    ppermute x0 -> x3, starting transfers between devices: none -> 5.74 us  [per_device(): lax.ppermute(cuts[d], 'swap', [(w, w ^ 2 * d) for w in senders])]
    ppermute x1, waiting for transfers between devices: 3.82 us -> 0.01 us  [per_device(): far = lax.ppermute(outer, ('slab', 'swap'), ring)]
    ppermute x9 -> x6, waiting for transfers between devices: 13.5 us -> 17.2 us  [to_chip(): return lax.ppermute(block, 'swap', swap_pairs(members, 2 * d))]
    ppermute x3, waiting for transfers between devices: 0.75 us -> 3.96 us  [per_device(): pieces.append(lax.ppermute(tile, 'slab', swap_pairs(slabs, away)))]
    ppermute x0 -> x3, waiting for transfers between devices: none -> 2.25 us  [per_device(): lax.ppermute(cuts[d], 'swap', [(w, w ^ 2 * d) for w in senders])]
    pallas_call x4, Pallas kernels: 3.65 us -> 4.84 us  [call(): pl.pallas_call(kernel, out_shape=[jax.ShapeDtypeStruct(shape, F32) for sh...]
    unnamed x7, local copies, waits for them, and re-layouts: 1.27 us -> 0.69 us
  transfers between devices with their start and end apart: 16 -> 17, of which waited for: 9 -> 9; matrix products, arithmetic and copies ran while one was open for 2% -> 4% of each run, Pallas kernels for 5% -> 5%
where the time goes in v4:
time: 56.7 us; the launch traced here: 56.5 us
  waiting for transfers between devices  24.7 us (44%)
  starting transfers between devices  22.7 us (40%)
  Pallas kernels  4.84 us (9%)
  local copies, waits for them, and re-layouts  1.96 us (3%)
  other arithmetic  1.35 us (2%)
  between operations  0.89 us (2%)
    ppermute x6, waiting for transfers between devices, to_chip(): return lax.ppermute(block, 'swap', swap_pairs(members, 2 * d))  17.2 us
    ppermute x6, starting transfers between devices, to_chip(): return lax.ppermute(block, 'swap', swap_pairs(members, 2 * d))  8.14 us
    ppermute x3, starting transfers between devices, per_device(): lax.ppermute(cuts[d], 'swap', [(w, w ^ 2 * d) for w in senders])  5.74 us
    pallas_call x4, Pallas kernels, call(): pl.pallas_call(kernel, out_shape=[jax.ShapeDtypeStruct(shape, F32) for sh...  4.84 us
    ppermute x3, starting transfers between devices, per_device(): pieces.append(lax.ppermute(tile, 'slab', swap_pairs(slabs, away)))  4.45 us
    ppermute x3, waiting for transfers between devices, per_device(): pieces.append(lax.ppermute(tile, 'slab', swap_pairs(slabs, away)))  3.96 us
    ppermute x1, starting transfers between devices, per_device(): far = lax.ppermute(outer, ('slab', 'swap'), ring)  3.7 us
    ppermute x3, waiting for transfers between devices, per_device(): lax.ppermute(cuts[d], 'swap', [(w, w ^ 2 * d) for w in senders])  2.25 us
  transfers between devices with their start and end apart: 17, of which 9 were waited for; matrix products, arithmetic and copies ran while one was open for 4% of the time, Pallas kernels for 5%

profile of v4, /device:TPU:0, one launch (start us, length us, event | category | flops | bytes accessed | tf_op | source)
XLA Modules:
  0.0 56.5 jit_solution(1703188462675496776)
XLA Ops:
  0.6 0.6 collective-permute-start.9
  1.2 1.3 %constant_dynamic-slice_fusion = (f32[2,4,32,256]{3,2,1,0:T(8,128)S(1)}, f32[2,4,32,256]{3,2,1,0:T(8,128)S(1)}, f32[2,4,32,256]{3,2,1,0:T(8,128)S(1)}, f32[2,4,32,256]{3,2,1,0:T(8,128)S(1)}) fusion(f32[2,4,128,256]{3,2,1,0:T(8,128)} %param.4, s32[]{:T(128)S(6)} %select_n.327, s32[]{:T(128)S(6)} %select_n.325, s32[]{:T(128)S(6)} %select_n.324, s32[]{:T(128)S(6)} %select_n.326), kind=kLoop, calls=%fused_computation.55 | loop fusion | bytes 2097168 | tf_op jit(solution)/shard_map/dynamic_slice | solution.py:261
  2.5 2.6 %collective-permute-start = (f32[2,4,32,256]{3,2,1,0:T(8,128)S(1)}, f32[2,4,32,256]{3,2,1,0:T(8,128)S(1)}, u32[]{:S(2)}, u32[]{:S(2)}) collective-permute-start(f32[2,4,32,256]{3,2,1,0:T(8,128)S(1)} %get-tuple-element.27), channel_id=1, source_target_pairs={{0,2},{1,3},{2,0},{3,1},{4,6},{5,7},{6,4},{7,5},{8,10},{9,11},{10,... | collective-permute-start | bytes 786440 | tf_op jit(solution)/shard_map/ppermute | solution.py:250
  5.1 1.5 %collective-permute-start.1 = (f32[2,4,32,256]{3,2,1,0:T(8,128)S(1)}, f32[2,4,32,256]{3,2,1,0:T(8,128)S(1)}, u32[]{:S(2)}, u32[]{:S(2)}) collective-permute-start(f32[2,4,32,256]{3,2,1,0:T(8,128)S(1)} %get-tuple-element.29), channel_id=1, source_target_pairs={{0,4},{1,5},{2,6},{3,7},{4,0},{5,1},{6,2},{7,3},{8,12},{9,13},{10,... | collective-permute-start | bytes 786440 | tf_op jit(solution)/shard_map/ppermute | solution.py:250
  6.6 0.0 collective-permute-start.2
  6.6 5.6 %collective-permute-done.refs_1_ = f32[2,4,32,256]{3,2,1,0:T(8,128)S(1)} collective-permute-done((f32[2,4,32,256]{3,2,1,0:T(8,128)S(1)}, f32[2,4,32,256]{3,2,1,0:T(8,128)S(1)}, u32[]{:S(2)}, u32[]{:S(2)}) %collective-permute-start) | collective-permute-done | bytes 262176 | tf_op jit(solution)/shard_map/ppermute | solution.py:250
  12.2 6.8 %collective-permute-done.1.refs_2_ = f32[2,4,32,256]{3,2,1,0:T(8,128)S(1)} collective-permute-done((f32[2,4,32,256]{3,2,1,0:T(8,128)S(1)}, f32[2,4,32,256]{3,2,1,0:T(8,128)S(1)}, u32[]{:S(2)}, u32[]{:S(2)}) %collective-permute-start.1) | collective-permute-done | bytes 262176 | tf_op jit(solution)/shard_map/ppermute | solution.py:250
  19.1 0.0 collective-permute-done.2.refs_3_
  19.1 0.1 shard_map.59
  19.2 0.1 collective-permute-start.4
  19.2 3.7 %collective-permute-start.3 = (f32[2,4,32,256]{3,2,1,0:T(8,128)S(1)}, f32[2,4,32,256]{3,2,1,0:T(8,128)S(1)}, u32[]{:S(2)}, u32[]{:S(2)}) collective-permute-start(f32[2,4,32,256]{3,2,1,0:T(8,128)S(1)} %get-tuple-element.10), channel_id=1, source_target_pairs={{0,25},{1,8},{2,27},{3,10},{4,29},{5,12},{6,31},{7,14},{8,1},{9,16... | collective-permute-start | bytes 786440 | tf_op jit(solution)/shard_map/ppermute | solution.py:282
  22.9 0.0 collective-permute-done.9
  23.0 0.1 select_bitcast_fusion
  23.1 0.1 fusion
  23.2 3.1 %collective-permute-start.10 = (s32[2,4,32,256]{3,2,1,0:T(8,128)S(1)}, s32[2,4,32,256]{3,2,1,0:T(8,128)S(1)}, u32[]{:S(2)}, u32[]{:S(2)}) collective-permute-start(s32[2,4,32,256]{3,2,1,0:T(8,128)S(1)} %get-tuple-element.22), channel_id=1, source_target_pairs={{0,2},{2,0},{5,7},{7,5},{8,10},{10,8},{13,15},{15,13},{16,18},{18,... | collective-permute-start | bytes 786440 | tf_op jit(solution)/shard_map/ppermute | solution.py:271
  26.3 0.0 copy-start.2
  26.3 0.0 copy-start.1
  26.3 1.3 %collective-permute-start.11 = (s32[2,4,32,256]{3,2,1,0:T(8,128)S(1)}, s32[2,4,32,256]{3,2,1,0:T(8,128)S(1)}, u32[]{:S(2)}, u32[]{:S(2)}) collective-permute-start(s32[2,4,32,256]{3,2,1,0:T(8,128)S(1)} %get-tuple-element.23), channel_id=1, source_target_pairs={{0,4},{2,6},{5,1},{7,3},{8,12},{10,14},{13,9},{15,11},{16,20},{18,... | collective-permute-start | bytes 786440 | tf_op jit(solution)/shard_map/ppermute | solution.py:271
  27.6 1.3 %collective-permute-start.12 = (s32[2,4,32,256]{3,2,1,0:T(8,128)S(1)}, s32[2,4,32,256]{3,2,1,0:T(8,128)S(1)}, u32[]{:S(2)}, u32[]{:S(2)}) collective-permute-start(s32[2,4,32,256]{3,2,1,0:T(8,128)S(1)} %get-tuple-element.20), channel_id=1, source_target_pairs={{0,6},{2,4},{5,3},{7,1},{8,14},{10,12},{13,11},{15,9},{16,22},{18,... | collective-permute-start | bytes 786440 | tf_op jit(solution)/shard_map/ppermute | solution.py:271
  29.0 0.0 collective-permute-done.4.refs_4_
  29.0 2.0 %shard_map.60 = (f32[16,32,256]{2,1,0:T(8,128)S(1)}, f32[2,8,32,256]{3,2,1,0:T(8,128)S(1)}) custom-call(f32[2,4,32,256]{3,2,1,0:T(8,128)S(1)} %get-tuple-element.28.refs_0_, f32[2,4,32,256]{3,2,1,0:T(8,128)S(1)} %collective-permute-done.refs_1_, f32[2,4,32,256]{3,2,1,0:T(8,128)S(1)} %collective-permute-done.1.refs_2_, ...), custom_call_target="tpu_custom_call" | custom-call | flops 39321600 | bytes 2097152 | tf_op jit(solution)/shard_map/pallas_call | solution.py:221
  31.0 0.0 collective-permute-done.3.far
  31.0 1.0 %shard_map.61 = (f32[2,4,32,256]{3,2,1,0:T(8,128)S(1)}, f32[2,4,32,256]{3,2,1,0:T(8,128)S(1)}) custom-call(f32[2,4,32,256]{3,2,1,0:T(8,128)S(1)} %collective-permute-done.3.far, f32[2,8,32,256]{3,2,1,0:T(8,128)S(1)} %get-tuple-element.12.edge, f32[16,32,256]{2,1,0:T(8,128)S(1)} %get-tuple-element.13.dense), custom_call_target="tpu_custom_call" | custom-call | flops 9830400 | bytes 524288 | tf_op jit(solution)/shard_map/pallas_call | solution.py:221
  32.1 0.0 collective-permute-done.10.refs_1_
  32.1 2.2 %collective-permute-done.11.refs_2_ = s32[2,4,32,256]{3,2,1,0:T(8,128)S(1)} collective-permute-done((s32[2,4,32,256]{3,2,1,0:T(8,128)S(1)}, s32[2,4,32,256]{3,2,1,0:T(8,128)S(1)}, u32[]{:S(2)}, u32[]{:S(2)}) %collective-permute-start.11) | collective-permute-done | bytes 262176 | tf_op jit(solution)/shard_map/ppermute | solution.py:271
  34.3 0.0 collective-permute-done.12.refs_3_
  34.3 1.7 %shard_map.62 = (f32[4,16,256]{2,1,0:T(8,128)S(1)}, f32[4,16,256]{2,1,0:T(8,128)S(1)}) custom-call(s32[2,4,32,256]{3,2,1,0:T(8,128)S(1)} %get-tuple-element.21.refs_0_, s32[2,4,32,256]{3,2,1,0:T(8,128)S(1)} %collective-permute-done.10.refs_1_, s32[2,4,32,256]{3,2,1,0:T(8,128)S(1)} %collective-permute-done.11.refs_2_, ...), custom_call_target="tpu_custom_call" | custom-call | flops 39321600 | bytes 2097152 | tf_op jit(solution)/shard_map/pallas_call | solution.py:221
  36.1 0.1 collective-permute-start.13
  36.1 1.2 %collective-permute-done.13 = f32[4,16,256]{2,1,0:T(8,128)S(1)} collective-permute-done((f32[4,16,256]{2,1,0:T(8,128)S(1)}, f32[4,16,256]{2,1,0:T(8,128)S(1)}, u32[]{:S(2)}, u32[]{:S(2)}) %collective-permute-start.13) | collective-permute-done | bytes 65568 | tf_op jit(solution)/shard_map/ppermute | solution.py:253
  37.4 0.8 %collective-permute-start.14 = (f32[4,16,256]{2,1,0:T(8,128)S(1)}, f32[4,16,256]{2,1,0:T(8,128)S(1)}, u32[]{:S(2)}, u32[]{:S(2)}) collective-permute-start(f32[4,16,256]{2,1,0:T(8,128)S(1)} %pad_maximum_fusion.1), channel_id=1, source_target_pairs={{0,24},{8,16},{16,8},{24,0},{1,25},{9,17},{17,9},{25,1},{2,26},{10... | collective-permute-start | bytes 196616 | tf_op jit(solution)/shard_map/ppermute | solution.py:321
  38.3 0.1 collective-permute-start.15
  38.4 3.5 %collective-permute-start.16 = (f32[4,16,256]{2,1,0:T(8,128)S(1)}, f32[4,16,256]{2,1,0:T(8,128)S(1)}, u32[]{:S(2)}, u32[]{:S(2)}) collective-permute-start(f32[4,16,256]{2,1,0:T(8,128)S(1)} %pad_maximum_fusion.1), channel_id=1, source_target_pairs={{0,8},{8,0},{16,24},{24,16},{1,9},{9,1},{17,25},{25,17},{2,10},{10... | collective-permute-start | bytes 196616 | tf_op jit(solution)/shard_map/ppermute | solution.py:321
  41.9 0.0 collective-permute-start.5
  41.9 2.4 %collective-permute-done.14 = f32[4,16,256]{2,1,0:T(8,128)S(1)} collective-permute-done((f32[4,16,256]{2,1,0:T(8,128)S(1)}, f32[4,16,256]{2,1,0:T(8,128)S(1)}, u32[]{:S(2)}, u32[]{:S(2)}) %collective-permute-start.14) | collective-permute-done | bytes 65568 | tf_op jit(solution)/shard_map/ppermute | solution.py:321
  44.3 1.5 %collective-permute-done.15 = f32[4,16,256]{2,1,0:T(8,128)S(1)} collective-permute-done((f32[4,16,256]{2,1,0:T(8,128)S(1)}, f32[4,16,256]{2,1,0:T(8,128)S(1)}, u32[]{:S(2)}, u32[]{:S(2)}) %collective-permute-start.15) | collective-permute-done | bytes 65568 | tf_op jit(solution)/shard_map/ppermute | solution.py:321
  45.9 0.0 collective-permute-done.16
  45.9 0.0 collective-permute-done.5
  46.0 0.1 select_bitcast_fusion.2
  46.0 2.8 %collective-permute-start.6 = (f32[4,32,256]{2,1,0:T(8,128)S(1)}, f32[4,32,256]{2,1,0:T(8,128)S(1)}, u32[]{:S(2)}, u32[]{:S(2)}) collective-permute-start(f32[4,32,256]{2,1,0:T(8,128)S(1)} %get-tuple-element.34), channel_id=1, source_target_pairs={{0,6},{1,7},{2,4},{3,5},{4,2},{5,3},{6,0},{7,1},{8,14},{9,15},{10,... | collective-permute-start | bytes 393224 | tf_op jit(solution)/shard_map/ppermute | solution.py:250
  48.8 0.0 collective-permute-start.7
  48.8 1.2 %collective-permute-start.8 = (f32[4,32,256]{2,1,0:T(8,128)S(1)}, f32[4,32,256]{2,1,0:T(8,128)S(1)}, u32[]{:S(2)}, u32[]{:S(2)}) collective-permute-start(f32[4,32,256]{2,1,0:T(8,128)S(1)} %get-tuple-element.33), channel_id=1, source_target_pairs={{0,2},{1,3},{2,0},{3,1},{4,6},{5,7},{6,4},{7,5},{8,10},{9,11},{10,... | collective-permute-start | bytes 393224 | tf_op jit(solution)/shard_map/ppermute | solution.py:250
  50.0 0.7 %copy.6 = f32[1,4,16,256]{3,1,2,0:T(4,128)} copy(f32[1,4,16,256]{3,2,1,0:T(8,128)S(1)} %maximum_bitcast_fusion) | data formatting | bytes 131072
  50.7 1.7 %collective-permute-done.6 = f32[4,32,256]{2,1,0:T(8,128)S(1)} collective-permute-done((f32[4,32,256]{2,1,0:T(8,128)S(1)}, f32[4,32,256]{2,1,0:T(8,128)S(1)}, u32[]{:S(2)}, u32[]{:S(2)}) %collective-permute-start.6) | collective-permute-done | bytes 131104 | tf_op jit(solution)/shard_map/ppermute | solution.py:250
  52.4 2.2 %collective-permute-done.7 = f32[4,32,256]{2,1,0:T(8,128)S(1)} collective-permute-done((f32[4,32,256]{2,1,0:T(8,128)S(1)}, f32[4,32,256]{2,1,0:T(8,128)S(1)}, u32[]{:S(2)}, u32[]{:S(2)}) %collective-permute-start.7) | collective-permute-done | bytes 131104 | tf_op jit(solution)/shard_map/ppermute | solution.py:250
  54.6 0.9 %collective-permute-done.8 = f32[4,32,256]{2,1,0:T(8,128)S(1)} collective-permute-done((f32[4,32,256]{2,1,0:T(8,128)S(1)}, f32[4,32,256]{2,1,0:T(8,128)S(1)}, u32[]{:S(2)}, u32[]{:S(2)}) %collective-permute-start.8) | collective-permute-done | bytes 131104 | tf_op jit(solution)/shard_map/ppermute | solution.py:250
  55.5 0.1 fusion.5
  55.6 0.1 fusion.7
  55.6 0.8 %pad_maximum_fusion = f32[4,128,256]{2,1,0:T(8,128)} fusion(f32[4,32,256]{2,1,0:T(8,128)S(1)} %get-tuple-element.31, f32[4,32,256]{2,1,0:T(8,128)S(1)} %get-tuple-element.32, f32[4,32,256]{2,1,0:T(8,128)S(1)} %get-tuple-element.30, f32[4,32,256]{2,1,0:T(8,128)S(1)} %get-tuple-element.18), kind=kLoop, calls=%fused_computation.8 | loop fusion | flops 393216 | bytes 1048576 | tf_op jit(solution)/shard_map/concatenate | solution.py:316
  (16 shorter events, 0.1 us)
Async XLA Ops:
  0.6 22.3 %collective-permute-start.9 = (s32[4,128,256]{2,1,0:T(8,128)}, s32[4,128,256]{2,1,0:T(8,128)S(1)}, u32[]{:S(2)}, u32[]{:S(2)}) collective-permute-start(s32[4,128,256]{2,1,0:T(8,128)} %param.5), channel_id=1, source_target_pairs={{0,1},{1,0},{2,3},{3,2},{4,5},{5,4},{6,7},{7,6},{8,9},{9,8},{10,11... | collective-permute-start | bytes 1572872 | tf_op jit(solution)/shard_map/ppermute | solution.py:253
  2.5 9.8 %collective-permute-start = (f32[2,4,32,256]{3,2,1,0:T(8,128)S(1)}, f32[2,4,32,256]{3,2,1,0:T(8,128)S(1)}, u32[]{:S(2)}, u32[]{:S(2)}) collective-permute-start(f32[2,4,32,256]{3,2,1,0:T(8,128)S(1)} %get-tuple-element.27), channel_id=1, source_target_pairs={{0,2},{1,3},{2,0},{3,1},{4,6},{5,7},{6,4},{7,5},{8,10},{9,11},{10,... | collective-permute-start | bytes 786440 | tf_op jit(solution)/shard_map/ppermute | solution.py:250
  5.1 14.0 %collective-permute-start.1 = (f32[2,4,32,256]{3,2,1,0:T(8,128)S(1)}, f32[2,4,32,256]{3,2,1,0:T(8,128)S(1)}, u32[]{:S(2)}, u32[]{:S(2)}) collective-permute-start(f32[2,4,32,256]{3,2,1,0:T(8,128)S(1)} %get-tuple-element.29), channel_id=1, source_target_pairs={{0,4},{1,5},{2,6},{3,7},{4,0},{5,1},{6,2},{7,3},{8,12},{9,13},{10,... | collective-permute-start | bytes 786440 | tf_op jit(solution)/shard_map/ppermute | solution.py:250
  6.6 12.5 %collective-permute-start.2 = (f32[2,4,32,256]{3,2,1,0:T(8,128)S(1)}, f32[2,4,32,256]{3,2,1,0:T(8,128)S(1)}, u32[]{:S(2)}, u32[]{:S(2)}) collective-permute-start(f32[2,4,32,256]{3,2,1,0:T(8,128)S(1)} %get-tuple-element.26), channel_id=1, source_target_pairs={{0,6},{1,7},{2,4},{3,5},{4,2},{5,3},{6,0},{7,1},{8,14},{9,15},{10,... | collective-permute-start | bytes 786440 | tf_op jit(solution)/shard_map/ppermute | solution.py:250
  19.1 3.9 %copy-start = (s32[4,128,256]{2,1,0:T(8,128)S(1)}, s32[4,128,256]{2,1,0:T(8,128)}, u32[]{:S(2)}) copy-start(s32[4,128,256]{2,1,0:T(8,128)} %param.5) | copy-start | bytes 1572868
  19.2 9.8 %collective-permute-start.4 = (f32[2,2,4,32,256]{4,3,2,1,0:T(8,128)S(1)}, f32[2,2,4,32,256]{4,3,2,1,0:T(8,128)S(1)}, u32[]{:S(2)}, u32[]{:S(2)}) collective-permute-start(f32[2,2,4,32,256]{4,3,2,1,0:T(8,128)S(1)} %get-tuple-element.11), channel_id=1, source_target_pairs={{0,1},{1,0},{2,3},{3,2},{4,5},{5,4},{6,7},{7,6},{8,9},{9,8},{10,11... | collective-permute-start | bytes 1572872 | tf_op jit(solution)/shard_map/ppermute | solution.py:253
  19.2 11.8 %collective-permute-start.3 = (f32[2,4,32,256]{3,2,1,0:T(8,128)S(1)}, f32[2,4,32,256]{3,2,1,0:T(8,128)S(1)}, u32[]{:S(2)}, u32[]{:S(2)}) collective-permute-start(f32[2,4,32,256]{3,2,1,0:T(8,128)S(1)} %get-tuple-element.10), channel_id=1, source_target_pairs={{0,25},{1,8},{2,27},{3,10},{4,29},{5,12},{6,31},{7,14},{8,1},{9,16... | collective-permute-start | bytes 786440 | tf_op jit(solution)/shard_map/ppermute | solution.py:282
  23.2 8.9 %collective-permute-start.10 = (s32[2,4,32,256]{3,2,1,0:T(8,128)S(1)}, s32[2,4,32,256]{3,2,1,0:T(8,128)S(1)}, u32[]{:S(2)}, u32[]{:S(2)}) collective-permute-start(s32[2,4,32,256]{3,2,1,0:T(8,128)S(1)} %get-tuple-element.22), channel_id=1, source_target_pairs={{0,2},{2,0},{5,7},{7,5},{8,10},{10,8},{13,15},{15,13},{16,18},{18,... | collective-permute-start | bytes 786440 | tf_op jit(solution)/shard_map/ppermute | solution.py:271
  26.3 2.7 %copy-start.2 = (f32[8]{0:T(128)S(1)}, f32[8]{0:T(128)}, u32[]{:S(2)}) copy-start(f32[8]{0:T(128)} %param.7) | copy-start | bytes 100
  26.3 2.7 %copy-start.1 = (f32[3,8]{1,0:T(4,128)S(1)}, f32[3,8]{1,0:T(4,128)}, u32[]{:S(2)}) copy-start(f32[3,8]{1,0:T(4,128)} %param.6) | copy-start | bytes 292
  26.3 8.0 %collective-permute-start.11 = (s32[2,4,32,256]{3,2,1,0:T(8,128)S(1)}, s32[2,4,32,256]{3,2,1,0:T(8,128)S(1)}, u32[]{:S(2)}, u32[]{:S(2)}) collective-permute-start(s32[2,4,32,256]{3,2,1,0:T(8,128)S(1)} %get-tuple-element.23), channel_id=1, source_target_pairs={{0,4},{2,6},{5,1},{7,3},{8,12},{10,14},{13,9},{15,11},{16,20},{18,... | collective-permute-start | bytes 786440 | tf_op jit(solution)/shard_map/ppermute | solution.py:271
  27.6 6.7 %collective-permute-start.12 = (s32[2,4,32,256]{3,2,1,0:T(8,128)S(1)}, s32[2,4,32,256]{3,2,1,0:T(8,128)S(1)}, u32[]{:S(2)}, u32[]{:S(2)}) collective-permute-start(s32[2,4,32,256]{3,2,1,0:T(8,128)S(1)} %get-tuple-element.20), channel_id=1, source_target_pairs={{0,6},{2,4},{5,3},{7,1},{8,14},{10,12},{13,11},{15,9},{16,22},{18,... | collective-permute-start | bytes 786440 | tf_op jit(solution)/shard_map/ppermute | solution.py:271
  36.1 1.3 %collective-permute-start.13 = (f32[4,16,256]{2,1,0:T(8,128)S(1)}, f32[4,16,256]{2,1,0:T(8,128)S(1)}, u32[]{:S(2)}, u32[]{:S(2)}) collective-permute-start(f32[4,16,256]{2,1,0:T(8,128)S(1)} %get-tuple-element.16), channel_id=1, source_target_pairs={{0,1},{1,0},{2,3},{3,2},{4,5},{5,4},{6,7},{7,6},{8,9},{9,8},{10,11... | collective-permute-start | bytes 196616 | tf_op jit(solution)/shard_map/ppermute | solution.py:253
  37.4 6.9 %collective-permute-start.14 = (f32[4,16,256]{2,1,0:T(8,128)S(1)}, f32[4,16,256]{2,1,0:T(8,128)S(1)}, u32[]{:S(2)}, u32[]{:S(2)}) collective-permute-start(f32[4,16,256]{2,1,0:T(8,128)S(1)} %pad_maximum_fusion.1), channel_id=1, source_target_pairs={{0,24},{8,16},{16,8},{24,0},{1,25},{9,17},{17,9},{25,1},{2,26},{10... | collective-permute-start | bytes 196616 | tf_op jit(solution)/shard_map/ppermute | solution.py:321
  38.3 7.6 %collective-permute-start.15 = (f32[4,16,256]{2,1,0:T(8,128)S(1)}, f32[4,16,256]{2,1,0:T(8,128)S(1)}, u32[]{:S(2)}, u32[]{:S(2)}) collective-permute-start(f32[4,16,256]{2,1,0:T(8,128)S(1)} %pad_maximum_fusion.1), channel_id=1, source_target_pairs={{0,16},{8,24},{16,0},{24,8},{1,17},{9,25},{17,1},{25,9},{2,18},{10... | collective-permute-start | bytes 196616 | tf_op jit(solution)/shard_map/ppermute | solution.py:321
  38.4 7.5 %collective-permute-start.16 = (f32[4,16,256]{2,1,0:T(8,128)S(1)}, f32[4,16,256]{2,1,0:T(8,128)S(1)}, u32[]{:S(2)}, u32[]{:S(2)}) collective-permute-start(f32[4,16,256]{2,1,0:T(8,128)S(1)} %pad_maximum_fusion.1), channel_id=1, source_target_pairs={{0,8},{8,0},{16,24},{24,16},{1,9},{9,1},{17,25},{25,17},{2,10},{10... | collective-permute-start | bytes 196616 | tf_op jit(solution)/shard_map/ppermute | solution.py:321
  41.9 4.0 %collective-permute-start.5 = (f32[2,4,32,256]{3,2,1,0:T(8,128)S(1)}, f32[2,4,32,256]{3,2,1,0:T(8,128)S(1)}, u32[]{:S(2)}, u32[]{:S(2)}) collective-permute-start(f32[2,4,32,256]{3,2,1,0:T(8,128)S(1)} %get-tuple-element.15.refs_6_), channel_id=1, source_target_pairs={{0,1},{1,0},{2,3},{3,2},{4,5},{5,4},{6,7},{7,6},{8,9},{9,8},{10,11... | collective-permute-start | bytes 786440 | tf_op jit(solution)/shard_map/ppermute | solution.py:253
  46.0 6.4 %collective-permute-start.6 = (f32[4,32,256]{2,1,0:T(8,128)S(1)}, f32[4,32,256]{2,1,0:T(8,128)S(1)}, u32[]{:S(2)}, u32[]{:S(2)}) collective-permute-start(f32[4,32,256]{2,1,0:T(8,128)S(1)} %get-tuple-element.34), channel_id=1, source_target_pairs={{0,6},{1,7},{2,4},{3,5},{4,2},{5,3},{6,0},{7,1},{8,14},{9,15},{10,... | collective-permute-start | bytes 393224 | tf_op jit(solution)/shard_map/ppermute | solution.py:250
  48.8 5.8 %collective-permute-start.7 = (f32[4,32,256]{2,1,0:T(8,128)S(1)}, f32[4,32,256]{2,1,0:T(8,128)S(1)}, u32[]{:S(2)}, u32[]{:S(2)}) collective-permute-start(f32[4,32,256]{2,1,0:T(8,128)S(1)} %get-tuple-element.35), channel_id=1, source_target_pairs={{0,4},{1,5},{2,6},{3,7},{4,0},{5,1},{6,2},{7,3},{8,12},{9,13},{10,... | collective-permute-start | bytes 393224 | tf_op jit(solution)/shard_map/ppermute | solution.py:250
  48.8 6.7 %collective-permute-start.8 = (f32[4,32,256]{2,1,0:T(8,128)S(1)}, f32[4,32,256]{2,1,0:T(8,128)S(1)}, u32[]{:S(2)}, u32[]{:S(2)}) collective-permute-start(f32[4,32,256]{2,1,0:T(8,128)S(1)} %get-tuple-element.33), channel_id=1, source_target_pairs={{0,2},{1,3},{2,0},{3,1},{4,6},{5,7},{6,4},{7,5},{8,10},{9,11},{10,... | collective-permute-start | bytes 393224 | tf_op jit(solution)/shard_map/ppermute | solution.py:250

commit v5 on v3

--- a/solution.py
+++ b/solution.py
@@ -103,21 +103,20 @@
 
 
 def inner_kernel(chips, *refs):
-    own, own_kind = refs[:chips], refs[chips : 2 * chips]
-    other, other_kind, table, dense, image, edge, edge_kind, fluid, kind = refs[2 * chips :]
+    own, kinds = refs[:chips], refs[chips : 2 * chips]
+    other, table, dense, image, edge, edge_kind, fluid, kind = refs[2 * chips :]
     member = lax.axis_index("swap")
     chip, upper = member // 2, member % 2
     half = chips // 2
     _, layers, rows, columns = own[0].shape
-    shift = upper
     for d in range(chips):
         k = chip ^ d
 
         @pl.when(k // half == upper)
         def _():
-            at = 2 * (k - upper * half) + upper
-            fluid[:, pl.ds((at + shift) * layers, layers)] = own[d][...]
-            kind[pl.ds(at * layers, layers)] = own_kind[d][...]
+            at = 2 * (k - upper * half)
+            fluid[:, pl.ds((at + 2 * upper) * layers, layers)] = own[d][...]
+            kind[pl.ds(at * layers, 2 * layers)] = kinds[d][...].reshape(2 * layers, rows, columns)
 
         @pl.when(k == jnp.where(upper == 1, half - 1, half))
         def _():
@@ -125,9 +124,7 @@
             fluid[:, pl.ds(at * layers, layers)] = own[d][...]
 
     for i in range(half):
-        at = 2 * i + 1 - upper
-        fluid[:, pl.ds((at + shift) * layers, layers)] = other[i]
-        kind[pl.ds(at * layers, layers)] = other_kind[i]
+        fluid[:, pl.ds((2 * i + 1) * layers, layers)] = other[i]
 
     total = (chips + 1) * layers
     sign = jnp.where(upper == 1, 1.0, -1.0)
@@ -146,7 +143,6 @@
     sweep_tiles(rows, columns, layers, chips + 1, upper == 0, load, place, dense, place, kind, table, finish)
     start = jnp.where(upper == 1, chips - 1, 0) * layers
     edge[...] = fluid[:, pl.ds(start, 2 * layers)]
-    start = jnp.where(upper == 1, chips - 1, 0) * layers
     edge_kind[...] = kind[pl.ds(start, layers)]
 
 
@@ -193,8 +189,8 @@
         give[half * layers + n // 2, (n % 2) * short : (n % 2 + 1) * short] = given
 
 
-def route_kernel(chips, with_far, *refs):
-    own, given = refs[:chips], refs[chips]
+def route_kernel(chips, *refs):
+    own, (other, outer) = refs[:chips], refs[chips:]
     member = lax.axis_index("swap")
     chip, upper = member // 2, member % 2
     half = chips // 2
@@ -203,79 +199,23 @@
 
         @pl.when(k // half != upper)
         def _():
-            given[k - (1 - upper) * half] = own[d][...]
-
-        if with_far:
-
-            @pl.when(k == upper * (chips - 1))
-            def _():
-                refs[chips + 1][...] = own[d][...]
-
-
-def route(blocks, with_far):
-    chips = len(blocks)
-    shape, dtype = blocks[0].shape, blocks[0].dtype
-    shapes = [jax.ShapeDtypeStruct((chips // 2, *shape), dtype)] + [jax.ShapeDtypeStruct(shape, dtype)] * with_far
+            other[k - (1 - upper) * half] = own[d][...]
+
+        @pl.when(k == upper * (chips - 1))
+        def _():
+            outer[...] = own[d][...]
+
+
+def call(kernel, operands, outs, scratch=(), cells=0):
     return pl.pallas_call(
-        functools.partial(route_kernel, chips, with_far),
-        out_shape=shapes,
-        in_specs=[VMEM] * chips,
-        out_specs=[VMEM] * len(shapes),
+        kernel,
+        out_shape=[jax.ShapeDtypeStruct(shape, dtype) for shape, dtype in outs],
+        in_specs=[VMEM] * len(operands),
+        out_specs=[VMEM] * len(outs),
+        scratch_shapes=[pltpu.VMEM(shape, dtype) for shape, dtype in scratch],
         compiler_params=pltpu.CompilerParams(vmem_limit_bytes=GRANT),
-        cost_estimate=pl.CostEstimate(flops=1000, bytes_accessed=1 << 20, transcendentals=0),
-        name="route",
-    )(*blocks)
-
-
-def cost(cells):
-    return pl.CostEstimate(flops=300 * cells, bytes_accessed=16 * cells, transcendentals=6 * cells)
-
-
-def sweep_inner(own, own_kind, other, other_kind, table):
-    chips = len(own)
-    _, layers, rows, columns = own[0].shape
-    shape = lambda *dims, dtype=F32: jax.ShapeDtypeStruct((*dims, rows, columns), dtype)
-    return pl.pallas_call(
-        functools.partial(inner_kernel, chips),
-        out_shape=[
-            shape(chips * layers),
-            shape(4),
-            shape(2, 2 * layers),
-            shape(layers, dtype=jnp.int32),
-        ],
-        in_specs=[VMEM] * (2 * chips + 3),
-        out_specs=[VMEM] * 4,
-        scratch_shapes=[
-            pltpu.VMEM((2, (chips + 1) * layers, rows, columns), F32),
-            pltpu.VMEM((chips * layers, rows, columns), jnp.int32),
-        ],
-        cost_estimate=cost(chips * layers * rows * columns),
-        compiler_params=pltpu.CompilerParams(vmem_limit_bytes=GRANT),
-        name="sweep_inner",
-    )(*own, *own_kind, other, other_kind, table)
-
-
-def sweep_outer(far, edge, edge_kind, table, dense, image):
-    layers, rows, columns = edge_kind.shape
-    half = dense.shape[0] // layers // 2
-    shape = lambda *dims: jax.ShapeDtypeStruct(dims, F32)
-    return pl.pallas_call(
-        functools.partial(outer_kernel, 2 * half),
-        out_shape=[
-            shape(half, layers, rows, columns),
-            shape(half * layers + 2, rows, columns),
-            shape(4, rows // 2, columns),
-        ],
-        in_specs=[VMEM] * 6,
-        out_specs=[VMEM] * 3,
-        scratch_shapes=[
-            pltpu.VMEM((layers, rows, columns), F32),
-            pltpu.VMEM((4, rows, columns), F32),
-        ],
-        cost_estimate=cost(layers * rows * columns),
-        compiler_params=pltpu.CompilerParams(vmem_limit_bytes=GRANT),
-        name="sweep_outer",
-    )(far, edge, edge_kind, table, dense, image)
+        cost_estimate=pl.CostEstimate(flops=300 * cells, bytes_accessed=16 * cells, transcendentals=6 * cells),
+    )(*operands)
 
 
 def over(nearer, farther):
@@ -306,11 +246,22 @@
     table = jnp.pad(table, ((0, 0), (0, LANES - table.shape[1])))
     table = jnp.broadcast_to(table[:, None, :], (4, 8, LANES))
 
-    sent = [lax.dynamic_slice_in_dim(fluid_state, (chip ^ d) * rows, rows, axis=2) for d in range(chips)]
-    own = [to_chip(sent[d], d) for d in range(chips)]
-    own_kind = [to_chip(lax.dynamic_slice_in_dim(material, (chip ^ d) * rows, rows, axis=1), d) for d in range(chips)]
-    other, outer = route(own, True)
-    *own_kind, table, _ = lax.optimization_barrier((*own_kind, table, outer))
+    def cut(array, j, axis):
+        return lax.dynamic_slice_in_dim(array, j * rows, rows, axis=axis)
+
+    own = [to_chip(cut(fluid_state, chip ^ d, 2), d) for d in range(chips)]
+
+    theirs = to_core(material)
+    both = jnp.stack([jnp.where(upper == 1, theirs, material), jnp.where(upper == 1, material, theirs)])
+    kinds = [cut(both, chip, 2)]
+    for d in range(1, chips):
+        pairs = [(2 * k, 2 * (k ^ d) + k // half) for k in range(chips)]
+        kinds.append(lax.ppermute(cut(both, chip ^ d, 2), "swap", pairs))
+
+    block = (layers, rows, width)
+    cells = layers * rows * width
+    other, outer = call(functools.partial(route_kernel, chips), own, [((half, 2, *block), F32), ((2, *block), F32)])
+    *kinds, _ = lax.optimization_barrier((*kinds, outer))
     other = to_core(other)
     ring = []
     for z in range(slabs):
@@ -318,10 +269,22 @@
             to = ((z + 1) % slabs, w - 1) if w % 2 else ((z - 1) % slabs, w + 1)
             ring.append((z * members + w, to[0] * members + to[1]))
     far = lax.ppermute(outer, ("slab", "swap"), ring)
-    other_kind = to_core(route(own_kind, False)[0])
-
-    dense, image, edge, edge_kind = sweep_inner(own, own_kind, other, other_kind, table)
-    keep, give, tile = sweep_outer(far, edge, edge_kind, table, dense, image)
+
+    deep = (chips * layers, rows, width)
+    dense, image, edge, edge_kind = call(
+        functools.partial(inner_kernel, chips),
+        [*own, *kinds, other, table],
+        [(deep, F32), ((4, rows, width), F32), ((2, 2 * layers, rows, width), F32), (block, jnp.int32)],
+        [((2, (chips + 1) * layers, rows, width), F32), (deep, jnp.int32)],
+        chips * cells,
+    )
+    keep, give, tile = call(
+        functools.partial(outer_kernel, chips),
+        [far, edge, edge_kind, table, dense, image],
+        [((half, *block), F32), ((half * layers + 2, rows, width), F32), ((4, rows // 2, width), F32)],
+        [(block, F32), ((4, rows, width), F32)],
+        cells,
+    )
     got = to_core(give)
 
     kept = [keep[i] for i in range(half)]
@@ -329,18 +292,17 @@
     chunks = []
     for d in range(chips):
         k = chip ^ d
-        block = jnp.where(k // half == upper, pick(kept, k % half), pick(gotten, k % half))
-        chunks.append(to_chip(block, d))
+        back = jnp.where(k // half == upper, pick(kept, k % half), pick(gotten, k % half))
+        chunks.append(to_chip(back, d))
     density = jnp.concatenate([pick(chunks, chip ^ j) for j in range(chips)], axis=1)
 
     partner = got[half * layers :].reshape(4, rows // 2, width)
     tile = over(jnp.where(upper == 1, partner, tile), jnp.where(upper == 1, tile, partner))
-    pieces = [tile]
-    for away in range(1, slabs):
-        pieces.append(lax.ppermute(tile, "slab", swap_pairs(slabs, away)))
-    ordered = [pick(pieces, slab ^ z) for z in range(slabs)]
-    rendered = functools.reduce(over, ordered)
-    rendered = jnp.concatenate([rendered[:3], 1.0 - rendered[3:4]], axis=0).reshape(4, height * width // members)
+    for bit in range(slabs.bit_length() - 1):
+        partner = lax.ppermute(tile, "slab", swap_pairs(slabs, 1 << bit))
+        behind = slab >> bit & 1
+        tile = over(jnp.where(behind == 1, partner, tile), jnp.where(behind == 1, tile, partner))
+    rendered = jnp.concatenate([tile[:3], 1.0 - tile[3:4]], axis=0).reshape(4, height * width // members)
     return density, rendered
 
 

time: 51.2 us -> 52.5 us (1.025)
  waiting for transfers between devices: 19.5 us -> 22 us
  local copies, waits for them, and re-layouts: 2.66 us -> 1.96 us
  starting transfers between devices: 23 us -> 22.4 us
    ppermute x9 -> x6, starting transfers between devices: 14.6 us -> 8.22 us  [to_chip(): return lax.ppermute(block, 'swap', swap_pairs(members, 2 * d))]
    ppermute x3 -> x5, starting transfers between devices: 4.45 us -> 8.59 us  [the longest x3 6.64 us: per_device(): kinds.append(lax.ppermute(cut(both, chip ^ d, 2), 'swap', pairs))]
    ppermute x1, waiting for transfers between devices: 3.82 us -> 0.01 us  [per_device(): far = lax.ppermute(outer, ('slab', 'swap'), ring)]
    ppermute x9 -> x6, waiting for transfers between devices: 13.5 us -> 16.9 us  [to_chip(): return lax.ppermute(block, 'swap', swap_pairs(members, 2 * d))]
    ppermute x3 -> x5, waiting for transfers between devices: 0.75 us -> 3.81 us  [the longest x3 3.81 us: per_device(): kinds.append(lax.ppermute(cut(both, chip ^ d, 2), 'swap', pairs))]
    ppermute x3, starting transfers between devices: 0.21 us -> 1.92 us  [to_core(): return lax.ppermute(block, 'swap', swap_pairs(members, 1))]
    unnamed x7, local copies, waits for them, and re-layouts: 1.27 us -> 0.69 us
    dynamic_slice x2 -> x1, local copies, waits for them, and re-layouts: 1.38 us -> 1.26 us  [cut(): return lax.dynamic_slice_in_dim(array, j * rows, rows, axis=axis)]
  transfers between devices with their start and end apart: 16 -> 15, of which waited for: 9 -> 9; matrix products, arithmetic and copies ran while one was open for 2% -> 5% of each run, Pallas kernels for 5% -> 5%
where the time goes in v5:
time: 52.5 us; the launch traced here: 52.3 us
  starting transfers between devices  22.4 us (43%)
  waiting for transfers between devices  22 us (42%)
  Pallas kernels  3.65 us (7%)
  local copies, waits for them, and re-layouts  1.96 us (4%)
  other arithmetic  1.32 us (3%)
  between operations  0.87 us (2%)
    ppermute x6, waiting for transfers between devices, to_chip(): return lax.ppermute(block, 'swap', swap_pairs(members, 2 * d))  16.9 us
    ppermute x6, starting transfers between devices, to_chip(): return lax.ppermute(block, 'swap', swap_pairs(members, 2 * d))  8.22 us
    ppermute x3, starting transfers between devices, per_device(): kinds.append(lax.ppermute(cut(both, chip ^ d, 2), 'swap', pairs))  6.64 us
    ppermute x3, waiting for transfers between devices, per_device(): kinds.append(lax.ppermute(cut(both, chip ^ d, 2), 'swap', pairs))  3.81 us
    ppermute x1, starting transfers between devices, per_device(): far = lax.ppermute(outer, ('slab', 'swap'), ring)  3.7 us
    pallas_call x3, Pallas kernels, call(): pl.pallas_call(kernel, out_shape=[jax.ShapeDtypeStruct(shape, dtype) for...  3.65 us
    ppermute x2, starting transfers between devices, per_device(): partner = lax.ppermute(tile, 'slab', swap_pairs(slabs, 1 << bit))  1.95 us
    ppermute x3, starting transfers between devices, to_core(): return lax.ppermute(block, 'swap', swap_pairs(members, 1))  1.92 us
  transfers between devices with their start and end apart: 15, of which 9 were waited for; matrix products, arithmetic and copies ran while one was open for 5% of the time, Pallas kernels for 5%

profile of v5, /device:TPU:0, one launch (start us, length us, event | category | flops | bytes accessed | tf_op | source)
XLA Modules:
  0.0 52.3 jit_solution(5824103874414023970)
XLA Ops:
  0.6 0.6 %collective-permute-start.4 = (s32[4,128,256]{2,1,0:T(8,128)}, s32[4,128,256]{2,1,0:T(8,128)S(1)}, u32[]{:S(2)}, u32[]{:S(2)}) collective-permute-start(s32[4,128,256]{2,1,0:T(8,128)} %param.5), channel_id=1, source_target_pairs={{0,1},{1,0},{2,3},{3,2},{4,5},{5,4},{6,7},{7,6},{8,9},{9,8},{10,11... | collective-permute-start | bytes 1572872 | tf_op jit(solution)/shard_map/ppermute | solution.py:242
  1.2 1.3 %constant_dynamic-slice_fusion = (f32[2,4,32,256]{3,2,1,0:T(8,128)S(1)}, f32[2,4,32,256]{3,2,1,0:T(8,128)S(1)}, f32[2,4,32,256]{3,2,1,0:T(8,128)S(1)}, f32[2,4,32,256]{3,2,1,0:T(8,128)S(1)}) fusion(f32[2,4,128,256]{3,2,1,0:T(8,128)} %param.4, s32[]{:T(128)S(6)} %select_n.275, s32[]{:T(128)S(6)} %select_n.273, s32[]{:T(128)S(6)} %select_n.272, s32[]{:T(128)S(6)} %select_n.274), kind=kLoop, calls=%fused_computation.45 | loop fusion | bytes 2097168 | tf_op jit(solution)/shard_map/dynamic_slice | solution.py:250
  2.5 2.6 %collective-permute-start = (f32[2,4,32,256]{3,2,1,0:T(8,128)S(1)}, f32[2,4,32,256]{3,2,1,0:T(8,128)S(1)}, u32[]{:S(2)}, u32[]{:S(2)}) collective-permute-start(f32[2,4,32,256]{3,2,1,0:T(8,128)S(1)} %get-tuple-element.37), channel_id=1, source_target_pairs={{0,2},{1,3},{2,0},{3,1},{4,6},{5,7},{6,4},{7,5},{8,10},{9,11},{10,... | collective-permute-start | bytes 786440 | tf_op jit(solution)/shard_map/ppermute | solution.py:239
  5.1 1.5 %collective-permute-start.1 = (f32[2,4,32,256]{3,2,1,0:T(8,128)S(1)}, f32[2,4,32,256]{3,2,1,0:T(8,128)S(1)}, u32[]{:S(2)}, u32[]{:S(2)}) collective-permute-start(f32[2,4,32,256]{3,2,1,0:T(8,128)S(1)} %get-tuple-element.39), channel_id=1, source_target_pairs={{0,4},{1,5},{2,6},{3,7},{4,0},{5,1},{6,2},{7,3},{8,12},{9,13},{10,... | collective-permute-start | bytes 786440 | tf_op jit(solution)/shard_map/ppermute | solution.py:239
  6.6 0.0 collective-permute-start.2
  6.6 5.6 %collective-permute-done.refs_1_ = f32[2,4,32,256]{3,2,1,0:T(8,128)S(1)} collective-permute-done((f32[2,4,32,256]{3,2,1,0:T(8,128)S(1)}, f32[2,4,32,256]{3,2,1,0:T(8,128)S(1)}, u32[]{:S(2)}, u32[]{:S(2)}) %collective-permute-start) | collective-permute-done | bytes 262176 | tf_op jit(solution)/shard_map/ppermute | solution.py:239
  12.2 6.8 %collective-permute-done.1.refs_2_ = f32[2,4,32,256]{3,2,1,0:T(8,128)S(1)} collective-permute-done((f32[2,4,32,256]{3,2,1,0:T(8,128)S(1)}, f32[2,4,32,256]{3,2,1,0:T(8,128)S(1)}, u32[]{:S(2)}, u32[]{:S(2)}) %collective-permute-start.1) | collective-permute-done | bytes 262176 | tf_op jit(solution)/shard_map/ppermute | solution.py:239
  19.1 0.0 collective-permute-done.2.refs_3_
  19.1 0.0 copy-start
  19.1 0.1 shard_map.59
  19.2 0.1 collective-permute-start.8
  19.2 3.7 %collective-permute-start.3 = (f32[2,4,32,256]{3,2,1,0:T(8,128)S(1)}, f32[2,4,32,256]{3,2,1,0:T(8,128)S(1)}, u32[]{:S(2)}, u32[]{:S(2)}) collective-permute-start(f32[2,4,32,256]{3,2,1,0:T(8,128)S(1)} %get-tuple-element.15), channel_id=1, source_target_pairs={{0,25},{1,8},{2,27},{3,10},{4,29},{5,12},{6,31},{7,14},{8,1},{9,16... | collective-permute-start | bytes 786440 | tf_op jit(solution)/shard_map/ppermute | solution.py:271
  22.9 0.0 collective-permute-done.4
  23.0 0.0 copy-done
  23.0 0.1 select_bitcast_fusion
  23.1 0.1 fusion
  23.2 3.1 %collective-permute-start.5 = (s32[2,4,32,256]{3,2,1,0:T(8,128)S(1)}, s32[2,4,32,256]{3,2,1,0:T(8,128)S(1)}, u32[]{:S(2)}, u32[]{:S(2)}) collective-permute-start(s32[2,4,32,256]{3,2,1,0:T(8,128)S(1)} %get-tuple-element.32), channel_id=1, source_target_pairs={{0,2},{2,0},{4,7},{6,5},{8,10},{10,8},{12,15},{14,13},{16,18},{18,... | collective-permute-start | bytes 786440 | tf_op jit(solution)/shard_map/ppermute | solution.py:259
  26.3 0.0 copy-start.2
  26.3 0.0 copy-start.1
  26.3 1.6 %collective-permute-start.6 = (s32[2,4,32,256]{3,2,1,0:T(8,128)S(1)}, s32[2,4,32,256]{3,2,1,0:T(8,128)S(1)}, u32[]{:S(2)}, u32[]{:S(2)}) collective-permute-start(s32[2,4,32,256]{3,2,1,0:T(8,128)S(1)} %get-tuple-element.33), channel_id=1, source_target_pairs={{0,4},{2,6},{4,1},{6,3},{8,12},{10,14},{12,9},{14,11},{16,20},{18,... | collective-permute-start | bytes 786440 | tf_op jit(solution)/shard_map/ppermute | solution.py:259
  27.9 1.9 %collective-permute-start.7 = (s32[2,4,32,256]{3,2,1,0:T(8,128)S(1)}, s32[2,4,32,256]{3,2,1,0:T(8,128)S(1)}, u32[]{:S(2)}, u32[]{:S(2)}) collective-permute-start(s32[2,4,32,256]{3,2,1,0:T(8,128)S(1)} %get-tuple-element.30), channel_id=1, source_target_pairs={{0,6},{2,4},{4,3},{6,1},{8,14},{10,12},{12,11},{14,9},{16,22},{18,... | collective-permute-start | bytes 786440 | tf_op jit(solution)/shard_map/ppermute | solution.py:259
  29.8 0.0 copy-done.2
  29.9 0.0 copy-done.1
  29.9 1.5 %collective-permute-done.5.refs_5_ = s32[2,4,32,256]{3,2,1,0:T(8,128)S(1)} collective-permute-done((s32[2,4,32,256]{3,2,1,0:T(8,128)S(1)}, s32[2,4,32,256]{3,2,1,0:T(8,128)S(1)}, u32[]{:S(2)}, u32[]{:S(2)}) %collective-permute-start.5) | collective-permute-done | bytes 262176 | tf_op jit(solution)/shard_map/ppermute | solution.py:259
  31.4 0.4 collective-permute-done.6.refs_6_
  31.8 1.9 %collective-permute-done.7.refs_7_ = s32[2,4,32,256]{3,2,1,0:T(8,128)S(1)} collective-permute-done((s32[2,4,32,256]{3,2,1,0:T(8,128)S(1)}, s32[2,4,32,256]{3,2,1,0:T(8,128)S(1)}, u32[]{:S(2)}, u32[]{:S(2)}) %collective-permute-start.7) | collective-permute-done | bytes 262176 | tf_op jit(solution)/shard_map/ppermute | solution.py:259
  33.7 0.0 collective-permute-done.8.refs_8_
  33.7 2.3 %shard_map.60 = (f32[16,32,256]{2,1,0:T(8,128)S(1)}, f32[4,32,256]{2,1,0:T(8,128)S(1)}, f32[2,8,32,256]{3,2,1,0:T(8,128)S(1)}, s32[4,32,256]{2,1,0:T(8,128)S(1)}) custom-call(f32[2,4,32,256]{3,2,1,0:T(8,128)S(1)} %get-tuple-element.38.refs_0_, f32[2,4,32,256]{3,2,1,0:T(8,128)S(1)} %collective-permute-done.refs_1_, ...), custom_call_target="tpu_custom_call" | custom-call | flops 39321600 | bytes 2097152 | tf_op jit(solution)/shard_map/pallas_call | solution.py:210
  36.0 0.0 collective-permute-done.3.far
  36.0 1.3 %shard_map.61 = (f32[2,4,32,256]{3,2,1,0:T(8,128)S(1)}, f32[10,32,256]{2,1,0:T(8,128)S(1)}, f32[4,16,256]{2,1,0:T(8,128)S(1)}) custom-call(f32[2,4,32,256]{3,2,1,0:T(8,128)S(1)} %collective-permute-done.3.far, f32[2,8,32,256]{3,2,1,0:T(8,128)S(1)} %get-tuple-element.21.edge, s32[4,32,256]{2,1,0:T(8,128)S(1)} %get-tuple-element.22.edge_kind, ...), custom_call_target="tpu_custom_call" | custom-call | flops 9830400 | bytes 524288 | tf_op jit(solution)/shard_map/pallas_call | solution.py:210
  37.3 1.3 %collective-permute-start.9 = (f32[10,32,256]{2,1,0:T(8,128)S(1)}, f32[10,32,256]{2,1,0:T(8,128)S(1)}, u32[]{:S(2)}, u32[]{:S(2)}) collective-permute-start(f32[10,32,256]{2,1,0:T(8,128)S(1)} %get-tuple-element.26), channel_id=1, source_target_pairs={{0,1},{1,0},{2,3},{3,2},{4,5},{5,4},{6,7},{7,6},{8,9},{9,8},{10,11... | collective-permute-start | bytes 983048 | tf_op jit(solution)/shard_map/ppermute | solution.py:242
  38.6 1.3 %collective-permute-done.9 = f32[10,32,256]{2,1,0:T(8,128)S(1)} collective-permute-done((f32[10,32,256]{2,1,0:T(8,128)S(1)}, f32[10,32,256]{2,1,0:T(8,128)S(1)}, u32[]{:S(2)}, u32[]{:S(2)}) %collective-permute-start.9) | collective-permute-done | bytes 327712 | tf_op jit(solution)/shard_map/ppermute | solution.py:242
  39.9 0.6 %collective-permute-start.13 = (f32[4,16,256]{2,1,0:T(8,128)S(1)}, f32[4,16,256]{2,1,0:T(8,128)S(1)}, u32[]{:S(2)}, u32[]{:S(2)}) collective-permute-start(f32[4,16,256]{2,1,0:T(8,128)S(1)} %pad_maximum_fusion.1), channel_id=1, source_target_pairs={{0,8},{8,0},{16,24},{24,16},{1,9},{9,1},{17,25},{25,17},{2,10},{10... | collective-permute-start | bytes 196616 | tf_op jit(solution)/shard_map/ppermute | solution.py:302
  40.5 3.4 %collective-permute-start.10 = (f32[4,32,256]{2,1,0:T(8,128)S(1)}, f32[4,32,256]{2,1,0:T(8,128)S(1)}, u32[]{:S(2)}, u32[]{:S(2)}) collective-permute-start(f32[4,32,256]{2,1,0:T(8,128)S(1)} %get-tuple-element.41), channel_id=1, source_target_pairs={{0,6},{1,7},{2,4},{3,5},{4,2},{5,3},{6,0},{7,1},{8,14},{9,15},{10,... | collective-permute-start | bytes 393224 | tf_op jit(solution)/shard_map/ppermute | solution.py:239
  43.9 0.0 collective-permute-start.11
  43.9 0.6 %collective-permute-start.12 = (f32[4,32,256]{2,1,0:T(8,128)S(1)}, f32[4,32,256]{2,1,0:T(8,128)S(1)}, u32[]{:S(2)}, u32[]{:S(2)}) collective-permute-start(f32[4,32,256]{2,1,0:T(8,128)S(1)} %get-tuple-element.40), channel_id=1, source_target_pairs={{0,2},{1,3},{2,0},{3,1},{4,6},{5,7},{6,4},{7,5},{8,10},{9,11},{10,... | collective-permute-start | bytes 393224 | tf_op jit(solution)/shard_map/ppermute | solution.py:239
  44.6 0.0 collective-permute-done.13
  44.6 1.4 %collective-permute-start.14 = (f32[4,16,256]{2,1,0:T(8,128)S(1)}, f32[4,16,256]{2,1,0:T(8,128)S(1)}, u32[]{:S(2)}, u32[]{:S(2)}) collective-permute-start(f32[4,16,256]{2,1,0:T(8,128)S(1)} %pad_maximum_fusion.2), channel_id=1, source_target_pairs={{0,16},{8,24},{16,0},{24,8},{1,17},{9,25},{17,1},{25,9},{2,18},{10... | collective-permute-start | bytes 196616 | tf_op jit(solution)/shard_map/ppermute | solution.py:302
  46.0 1.8 %collective-permute-done.10 = f32[4,32,256]{2,1,0:T(8,128)S(1)} collective-permute-done((f32[4,32,256]{2,1,0:T(8,128)S(1)}, f32[4,32,256]{2,1,0:T(8,128)S(1)}, u32[]{:S(2)}, u32[]{:S(2)}) %collective-permute-start.10) | collective-permute-done | bytes 131104 | tf_op jit(solution)/shard_map/ppermute | solution.py:239
  47.8 2.4 %collective-permute-done.11 = f32[4,32,256]{2,1,0:T(8,128)S(1)} collective-permute-done((f32[4,32,256]{2,1,0:T(8,128)S(1)}, f32[4,32,256]{2,1,0:T(8,128)S(1)}, u32[]{:S(2)}, u32[]{:S(2)}) %collective-permute-start.11) | collective-permute-done | bytes 131104 | tf_op jit(solution)/shard_map/ppermute | solution.py:239
  50.3 0.3 collective-permute-done.12
  50.5 0.1 select_select_fusion.3
  50.6 0.1 select_select_fusion.2
  50.7 0.8 %pad_maximum_fusion = f32[4,128,256]{2,1,0:T(8,128)} fusion(f32[4,32,256]{2,1,0:T(8,128)S(1)} %get-tuple-element.44, f32[4,32,256]{2,1,0:T(8,128)S(1)} %get-tuple-element.45, f32[4,32,256]{2,1,0:T(8,128)S(1)} %get-tuple-element.43, f32[4,32,256]{2,1,0:T(8,128)S(1)} %get-tuple-element.28), kind=kLoop, calls=%fused_computation.8 | loop fusion | flops 393216 | bytes 1048576 | tf_op jit(solution)/shard_map/concatenate | solution.py:297
  51.5 0.0 collective-permute-done.14
  51.6 0.7 %copy.6 = f32[1,4,16,256]{3,1,2,0:T(4,128)} copy(f32[1,4,16,256]{3,2,1,0:T(8,128)S(1)} %maximum_bitcast_fusion) | data formatting | bytes 131072
  (17 shorter events, 0.2 us)
Async XLA Ops:
  0.6 22.3 %collective-permute-start.4 = (s32[4,128,256]{2,1,0:T(8,128)}, s32[4,128,256]{2,1,0:T(8,128)S(1)}, u32[]{:S(2)}, u32[]{:S(2)}) collective-permute-start(s32[4,128,256]{2,1,0:T(8,128)} %param.5), channel_id=1, source_target_pairs={{0,1},{1,0},{2,3},{3,2},{4,5},{5,4},{6,7},{7,6},{8,9},{9,8},{10,11... | collective-permute-start | bytes 1572872 | tf_op jit(solution)/shard_map/ppermute | solution.py:242
  2.5 9.8 %collective-permute-start = (f32[2,4,32,256]{3,2,1,0:T(8,128)S(1)}, f32[2,4,32,256]{3,2,1,0:T(8,128)S(1)}, u32[]{:S(2)}, u32[]{:S(2)}) collective-permute-start(f32[2,4,32,256]{3,2,1,0:T(8,128)S(1)} %get-tuple-element.37), channel_id=1, source_target_pairs={{0,2},{1,3},{2,0},{3,1},{4,6},{5,7},{6,4},{7,5},{8,10},{9,11},{10,... | collective-permute-start | bytes 786440 | tf_op jit(solution)/shard_map/ppermute | solution.py:239
  5.1 14.0 %collective-permute-start.1 = (f32[2,4,32,256]{3,2,1,0:T(8,128)S(1)}, f32[2,4,32,256]{3,2,1,0:T(8,128)S(1)}, u32[]{:S(2)}, u32[]{:S(2)}) collective-permute-start(f32[2,4,32,256]{3,2,1,0:T(8,128)S(1)} %get-tuple-element.39), channel_id=1, source_target_pairs={{0,4},{1,5},{2,6},{3,7},{4,0},{5,1},{6,2},{7,3},{8,12},{9,13},{10,... | collective-permute-start | bytes 786440 | tf_op jit(solution)/shard_map/ppermute | solution.py:239
  6.6 12.5 %collective-permute-start.2 = (f32[2,4,32,256]{3,2,1,0:T(8,128)S(1)}, f32[2,4,32,256]{3,2,1,0:T(8,128)S(1)}, u32[]{:S(2)}, u32[]{:S(2)}) collective-permute-start(f32[2,4,32,256]{3,2,1,0:T(8,128)S(1)} %get-tuple-element.36), channel_id=1, source_target_pairs={{0,6},{1,7},{2,4},{3,5},{4,2},{5,3},{6,0},{7,1},{8,14},{9,15},{10,... | collective-permute-start | bytes 786440 | tf_op jit(solution)/shard_map/ppermute | solution.py:239
  19.1 3.9 %copy-start = (s32[4,128,256]{2,1,0:T(8,128)S(1)}, s32[4,128,256]{2,1,0:T(8,128)}, u32[]{:S(2)}) copy-start(s32[4,128,256]{2,1,0:T(8,128)} %param.5) | copy-start | bytes 1572868
  19.2 14.5 %collective-permute-start.8 = (f32[2,2,4,32,256]{4,3,2,1,0:T(8,128)S(1)}, f32[2,2,4,32,256]{4,3,2,1,0:T(8,128)S(1)}, u32[]{:S(2)}, u32[]{:S(2)}) collective-permute-start(f32[2,2,4,32,256]{4,3,2,1,0:T(8,128)S(1)} %get-tuple-element.20), channel_id=1, source_target_pairs={{0,1},{1,0},{2,3},{3,2},{4,5},{5,4},{6,7},{7,6},{8,9},{9,8},{10,11... | collective-permute-start | bytes 1572872 | tf_op jit(solution)/shard_map/ppermute | solution.py:242
  19.2 16.8 %collective-permute-start.3 = (f32[2,4,32,256]{3,2,1,0:T(8,128)S(1)}, f32[2,4,32,256]{3,2,1,0:T(8,128)S(1)}, u32[]{:S(2)}, u32[]{:S(2)}) collective-permute-start(f32[2,4,32,256]{3,2,1,0:T(8,128)S(1)} %get-tuple-element.15), channel_id=1, source_target_pairs={{0,25},{1,8},{2,27},{3,10},{4,29},{5,12},{6,31},{7,14},{8,1},{9,16... | collective-permute-start | bytes 786440 | tf_op jit(solution)/shard_map/ppermute | solution.py:271
  23.2 8.3 %collective-permute-start.5 = (s32[2,4,32,256]{3,2,1,0:T(8,128)S(1)}, s32[2,4,32,256]{3,2,1,0:T(8,128)S(1)}, u32[]{:S(2)}, u32[]{:S(2)}) collective-permute-start(s32[2,4,32,256]{3,2,1,0:T(8,128)S(1)} %get-tuple-element.32), channel_id=1, source_target_pairs={{0,2},{2,0},{4,7},{6,5},{8,10},{10,8},{12,15},{14,13},{16,18},{18,... | collective-permute-start | bytes 786440 | tf_op jit(solution)/shard_map/ppermute | solution.py:259
  26.3 3.6 %copy-start.2 = (f32[8]{0:T(128)S(1)}, f32[8]{0:T(128)}, u32[]{:S(2)}) copy-start(f32[8]{0:T(128)} %param.7) | copy-start | bytes 100
  26.3 3.6 %copy-start.1 = (f32[3,8]{1,0:T(4,128)S(1)}, f32[3,8]{1,0:T(4,128)}, u32[]{:S(2)}) copy-start(f32[3,8]{1,0:T(4,128)} %param.6) | copy-start | bytes 292
  26.3 5.5 %collective-permute-start.6 = (s32[2,4,32,256]{3,2,1,0:T(8,128)S(1)}, s32[2,4,32,256]{3,2,1,0:T(8,128)S(1)}, u32[]{:S(2)}, u32[]{:S(2)}) collective-permute-start(s32[2,4,32,256]{3,2,1,0:T(8,128)S(1)} %get-tuple-element.33), channel_id=1, source_target_pairs={{0,4},{2,6},{4,1},{6,3},{8,12},{10,14},{12,9},{14,11},{16,20},{18,... | collective-permute-start | bytes 786440 | tf_op jit(solution)/shard_map/ppermute | solution.py:259
  27.9 5.8 %collective-permute-start.7 = (s32[2,4,32,256]{3,2,1,0:T(8,128)S(1)}, s32[2,4,32,256]{3,2,1,0:T(8,128)S(1)}, u32[]{:S(2)}, u32[]{:S(2)}) collective-permute-start(s32[2,4,32,256]{3,2,1,0:T(8,128)S(1)} %get-tuple-element.30), channel_id=1, source_target_pairs={{0,6},{2,4},{4,3},{6,1},{8,14},{10,12},{12,11},{14,9},{16,22},{18,... | collective-permute-start | bytes 786440 | tf_op jit(solution)/shard_map/ppermute | solution.py:259
  37.3 2.5 %collective-permute-start.9 = (f32[10,32,256]{2,1,0:T(8,128)S(1)}, f32[10,32,256]{2,1,0:T(8,128)S(1)}, u32[]{:S(2)}, u32[]{:S(2)}) collective-permute-start(f32[10,32,256]{2,1,0:T(8,128)S(1)} %get-tuple-element.26), channel_id=1, source_target_pairs={{0,1},{1,0},{2,3},{3,2},{4,5},{5,4},{6,7},{7,6},{8,9},{9,8},{10,11... | collective-permute-start | bytes 983048 | tf_op jit(solution)/shard_map/ppermute | solution.py:242
  39.9 4.7 %collective-permute-start.13 = (f32[4,16,256]{2,1,0:T(8,128)S(1)}, f32[4,16,256]{2,1,0:T(8,128)S(1)}, u32[]{:S(2)}, u32[]{:S(2)}) collective-permute-start(f32[4,16,256]{2,1,0:T(8,128)S(1)} %pad_maximum_fusion.1), channel_id=1, source_target_pairs={{0,8},{8,0},{16,24},{24,16},{1,9},{9,1},{17,25},{25,17},{2,10},{10... | collective-permute-start | bytes 196616 | tf_op jit(solution)/shard_map/ppermute | solution.py:302
  40.5 7.3 %collective-permute-start.10 = (f32[4,32,256]{2,1,0:T(8,128)S(1)}, f32[4,32,256]{2,1,0:T(8,128)S(1)}, u32[]{:S(2)}, u32[]{:S(2)}) collective-permute-start(f32[4,32,256]{2,1,0:T(8,128)S(1)} %get-tuple-element.41), channel_id=1, source_target_pairs={{0,6},{1,7},{2,4},{3,5},{4,2},{5,3},{6,0},{7,1},{8,14},{9,15},{10,... | collective-permute-start | bytes 393224 | tf_op jit(solution)/shard_map/ppermute | solution.py:239
  43.9 6.3 %collective-permute-start.11 = (f32[4,32,256]{2,1,0:T(8,128)S(1)}, f32[4,32,256]{2,1,0:T(8,128)S(1)}, u32[]{:S(2)}, u32[]{:S(2)}) collective-permute-start(f32[4,32,256]{2,1,0:T(8,128)S(1)} %get-tuple-element.42), channel_id=1, source_target_pairs={{0,4},{1,5},{2,6},{3,7},{4,0},{5,1},{6,2},{7,3},{8,12},{9,13},{10,... | collective-permute-start | bytes 393224 | tf_op jit(solution)/shard_map/ppermute | solution.py:239
  43.9 6.6 %collective-permute-start.12 = (f32[4,32,256]{2,1,0:T(8,128)S(1)}, f32[4,32,256]{2,1,0:T(8,128)S(1)}, u32[]{:S(2)}, u32[]{:S(2)}) collective-permute-start(f32[4,32,256]{2,1,0:T(8,128)S(1)} %get-tuple-element.40), channel_id=1, source_target_pairs={{0,2},{1,3},{2,0},{3,1},{4,6},{5,7},{6,4},{7,5},{8,10},{9,11},{10,... | collective-permute-start | bytes 393224 | tf_op jit(solution)/shard_map/ppermute | solution.py:239
  44.6 6.9 %collective-permute-start.14 = (f32[4,16,256]{2,1,0:T(8,128)S(1)}, f32[4,16,256]{2,1,0:T(8,128)S(1)}, u32[]{:S(2)}, u32[]{:S(2)}) collective-permute-start(f32[4,16,256]{2,1,0:T(8,128)S(1)} %pad_maximum_fusion.2), channel_id=1, source_target_pairs={{0,16},{8,24},{16,0},{24,8},{1,17},{9,25},{17,1},{25,9},{2,18},{10... | collective-permute-start | bytes 196616 | tf_op jit(solution)/shard_map/ppermute | solution.py:302

commit v6 on v5

--- a/solution.py
+++ b/solution.py
@@ -104,7 +104,7 @@
 
 def inner_kernel(chips, *refs):
     own, kinds = refs[:chips], refs[chips : 2 * chips]
-    other, table, dense, image, edge, edge_kind, fluid, kind = refs[2 * chips :]
+    other, table, keep, give, image, edge, edge_kind, fluid, kind, dense = refs[2 * chips :]
     member = lax.axis_index("swap")
     chip, upper = member // 2, member % 2
     half = chips // 2
@@ -144,11 +144,13 @@
     start = jnp.where(upper == 1, chips - 1, 0) * layers
     edge[...] = fluid[:, pl.ds(start, 2 * layers)]
     edge_kind[...] = kind[pl.ds(start, layers)]
-
-
-def outer_kernel(chips, far, edge, edge_kind, table, dense, image, keep, give, tile, last, drawn):
+    for i in range(half):
+        keep[i] = dense[pl.ds((2 * i + upper) * layers, layers)]
+        give[i] = dense[pl.ds((2 * i + 1 - upper) * layers, layers)]
+
+
+def outer_kernel(far, edge, edge_kind, table, image, last, tile, given, drawn):
     upper = lax.axis_index("swap") % 2
-    half = chips // 2
     _, layers, rows, columns = far.shape
     sign = jnp.where(upper == 1, -1.0, 1.0)
 
@@ -169,24 +171,11 @@
             drawn[n - 1, row, column] = front[n] + front[0] * back[n]
 
     sweep_tiles(rows, columns, layers, 3, upper == 1, load, place, last, place, edge_kind, table, finish)
-    for i in range(half):
-        keep[i] = dense[pl.ds((2 * i + upper) * layers, layers)]
-        give[pl.ds(i * layers, layers)] = dense[pl.ds((2 * i + 1 - upper) * layers, layers)]
-
-    @pl.when(upper == 0)
-    def _():
-        keep[0] = last[...]
-
-    @pl.when(upper == 1)
-    def _():
-        keep[half - 1] = last[...]
-
     short = rows // 2
     for n in range(4):
         low, high = drawn[n, :short], drawn[n, short:]
         tile[n] = jnp.where(upper == 1, high, low)
-        given = jnp.where(upper == 1, low, high)
-        give[half * layers + n // 2, (n % 2) * short : (n % 2 + 1) * short] = given
+        given[n] = jnp.where(upper == 1, low, high)
 
 
 def route_kernel(chips, *refs):
@@ -249,7 +238,11 @@
     def cut(array, j, axis):
         return lax.dynamic_slice_in_dim(array, j * rows, rows, axis=axis)
 
-    own = [to_chip(cut(fluid_state, chip ^ d, 2), d) for d in range(chips)]
+    own, uncut = [None] * chips, fluid_state
+    for d in [*range(1, chips), 0]:
+        piece = cut(uncut, chip ^ d, 2)
+        own[d] = to_chip(piece, d)
+        uncut, _ = lax.optimization_barrier((uncut, piece))
 
     theirs = to_core(material)
     both = jnp.stack([jnp.where(upper == 1, theirs, material), jnp.where(upper == 1, material, theirs)])
@@ -271,24 +264,27 @@
     far = lax.ppermute(outer, ("slab", "swap"), ring)
 
     deep = (chips * layers, rows, width)
-    dense, image, edge, edge_kind = call(
+    keep, give, image, edge, edge_kind = call(
         functools.partial(inner_kernel, chips),
         [*own, *kinds, other, table],
-        [(deep, F32), ((4, rows, width), F32), ((2, 2 * layers, rows, width), F32), (block, jnp.int32)],
-        [((2, (chips + 1) * layers, rows, width), F32), (deep, jnp.int32)],
+        [((half, *block), F32)] * 2
+        + [((4, rows, width), F32), ((2, 2 * layers, rows, width), F32), (block, jnp.int32)],
+        [((2, (chips + 1) * layers, rows, width), F32), (deep, jnp.int32), (deep, F32)],
         chips * cells,
     )
-    keep, give, tile = call(
-        functools.partial(outer_kernel, chips),
-        [far, edge, edge_kind, table, dense, image],
-        [((half, *block), F32), ((half * layers + 2, rows, width), F32), ((4, rows // 2, width), F32)],
-        [(block, F32), ((4, rows, width), F32)],
+    got = to_core(give)
+    short = (4, rows // 2, width)
+    last, tile, given = call(
+        outer_kernel,
+        [far, edge, edge_kind, table, image],
+        [(block, F32), (short, F32), (short, F32)],
+        [((4, rows, width), F32)],
         cells,
     )
-    got = to_core(give)
-
-    kept = [keep[i] for i in range(half)]
-    gotten = [got[i * layers : (i + 1) * layers] for i in range(half)]
+    partner = to_core(given)
+
+    kept = [jnp.where(i == upper * (half - 1), last, keep[i]) for i in range(half)]
+    gotten = [got[i] for i in range(half)]
     chunks = []
     for d in range(chips):
         k = chip ^ d
@@ -296,7 +292,6 @@
         chunks.append(to_chip(back, d))
     density = jnp.concatenate([pick(chunks, chip ^ j) for j in range(chips)], axis=1)
 
-    partner = got[half * layers :].reshape(4, rows // 2, width)
     tile = over(jnp.where(upper == 1, partner, tile), jnp.where(upper == 1, tile, partner))
     for bit in range(slabs.bit_length() - 1):
         partner = lax.ppermute(tile, "slab", swap_pairs(slabs, 1 << bit))

time: 52.5 us -> 58.7 us (1.12)
  waiting for transfers between devices: 22 us -> 27.9 us
  starting transfers between devices: 22.4 us -> 23.2 us
    ppermute x2, waiting for transfers between devices: 0.01 us -> 7.92 us  [per_device(): partner = lax.ppermute(tile, 'slab', swap_pairs(slabs, 1 << bit))]
    ppermute x6, waiting for transfers between devices: 16.9 us -> 15.2 us  [to_chip(): return lax.ppermute(block, 'swap', swap_pairs(members, 2 * d))]
    dynamic_slice x1 -> x4, local copies, waits for them, and re-layouts: 1.26 us -> 0.09 us  [cut(): return lax.dynamic_slice_in_dim(array, j * rows, rows, axis=axis)]
    unnamed x7 -> x9, local copies, waits for them, and re-layouts: 0.69 us -> 1.36 us
    ppermute x3 -> x4, waiting for transfers between devices: 1.26 us -> 0.91 us  [to_core(): return lax.ppermute(block, 'swap', swap_pairs(members, 1))]
    ppermute x3 -> x4, starting transfers between devices: 1.92 us -> 1.67 us  [to_core(): return lax.ppermute(block, 'swap', swap_pairs(members, 1))]
  transfers between devices with their start and end apart: 15 -> 16, of which waited for: 9 -> 12; matrix products, arithmetic and copies ran while one was open for 5% -> 2% of each run, Pallas kernels for 5% -> 4%
where the time goes in v6:
time: 58.7 us; the launch traced here: 58.4 us
  waiting for transfers between devices  27.9 us (48%)
  starting transfers between devices  23.2 us (40%)
  Pallas kernels  3.6 us (6%)
  local copies, waits for them, and re-layouts  1.45 us (2%)
  other arithmetic  1.36 us (2%)
  between operations  0.94 us (2%)
    ppermute x6, waiting for transfers between devices, to_chip(): return lax.ppermute(block, 'swap', swap_pairs(members, 2 * d))  15.2 us
    ppermute x6, starting transfers between devices, to_chip(): return lax.ppermute(block, 'swap', swap_pairs(members, 2 * d))  8.62 us
    ppermute x2, waiting for transfers between devices, per_device(): partner = lax.ppermute(tile, 'slab', swap_pairs(slabs, 1 << bit))  7.92 us
    ppermute x3, starting transfers between devices, per_device(): kinds.append(lax.ppermute(cut(both, chip ^ d, 2), 'swap', pairs))  6.8 us
    ppermute x3, waiting for transfers between devices, per_device(): kinds.append(lax.ppermute(cut(both, chip ^ d, 2), 'swap', pairs))  3.81 us
    ppermute x1, starting transfers between devices, per_device(): far = lax.ppermute(outer, ('slab', 'swap'), ring)  3.7 us
    pallas_call x3, Pallas kernels, call(): pl.pallas_call(kernel, out_shape=[jax.ShapeDtypeStruct(shape, dtype) for...  3.6 us
    ppermute x2, starting transfers between devices, per_device(): partner = lax.ppermute(tile, 'slab', swap_pairs(slabs, 1 << bit))  2.42 us
  transfers between devices with their start and end apart: 16, of which 12 were waited for; matrix products, arithmetic and copies ran while one was open for 2% of the time, Pallas kernels for 4%

profile of v6, /device:TPU:0, one launch (start us, length us, event | category | flops | bytes accessed | tf_op | source)
XLA Modules:
  0.0 58.4 jit_solution(11125029179479902489)
XLA Ops:
  0.6 0.0 copy-start
  0.6 0.6 collective-permute-start.4
  1.2 0.7 %copy-done = f32[2,4,128,256]{3,2,1,0:T(8,128)S(1)} copy-done((f32[2,4,128,256]{3,2,1,0:T(8,128)S(1)}, f32[2,4,128,256]{3,2,1,0:T(8,128)}, u32[]{:S(2)}) %copy-start) | copy-done | bytes 1048600
  2.0 4.0 %collective-permute-start.2 = (f32[2,4,32,256]{3,2,1,0:T(8,128)S(1)}, f32[2,4,32,256]{3,2,1,0:T(8,128)S(1)}, u32[]{:S(2)}, u32[]{:S(2)}) collective-permute-start(f32[2,4,32,256]{3,2,1,0:T(8,128)S(1)} %constant_dynamic-slice_fusion.1), channel_id=1, source_target_pairs={{0,6},{1,7},{2,4},{3,5},{4,2},{5,3},{6,0},{7,1},{8,14},{9,15},{10,... | collective-permute-start | bytes 786440 | tf_op jit(solution)/shard_map/ppermute | solution.py:228
  6.0 0.5 collective-permute-start.1
  6.5 0.1 collective-permute-start
  6.6 0.0 copy-start.1
  6.6 6.5 %collective-permute-done.2.refs_3_ = f32[2,4,32,256]{3,2,1,0:T(8,128)S(1)} collective-permute-done((f32[2,4,32,256]{3,2,1,0:T(8,128)S(1)}, f32[2,4,32,256]{3,2,1,0:T(8,128)S(1)}, u32[]{:S(2)}, u32[]{:S(2)}) %collective-permute-start.2) | collective-permute-done | bytes 262176 | tf_op jit(solution)/shard_map/ppermute | solution.py:228
  13.2 4.7 %collective-permute-done.1.refs_2_ = f32[2,4,32,256]{3,2,1,0:T(8,128)S(1)} collective-permute-done((f32[2,4,32,256]{3,2,1,0:T(8,128)S(1)}, f32[2,4,32,256]{3,2,1,0:T(8,128)S(1)}, u32[]{:S(2)}, u32[]{:S(2)}) %collective-permute-start.1) | collective-permute-done | bytes 262176 | tf_op jit(solution)/shard_map/ppermute | solution.py:228
  17.9 0.3 collective-permute-done.refs_1_
  18.2 0.1 shard_map.59
  18.3 0.1 collective-permute-start.8
  18.4 3.7 %collective-permute-start.3 = (f32[2,4,32,256]{3,2,1,0:T(8,128)S(1)}, f32[2,4,32,256]{3,2,1,0:T(8,128)S(1)}, u32[]{:S(2)}, u32[]{:S(2)}) collective-permute-start(f32[2,4,32,256]{3,2,1,0:T(8,128)S(1)} %get-tuple-element.22), channel_id=1, source_target_pairs={{0,25},{1,8},{2,27},{3,10},{4,29},{5,12},{6,31},{7,14},{8,1},{9,16... | collective-permute-start | bytes 786440 | tf_op jit(solution)/shard_map/ppermute | solution.py:264
  22.1 0.0 collective-permute-done.4
  22.1 0.0 copy-done.1
  22.1 0.1 select_bitcast_fusion
  22.2 0.1 fusion
  22.3 3.4 %collective-permute-start.5 = (s32[2,4,32,256]{3,2,1,0:T(8,128)S(1)}, s32[2,4,32,256]{3,2,1,0:T(8,128)S(1)}, u32[]{:S(2)}, u32[]{:S(2)}) collective-permute-start(s32[2,4,32,256]{3,2,1,0:T(8,128)S(1)} %get-tuple-element.43), channel_id=1, source_target_pairs={{0,2},{2,0},{4,7},{6,5},{8,10},{10,8},{12,15},{14,13},{16,18},{18,... | collective-permute-start | bytes 786440 | tf_op jit(solution)/shard_map/ppermute | solution.py:252
  25.7 0.0 copy-start.3
  25.7 0.0 copy-start.2
  25.7 1.3 %collective-permute-start.6 = (s32[2,4,32,256]{3,2,1,0:T(8,128)S(1)}, s32[2,4,32,256]{3,2,1,0:T(8,128)S(1)}, u32[]{:S(2)}, u32[]{:S(2)}) collective-permute-start(s32[2,4,32,256]{3,2,1,0:T(8,128)S(1)} %get-tuple-element.44), channel_id=1, source_target_pairs={{0,4},{2,6},{4,1},{6,3},{8,12},{10,14},{12,9},{14,11},{16,20},{18,... | collective-permute-start | bytes 786440 | tf_op jit(solution)/shard_map/ppermute | solution.py:252
  27.0 2.1 %collective-permute-start.7 = (s32[2,4,32,256]{3,2,1,0:T(8,128)S(1)}, s32[2,4,32,256]{3,2,1,0:T(8,128)S(1)}, u32[]{:S(2)}, u32[]{:S(2)}) collective-permute-start(s32[2,4,32,256]{3,2,1,0:T(8,128)S(1)} %get-tuple-element.41), channel_id=1, source_target_pairs={{0,6},{2,4},{4,3},{6,1},{8,14},{10,12},{12,11},{14,9},{16,22},{18,... | collective-permute-start | bytes 786440 | tf_op jit(solution)/shard_map/ppermute | solution.py:252
  29.1 0.0 copy-done.3
  29.2 1.4 %collective-permute-done.5.refs_5_ = s32[2,4,32,256]{3,2,1,0:T(8,128)S(1)} collective-permute-done((s32[2,4,32,256]{3,2,1,0:T(8,128)S(1)}, s32[2,4,32,256]{3,2,1,0:T(8,128)S(1)}, u32[]{:S(2)}, u32[]{:S(2)}) %collective-permute-start.5) | collective-permute-done | bytes 262176 | tf_op jit(solution)/shard_map/ppermute | solution.py:252
  30.5 0.3 collective-permute-done.6.refs_6_
  30.9 2.1 %collective-permute-done.7.refs_7_ = s32[2,4,32,256]{3,2,1,0:T(8,128)S(1)} collective-permute-done((s32[2,4,32,256]{3,2,1,0:T(8,128)S(1)}, s32[2,4,32,256]{3,2,1,0:T(8,128)S(1)}, u32[]{:S(2)}, u32[]{:S(2)}) %collective-permute-start.7) | collective-permute-done | bytes 262176 | tf_op jit(solution)/shard_map/ppermute | solution.py:252
  33.0 0.0 collective-permute-done.8.refs_8_
  33.0 2.3 %shard_map.60 = (f32[2,4,32,256]{3,2,1,0:T(8,128)S(1)}, f32[2,4,32,256]{3,2,1,0:T(8,128)S(1)}, f32[4,32,256]{2,1,0:T(8,128)S(1)}, f32[2,8,32,256]{3,2,1,0:T(8,128)S(1)}, s32[4,32,256]{2,1,0:T(8,128)S(1)}) custom-call(f32[2,4,32,256]{3,2,1,0:T(8,128)S(1)} %constant_dynamic-slice_fusion.refs_0_, f32[2,4,32,256]{3,2,1,0:T(8,128)S(1)} %collective-permute-done.refs_1_, ...), custom_call_target="tpu_custom_call" | custom-call | flops 39321600 | bytes 2097152 | tf_op jit(solution)/shard_map/pallas_call | solution.py:199
  35.3 0.0 collective-permute-done.3.far
  35.3 1.2 %shard_map.61 = (f32[4,32,256]{2,1,0:T(8,128)S(1)}, f32[4,16,256]{2,1,0:T(8,128)S(1)}, f32[4,16,256]{2,1,0:T(8,128)S(1)}) custom-call(f32[2,4,32,256]{3,2,1,0:T(8,128)S(1)} %collective-permute-done.3.far, f32[2,8,32,256]{3,2,1,0:T(8,128)S(1)} %get-tuple-element.28.edge, s32[4,32,256]{2,1,0:T(8,128)S(1)} %get-tuple-element.29.edge_kind, ...), custom_call_target="tpu_custom_call" | custom-call | flops 9830400 | bytes 524288 | tf_op jit(solution)/shard_map/pallas_call | solution.py:199
  36.5 1.0 %collective-permute-start.13 = (f32[4,16,256]{2,1,0:T(8,128)S(1)}, f32[4,16,256]{2,1,0:T(8,128)S(1)}, u32[]{:S(2)}, u32[]{:S(2)}) collective-permute-start(f32[4,16,256]{2,1,0:T(8,128)S(1)} %get-tuple-element.34), channel_id=1, source_target_pairs={{0,1},{1,0},{2,3},{3,2},{4,5},{5,4},{6,7},{7,6},{8,9},{9,8},{10,11... | collective-permute-start | bytes 196616 | tf_op jit(solution)/shard_map/ppermute | solution.py:231
  37.6 0.9 %collective-permute-done.13 = f32[4,16,256]{2,1,0:T(8,128)S(1)} collective-permute-done((f32[4,16,256]{2,1,0:T(8,128)S(1)}, f32[4,16,256]{2,1,0:T(8,128)S(1)}, u32[]{:S(2)}, u32[]{:S(2)}) %collective-permute-start.13) | collective-permute-done | bytes 65568 | tf_op jit(solution)/shard_map/ppermute | solution.py:231
  38.5 0.7 %collective-permute-start.14 = (f32[4,16,256]{2,1,0:T(8,128)S(1)}, f32[4,16,256]{2,1,0:T(8,128)S(1)}, u32[]{:S(2)}, u32[]{:S(2)}) collective-permute-start(f32[4,16,256]{2,1,0:T(8,128)S(1)} %pad_maximum_fusion.1), channel_id=1, source_target_pairs={{0,8},{8,0},{16,24},{24,16},{1,9},{9,1},{17,25},{25,17},{2,10},{10... | collective-permute-start | bytes 196616 | tf_op jit(solution)/shard_map/ppermute | solution.py:297
  39.2 3.7 %collective-permute-done.14 = f32[4,16,256]{2,1,0:T(8,128)S(1)} collective-permute-done((f32[4,16,256]{2,1,0:T(8,128)S(1)}, f32[4,16,256]{2,1,0:T(8,128)S(1)}, u32[]{:S(2)}, u32[]{:S(2)}) %collective-permute-start.14) | collective-permute-done | bytes 65568 | tf_op jit(solution)/shard_map/ppermute | solution.py:297
  43.0 1.7 %collective-permute-start.15 = (f32[4,16,256]{2,1,0:T(8,128)S(1)}, f32[4,16,256]{2,1,0:T(8,128)S(1)}, u32[]{:S(2)}, u32[]{:S(2)}) collective-permute-start(f32[4,16,256]{2,1,0:T(8,128)S(1)} %pad_maximum_fusion.2), channel_id=1, source_target_pairs={{0,16},{8,24},{16,0},{24,8},{1,17},{9,25},{17,1},{25,9},{2,18},{10... | collective-permute-start | bytes 196616 | tf_op jit(solution)/shard_map/ppermute | solution.py:297
  44.7 0.0 collective-permute-start.9
  44.7 4.2 %collective-permute-done.15 = f32[4,16,256]{2,1,0:T(8,128)S(1)} collective-permute-done((f32[4,16,256]{2,1,0:T(8,128)S(1)}, f32[4,16,256]{2,1,0:T(8,128)S(1)}, u32[]{:S(2)}, u32[]{:S(2)}) %collective-permute-start.15) | collective-permute-done | bytes 65568 | tf_op jit(solution)/shard_map/ppermute | solution.py:297
  49.0 0.0 collective-permute-done.9
  49.1 2.7 %collective-permute-start.10 = (f32[4,32,256]{2,1,0:T(8,128)S(1)}, f32[4,32,256]{2,1,0:T(8,128)S(1)}, u32[]{:S(2)}, u32[]{:S(2)}) collective-permute-start(f32[4,32,256]{2,1,0:T(8,128)S(1)} %get-tuple-element.51), channel_id=1, source_target_pairs={{0,6},{1,7},{2,4},{3,5},{4,2},{5,3},{6,0},{7,1},{8,14},{9,15},{10,... | collective-permute-start | bytes 393224 | tf_op jit(solution)/shard_map/ppermute | solution.py:228
  51.8 0.0 collective-permute-start.11
  51.8 1.3 %collective-permute-start.12 = (f32[4,32,256]{2,1,0:T(8,128)S(1)}, f32[4,32,256]{2,1,0:T(8,128)S(1)}, u32[]{:S(2)}, u32[]{:S(2)}) collective-permute-start(f32[4,32,256]{2,1,0:T(8,128)S(1)} %get-tuple-element.38), channel_id=1, source_target_pairs={{0,2},{1,3},{2,0},{3,1},{4,6},{5,7},{6,4},{7,5},{8,10},{9,11},{10,... | collective-permute-start | bytes 393224 | tf_op jit(solution)/shard_map/ppermute | solution.py:228
  53.1 0.7 %copy.6 = f32[1,4,16,256]{3,1,2,0:T(4,128)} copy(f32[1,4,16,256]{3,2,1,0:T(8,128)S(1)} %maximum_bitcast_fusion) | data formatting | bytes 131072
  53.8 2.3 %collective-permute-done.10 = f32[4,32,256]{2,1,0:T(8,128)S(1)} collective-permute-done((f32[4,32,256]{2,1,0:T(8,128)S(1)}, f32[4,32,256]{2,1,0:T(8,128)S(1)}, u32[]{:S(2)}, u32[]{:S(2)}) %collective-permute-start.10) | collective-permute-done | bytes 131104 | tf_op jit(solution)/shard_map/ppermute | solution.py:228
  56.1 1.2 %collective-permute-done.11 = f32[4,32,256]{2,1,0:T(8,128)S(1)} collective-permute-done((f32[4,32,256]{2,1,0:T(8,128)S(1)}, f32[4,32,256]{2,1,0:T(8,128)S(1)}, u32[]{:S(2)}, u32[]{:S(2)}) %collective-permute-start.11) | collective-permute-done | bytes 131104 | tf_op jit(solution)/shard_map/ppermute | solution.py:228
  57.3 0.2 collective-permute-done.12
  57.4 0.1 select_select_fusion.3
  57.5 0.1 select_select_fusion.2
  57.6 0.8 %pad_maximum_fusion = f32[4,128,256]{2,1,0:T(8,128)} fusion(f32[4,32,256]{2,1,0:T(8,128)S(1)} %get-tuple-element.48, f32[4,32,256]{2,1,0:T(8,128)S(1)} %get-tuple-element.49, f32[4,32,256]{2,1,0:T(8,128)S(1)} %get-tuple-element.47, f32[4,32,256]{2,1,0:T(8,128)S(1)} %get-tuple-element.36), kind=kLoop, calls=%fused_computation.8 | loop fusion | flops 393216 | bytes 1048576 | tf_op jit(solution)/shard_map/concatenate | solution.py:293
  (22 shorter events, 0.3 us)
Async XLA Ops:
  0.6 1.2 %copy-start = (f32[2,4,128,256]{3,2,1,0:T(8,128)S(1)}, f32[2,4,128,256]{3,2,1,0:T(8,128)}, u32[]{:S(2)}) copy-start(f32[2,4,128,256]{3,2,1,0:T(8,128)} %param.4) | copy-start | bytes 3145732
  0.6 21.4 %collective-permute-start.4 = (s32[4,128,256]{2,1,0:T(8,128)}, s32[4,128,256]{2,1,0:T(8,128)S(1)}, u32[]{:S(2)}, u32[]{:S(2)}) collective-permute-start(s32[4,128,256]{2,1,0:T(8,128)} %param.5), channel_id=1, source_target_pairs={{0,1},{1,0},{2,3},{3,2},{4,5},{5,4},{6,7},{7,6},{8,9},{9,8},{10,11... | collective-permute-start | bytes 1572872 | tf_op jit(solution)/shard_map/ppermute | solution.py:231
  2.0 11.2 %collective-permute-start.2 = (f32[2,4,32,256]{3,2,1,0:T(8,128)S(1)}, f32[2,4,32,256]{3,2,1,0:T(8,128)S(1)}, u32[]{:S(2)}, u32[]{:S(2)}) collective-permute-start(f32[2,4,32,256]{3,2,1,0:T(8,128)S(1)} %constant_dynamic-slice_fusion.1), channel_id=1, source_target_pairs={{0,6},{1,7},{2,4},{3,5},{4,2},{5,3},{6,0},{7,1},{8,14},{9,15},{10,... | collective-permute-start | bytes 786440 | tf_op jit(solution)/shard_map/ppermute | solution.py:228
  6.0 11.9 %collective-permute-start.1 = (f32[2,4,32,256]{3,2,1,0:T(8,128)S(1)}, f32[2,4,32,256]{3,2,1,0:T(8,128)S(1)}, u32[]{:S(2)}, u32[]{:S(2)}) collective-permute-start(f32[2,4,32,256]{3,2,1,0:T(8,128)S(1)} %constant_dynamic-slice_fusion.2), channel_id=1, source_target_pairs={{0,4},{1,5},{2,6},{3,7},{4,0},{5,1},{6,2},{7,3},{8,12},{9,13},{10,... | collective-permute-start | bytes 786440 | tf_op jit(solution)/shard_map/ppermute | solution.py:228
  6.5 11.7 %collective-permute-start = (f32[2,4,32,256]{3,2,1,0:T(8,128)S(1)}, f32[2,4,32,256]{3,2,1,0:T(8,128)S(1)}, u32[]{:S(2)}, u32[]{:S(2)}) collective-permute-start(f32[2,4,32,256]{3,2,1,0:T(8,128)S(1)} %constant_dynamic-slice_fusion.3), channel_id=1, source_target_pairs={{0,2},{1,3},{2,0},{3,1},{4,6},{5,7},{6,4},{7,5},{8,10},{9,11},{10,... | collective-permute-start | bytes 786440 | tf_op jit(solution)/shard_map/ppermute | solution.py:228
  6.6 15.4 %copy-start.1 = (s32[4,128,256]{2,1,0:T(8,128)S(1)}, s32[4,128,256]{2,1,0:T(8,128)}, u32[]{:S(2)}) copy-start(s32[4,128,256]{2,1,0:T(8,128)} %param.5) | copy-start | bytes 1572868
  18.3 14.7 %collective-permute-start.8 = (f32[2,2,4,32,256]{4,3,2,1,0:T(8,128)S(1)}, f32[2,2,4,32,256]{4,3,2,1,0:T(8,128)S(1)}, u32[]{:S(2)}, u32[]{:S(2)}) collective-permute-start(f32[2,2,4,32,256]{4,3,2,1,0:T(8,128)S(1)} %get-tuple-element.27), channel_id=1, source_target_pairs={{0,1},{1,0},{2,3},{3,2},{4,5},{5,4},{6,7},{7,6},{8,9},{9,8},{10,11... | collective-permute-start | bytes 1572872 | tf_op jit(solution)/shard_map/ppermute | solution.py:231
  18.4 17.0 %collective-permute-start.3 = (f32[2,4,32,256]{3,2,1,0:T(8,128)S(1)}, f32[2,4,32,256]{3,2,1,0:T(8,128)S(1)}, u32[]{:S(2)}, u32[]{:S(2)}) collective-permute-start(f32[2,4,32,256]{3,2,1,0:T(8,128)S(1)} %get-tuple-element.22), channel_id=1, source_target_pairs={{0,25},{1,8},{2,27},{3,10},{4,29},{5,12},{6,31},{7,14},{8,1},{9,16... | collective-permute-start | bytes 786440 | tf_op jit(solution)/shard_map/ppermute | solution.py:264
  22.3 8.3 %collective-permute-start.5 = (s32[2,4,32,256]{3,2,1,0:T(8,128)S(1)}, s32[2,4,32,256]{3,2,1,0:T(8,128)S(1)}, u32[]{:S(2)}, u32[]{:S(2)}) collective-permute-start(s32[2,4,32,256]{3,2,1,0:T(8,128)S(1)} %get-tuple-element.43), channel_id=1, source_target_pairs={{0,2},{2,0},{4,7},{6,5},{8,10},{10,8},{12,15},{14,13},{16,18},{18,... | collective-permute-start | bytes 786440 | tf_op jit(solution)/shard_map/ppermute | solution.py:252
  25.7 3.5 %copy-start.3 = (f32[8]{0:T(128)S(1)}, f32[8]{0:T(128)}, u32[]{:S(2)}) copy-start(f32[8]{0:T(128)} %param.7) | copy-start | bytes 100
  25.7 3.5 %copy-start.2 = (f32[3,8]{1,0:T(4,128)S(1)}, f32[3,8]{1,0:T(4,128)}, u32[]{:S(2)}) copy-start(f32[3,8]{1,0:T(4,128)} %param.6) | copy-start | bytes 292
  25.7 5.2 %collective-permute-start.6 = (s32[2,4,32,256]{3,2,1,0:T(8,128)S(1)}, s32[2,4,32,256]{3,2,1,0:T(8,128)S(1)}, u32[]{:S(2)}, u32[]{:S(2)}) collective-permute-start(s32[2,4,32,256]{3,2,1,0:T(8,128)S(1)} %get-tuple-element.44), channel_id=1, source_target_pairs={{0,4},{2,6},{4,1},{6,3},{8,12},{10,14},{12,9},{14,11},{16,20},{18,... | collective-permute-start | bytes 786440 | tf_op jit(solution)/shard_map/ppermute | solution.py:252
  27.0 6.0 %collective-permute-start.7 = (s32[2,4,32,256]{3,2,1,0:T(8,128)S(1)}, s32[2,4,32,256]{3,2,1,0:T(8,128)S(1)}, u32[]{:S(2)}, u32[]{:S(2)}) collective-permute-start(s32[2,4,32,256]{3,2,1,0:T(8,128)S(1)} %get-tuple-element.41), channel_id=1, source_target_pairs={{0,6},{2,4},{4,3},{6,1},{8,14},{10,12},{12,11},{14,9},{16,22},{18,... | collective-permute-start | bytes 786440 | tf_op jit(solution)/shard_map/ppermute | solution.py:252
  36.5 1.9 %collective-permute-start.13 = (f32[4,16,256]{2,1,0:T(8,128)S(1)}, f32[4,16,256]{2,1,0:T(8,128)S(1)}, u32[]{:S(2)}, u32[]{:S(2)}) collective-permute-start(f32[4,16,256]{2,1,0:T(8,128)S(1)} %get-tuple-element.34), channel_id=1, source_target_pairs={{0,1},{1,0},{2,3},{3,2},{4,5},{5,4},{6,7},{7,6},{8,9},{9,8},{10,11... | collective-permute-start | bytes 196616 | tf_op jit(solution)/shard_map/ppermute | solution.py:231
  38.5 4.4 %collective-permute-start.14 = (f32[4,16,256]{2,1,0:T(8,128)S(1)}, f32[4,16,256]{2,1,0:T(8,128)S(1)}, u32[]{:S(2)}, u32[]{:S(2)}) collective-permute-start(f32[4,16,256]{2,1,0:T(8,128)S(1)} %pad_maximum_fusion.1), channel_id=1, source_target_pairs={{0,8},{8,0},{16,24},{24,16},{1,9},{9,1},{17,25},{25,17},{2,10},{10... | collective-permute-start | bytes 196616 | tf_op jit(solution)/shard_map/ppermute | solution.py:297
  43.0 5.9 %collective-permute-start.15 = (f32[4,16,256]{2,1,0:T(8,128)S(1)}, f32[4,16,256]{2,1,0:T(8,128)S(1)}, u32[]{:S(2)}, u32[]{:S(2)}) collective-permute-start(f32[4,16,256]{2,1,0:T(8,128)S(1)} %pad_maximum_fusion.2), channel_id=1, source_target_pairs={{0,16},{8,24},{16,0},{24,8},{1,17},{9,25},{17,1},{25,9},{2,18},{10... | collective-permute-start | bytes 196616 | tf_op jit(solution)/shard_map/ppermute | solution.py:297
  44.7 4.2 %collective-permute-start.9 = (f32[2,4,32,256]{3,2,1,0:T(8,128)S(1)}, f32[2,4,32,256]{3,2,1,0:T(8,128)S(1)}, u32[]{:S(2)}, u32[]{:S(2)}) collective-permute-start(f32[2,4,32,256]{3,2,1,0:T(8,128)S(1)} %get-tuple-element.33), channel_id=1, source_target_pairs={{0,1},{1,0},{2,3},{3,2},{4,5},{5,4},{6,7},{7,6},{8,9},{9,8},{10,11... | collective-permute-start | bytes 786440 | tf_op jit(solution)/shard_map/ppermute | solution.py:231
  49.1 7.0 %collective-permute-start.10 = (f32[4,32,256]{2,1,0:T(8,128)S(1)}, f32[4,32,256]{2,1,0:T(8,128)S(1)}, u32[]{:S(2)}, u32[]{:S(2)}) collective-permute-start(f32[4,32,256]{2,1,0:T(8,128)S(1)} %get-tuple-element.51), channel_id=1, source_target_pairs={{0,6},{1,7},{2,4},{3,5},{4,2},{5,3},{6,0},{7,1},{8,14},{9,15},{10,... | collective-permute-start | bytes 393224 | tf_op jit(solution)/shard_map/ppermute | solution.py:228
  51.8 5.5 %collective-permute-start.11 = (f32[4,32,256]{2,1,0:T(8,128)S(1)}, f32[4,32,256]{2,1,0:T(8,128)S(1)}, u32[]{:S(2)}, u32[]{:S(2)}) collective-permute-start(f32[4,32,256]{2,1,0:T(8,128)S(1)} %get-tuple-element.50), channel_id=1, source_target_pairs={{0,4},{1,5},{2,6},{3,7},{4,0},{5,1},{6,2},{7,3},{8,12},{9,13},{10,... | collective-permute-start | bytes 393224 | tf_op jit(solution)/shard_map/ppermute | solution.py:228
  51.8 5.7 %collective-permute-start.12 = (f32[4,32,256]{2,1,0:T(8,128)S(1)}, f32[4,32,256]{2,1,0:T(8,128)S(1)}, u32[]{:S(2)}, u32[]{:S(2)}) collective-permute-start(f32[4,32,256]{2,1,0:T(8,128)S(1)} %get-tuple-element.38), channel_id=1, source_target_pairs={{0,2},{1,3},{2,0},{3,1},{4,6},{5,7},{6,4},{7,5},{8,10},{9,11},{10,... | collective-permute-start | bytes 393224 | tf_op jit(solution)/shard_map/ppermute | solution.py:228
